TPU v7x, 32 devices: a whole 2x2x4 slice. The times are simulated.
32 devices in a mesh: dom: 8 (over z, x), feat: 4 (over y, core).
Axes of the slice: x: 2, y: 2, z: 4, core: 2. Of those that a mesh axis runs over, the one named last changes fastest.
Arguments:
- feats: bfloat16 [256, 4096], P('feat', 'dom'), may hold values from -6 to 6
- self_weight: bfloat16 [256, 256], P(None, 'feat'), may hold values from -0.375 to 0.375
- bases: bfloat16 [30, 256, 256], P(None, 'feat'), may hold values from -0.375 to 0.375
- coef: float32 [237, 30], replicated, may hold values from -1.2 to 1.2
- src_part: int32 [8192, 1], P('dom'), may hold values from 0 to 7; in each aligned block of 1024 rows (0 to 1023, 1024 to 2047, ...) at most 256 rows name the same one
- src_row: int32 [8192], P('dom'), may hold values from 0 to 511
- edge_dst: int32 [8192], P('dom'), may hold values from 0 to 511
- edge_rel: int32 [8192], P('dom'), may hold values from 0 to 236
- block_owner: int32 [64, 1], P('dom'), may hold values from 0 to 7; in each aligned block of 8 rows (0 to 7, 8 to 15, ...) at most 2 rows name the same one
- block_valid: int32 [8, 8], P('dom'), may hold values from 1 to 128, 896 in all within a row
- cotangent: bfloat16 [256, 4096], P('feat', 'dom'), may hold values from -6 to 6
Outputs:
- output: bfloat16 [256, 4096], P('feat', 'dom')
- grad_feats: bfloat16 [256, 4096], P('feat', 'dom')
- grad_bases: float32 [30, 256, 256], P(None, 'feat')
- grad_self: float32 [256, 256], P(None, 'feat')
- grad_coef: float32 [237, 30], replicated
Inputs may be any that keep to these rules, and one draw needn't show every extreme that they name: `src_part`: among the edge rows of one index of dom, no partition is the source partition of more than 256 rows, and some partition of exactly 256. `block_owner`: among the blocks of one index of dom, no partition owns more than 2, a bound that some block reaches. `block_valid`: the valid rows of a block come first; the counts of one index of dom sum to 896.
All inputs are finite; a program needn't handle non-finite values.
Results may differ from a plain program's by a relative error of at most 0.0055.
Values may be sent and summed in bfloat16 or wider, within the bound.
No kernel may reach another device: no remote copies, remote signals or barrier semaphores. Data moves between devices by JAX's collectives and lax.ppermute only.
A program may use at most 64 MiB of HBM per device.

v0:
```python
import jax
import jax.numpy as jnp
from jax import lax
from jax.sharding import PartitionSpec as P


def body(
    feats,
    self_weight,
    bases,
    coef,
    src_part,
    src_row,
    edge_dst,
    edge_rel,
    block_owner,
    block_valid,
    cotangent,
):
    dom_count = lax.axis_size("dom")
    quarter = feats.shape[0]
    entities = feats.shape[1]
    edge_count = src_row.shape[0]
    block_count = block_valid.shape[1]
    block_rows = edge_count // block_count
    slot_cap = 128 * ((2 * edge_count + 128 * dom_count - 1) // (128 * dom_count))
    block_cap = (2 * block_count + dom_count - 1) // dom_count
    basis_count = bases.shape[0]
    model_width = bases.shape[2]
    relation_count = coef.shape[0]
    block_span = min(512, edge_count)
    block_total = edge_count // block_span
    live_rows = (jnp.arange(block_rows)[None, :] < block_valid[0][:, None]).reshape(edge_count)
    source_part = src_part[:, 0]
    onehot_float = (source_part[:, None] == jnp.arange(dom_count)[None, :]).astype(jnp.float32)
    onehot_float = onehot_float.reshape(block_count, block_rows, dom_count)
    before = (jnp.arange(block_rows)[None, :] < jnp.arange(block_rows)[:, None]).astype(jnp.float32)
    inside = jnp.einsum("jk,bkp->bjp", before, onehot_float, precision=lax.Precision.HIGHEST)
    totals = jnp.sum(onehot_float, axis=1)
    offsets = jnp.cumsum(totals, axis=0) - totals
    slot_rank = (
        jnp.sum((inside + offsets[:, None, :]) * onehot_float, axis=2)
        .reshape(edge_count)
        .astype(jnp.int32)
    )
    slot_index = source_part * slot_cap + slot_rank
    requests = jnp.full((dom_count * slot_cap,), entities, jnp.int32).at[slot_index].set(src_row)
    requests = requests.reshape(dom_count, slot_cap)
    owners = block_owner[:, 0]
    owner_hot = (owners[:, None] == jnp.arange(dom_count)[None, :]).astype(jnp.int32)
    block_rank = jnp.sum((jnp.cumsum(owner_hot, axis=0) - owner_hot) * owner_hot, axis=1)
    block_slot = owners * block_cap + block_rank
    dst_rows = jnp.where(live_rows, edge_dst, entities).reshape(block_count, block_rows)
    dst_send = (
        jnp.full((dom_count * block_cap, block_rows), entities, jnp.int32)
        .at[block_slot]
        .set(dst_rows)
    )
    dst_send = dst_send.reshape(dom_count, block_cap * block_rows)
    asked_rows, arriving = (
        lax.all_to_all(requests, "dom", split_axis=0, concat_axis=0, tiled=True),
        lax.all_to_all(dst_send, "dom", split_axis=0, concat_axis=0, tiled=True),
    )
    served = jnp.take(feats, asked_rows, axis=1, mode="fill", fill_value=0)
    fetched = lax.all_to_all(served, "dom", split_axis=1, concat_axis=1, tiled=True).reshape(
        quarter, dom_count * slot_cap
    )
    source_quarter = jnp.take(fetched, slot_index, axis=1)
    sources, own_full = (
        lax.all_gather(source_quarter, "feat", axis=0, tiled=True),
        lax.all_gather(feats, "feat", axis=0, tiled=True),
    )
    bases_flat = bases.reshape(basis_count * quarter, model_width)

    def block_weights(offset):
        relation_block = lax.dynamic_slice_in_dim(edge_rel, offset, block_span, 0)
        relation_hot = (relation_block[:, None] == jnp.arange(relation_count)[None, :]).astype(
            jnp.float32
        )
        weights = jnp.dot(relation_hot, coef, precision=lax.Precision.HIGHEST)
        return (relation_hot, weights)

    def block_terms(offset):
        source_block = lax.dynamic_slice_in_dim(sources, offset, block_span, 1)
        products = lax.dot_general(
            source_block, bases_flat, (((0,), (1,)), ((), ())), preferred_element_type=jnp.float32
        )
        relation_hot, weights = block_weights(offset)
        return (
            source_block,
            products.reshape(block_span, basis_count, quarter),
            relation_hot,
            weights,
        )

    def forward_step(step_index, messages):
        offset = step_index * block_span
        source_block, products, relation_hot, weights = block_terms(offset)
        live_block = lax.dynamic_slice_in_dim(live_rows, offset, block_span, 0)
        mixed = jnp.einsum("eb,ebo->oe", weights, products, precision=lax.Precision.HIGHEST)
        mixed = jnp.where(live_block[None, :], mixed, 0.0).astype(jnp.bfloat16)
        return lax.dynamic_update_slice_in_dim(messages, mixed, offset, 1)

    messages = lax.fori_loop(
        0, block_total, forward_step, jnp.zeros((quarter, edge_count), jnp.bfloat16)
    )
    message_send = jnp.zeros((quarter, dom_count * block_cap, block_rows), jnp.bfloat16)
    message_send = message_send.at[:, block_slot].set(
        messages.reshape(quarter, block_count, block_rows)
    )
    message_send = message_send.reshape(quarter, dom_count, block_cap * block_rows)
    received = lax.all_to_all(message_send, "dom", split_axis=1, concat_axis=1, tiled=True)
    aggregate = (
        jnp.zeros((quarter, entities), jnp.float32)
        .at[:, arriving]
        .add(received.astype(jnp.float32), mode="drop")
    )
    degree = jnp.zeros((entities,), jnp.float32).at[arriving].add(1.0, mode="drop")
    inverse_degree = 1.0 / jnp.maximum(degree, 1.0)
    preact = lax.dot_general(
        self_weight, own_full, (((0,), (0,)), ((), ())), preferred_element_type=jnp.float32
    )
    preact = preact + inverse_degree[None, :] * aggregate
    output = jax.nn.silu(preact).astype(jnp.bfloat16)
    sigmoid_pre = jax.nn.sigmoid(preact)
    grad_pre = (
        cotangent.astype(jnp.float32) * sigmoid_pre * (1.0 + preact * (1.0 - sigmoid_pre))
    ).astype(jnp.bfloat16)
    sent_back = jnp.take(grad_pre, arriving, axis=1, mode="fill", fill_value=0).astype(jnp.float32)
    sent_back = (
        sent_back * jnp.take(inverse_degree, arriving, mode="fill", fill_value=0.0)[None]
    ).astype(jnp.bfloat16)
    returned = lax.all_to_all(sent_back, "dom", split_axis=1, concat_axis=1, tiled=True)
    grad_message = returned.reshape(quarter, dom_count * block_cap, block_rows)[
        :, block_slot
    ].reshape(quarter, edge_count)

    def backward_step(step_index, totals_now):
        grad_bases, grad_coef, edge_partial = totals_now
        offset = step_index * block_span
        source_block, products, relation_hot, weights = block_terms(offset)
        grad_block = lax.dynamic_slice_in_dim(grad_message, offset, block_span, 1).astype(
            jnp.float32
        )
        scaled = jnp.einsum("ebo,oe->eb", products, grad_block, precision=lax.Precision.HIGHEST)
        grad_coef = grad_coef + lax.dot_general(
            relation_hot, scaled, (((0,), (0,)), ((), ())), precision=lax.Precision.HIGHEST
        )
        combined = (weights[:, :, None] * grad_block.T[:, None, :]).astype(jnp.bfloat16)
        combined = combined.reshape(block_span, basis_count * quarter)
        grad_bases = grad_bases + lax.dot_general(
            combined, source_block, (((0,), (1,)), ((), ())), preferred_element_type=jnp.float32
        )
        partial_grad = lax.dot_general(
            bases_flat, combined, (((0,), (1,)), ((), ())), preferred_element_type=jnp.float32
        )
        edge_partial = lax.dynamic_update_slice_in_dim(edge_partial, partial_grad, offset, 1)
        return (grad_bases, grad_coef, edge_partial)

    start_state = (
        jnp.zeros((basis_count * quarter, model_width), jnp.float32),
        jnp.zeros((relation_count, basis_count), jnp.float32),
        jnp.zeros((model_width, edge_count), jnp.float32),
    )
    grad_bases, grad_coef, edge_partial = lax.fori_loop(0, block_total, backward_step, start_state)
    self_partial = jnp.dot(self_weight, grad_pre, preferred_element_type=jnp.float32)
    edge_grads, self_grads = (
        lax.psum_scatter(edge_partial, "feat", scatter_dimension=0, tiled=True),
        lax.psum_scatter(self_partial, "feat", scatter_dimension=0, tiled=True),
    )
    slot_grads = (
        jnp.zeros((quarter, dom_count * slot_cap), jnp.float32).at[:, slot_index].set(edge_grads)
    )
    slot_grads = slot_grads.reshape(quarter, dom_count, slot_cap)
    arrived_grads = lax.all_to_all(slot_grads, "dom", split_axis=1, concat_axis=1, tiled=True)
    source_sum = (
        jnp.zeros((quarter, entities), jnp.float32)
        .at[:, asked_rows]
        .add(arrived_grads, mode="drop")
    )
    grad_feats = (self_grads + source_sum).astype(jnp.bfloat16)
    self_term = lax.dot_general(
        own_full, grad_pre, (((1,), (1,)), ((), ())), preferred_element_type=jnp.float32
    )
    scale = float(edge_count * dom_count) ** (-0.5)
    bases_total, self_total = lax.psum((grad_bases, self_term), "dom")
    coef_total = lax.psum(grad_coef, ("dom", "feat"))
    return (
        output,
        grad_feats,
        (bases_total * scale).reshape(basis_count, quarter, model_width),
        self_total * scale,
        coef_total * scale,
    )


def solution(mesh):
    return jax.shard_map(
        body,
        mesh=mesh,
        in_specs=(
            P("feat", "dom"),
            P(None, "feat"),
            P(None, "feat", None),
            P(),
            P("dom", None),
            P("dom"),
            P("dom"),
            P("dom"),
            P("dom", None),
            P("dom", None),
            P("feat", "dom"),
        ),
        out_specs=(P("feat", "dom"), P("feat", "dom"), P(None, "feat", None), P(None, "feat"), P()),
        check_vma=False,
    )
```

profile of v0, /device:TPU:0, one launch (start us, length us, event | category | flops | bytes accessed | tf_op | source)
XLA Modules:
  0.0 305.0 jit_solution(917960564627141620)
XLA Ops:
  8.0 0.8 convert_reduce_fusion
  8.8 0.9 fusion.17
  9.8 0.7 and_reduce_fusion
  10.5 5.0 %scatter_custom_fusion.2 = s32[2048]{0:T(1024)} fusion(s32[1024]{0:T(1024)S(1)} %bitcast.176, s32[1024]{0:T(1024)} %param.22, s32[]{:T(128)} %constant.135.clone.1), kind=kCustom, calls=%fused_computation.85 | custom fusion | bytes 8704 | tf_op jit(solution)/shard_map/scatter | solution.py:47
  15.5 7.3 %all-to-all-start.1 = ((s32[8,1,256]{2,1,0:T(1,128)}), s32[8,1,256]{2,1,0:T(1,128)S(1)}, u32[]{:S(2)}, u32[]{:S(2)}) async-start(s32[8,1,256]{2,1,0:T(1,128)} %bitcast.18), calls=%async_computation.1 | async-start | bytes 16384 | tf_op jit(solution)/shard_map/all_to_all | solution.py:61
  22.8 0.7 fusion.35
  23.6 0.7 fusion.33
  24.3 0.8 select_reduce_fusion
  25.8 6.0 %all_gather.6 = bf16[256,512]{1,0:T(8,128)(2,1)S(1)} all-gather(bf16[64,512]{1,0:T(8,128)(2,1)} %param.17), channel_id=1, replica_groups=mesh['dom'=8,'feat'=4] {'feat'}, dimensions={0}, use_global_device_ids=true | all-gather | bytes 327680 | tf_op jit(solution)/shard_map/all_gather | solution.py:71
  31.8 1.0 copy.90
  32.8 1.4 scatter_custom_fusion
  34.2 6.0 %all-to-all-start = ((s32[8,1,256]{2,1,0:T(1,128)}), s32[8,1,256]{2,1,0:T(1,128)S(1)}, u32[]{:S(2)}, u32[]{:S(2)}) async-start(s32[8,1,256]{2,1,0:T(1,128)} %bitcast.10), calls=%async_computation | async-start | bytes 16384 | tf_op jit(solution)/shard_map/all_to_all | solution.py:62
  40.2 6.2 %gather_fusion.3 = bf16[2048,64]{1,0:T(8,128)(2,1)S(1)} fusion(bf16[64,512]{0,1:T(8,128)(2,1)S(1)} %copy.90, s32[2048]{0:T(1024)S(1)} %broadcast_clamp_fusion.2), kind=kCustom, calls=%fused_computation.clone | custom fusion | bytes 532480 | tf_op jit(solution)/shard_map/jit(_take)/gather | solution.py:64
  46.6 0.7 select_bitcast_fusion
  47.4 6.0 %all-to-all-start.2 = ((bf16[64,8,256]{2,0,1:T(8,128)(2,1)}), bf16[64,8,256]{2,0,1:T(8,128)(2,1)S(1)}, u32[]{:S(2)}, u32[]{:S(2)}) async-start(bf16[64,8,256]{2,0,1:T(8,128)(2,1)} %select_bitcast_fusion), calls=%async_computation.2 | async-start | bytes 524288 | tf_op jit(solution)/shard_map/all_to_all | solution.py:65
  53.4 14.7 %scatter_custom_fusion.1 = f32[512]{0:T(512)S(1)} fusion(s32[2048]{0:T(1024)S(1)} %bitcast.169, f32[2048]{0:T(1024)S(1)} %broadcast.150, f32[]{:T(128)} %constant.134.clone.1), kind=kCustom, calls=%fused_computation.98 | custom fusion | flops 2048 | bytes 2052 | tf_op jit(solution)/shard_map/scatter-add | solution.py:118
  68.4 3.2 %gather_fusion = bf16[1024,64]{1,0:T(8,128)(2,1)S(1)} fusion(bf16[64,2048]{0,1:T(8,128)(2,1)S(1)} %bitcast.160, s32[1024]{0:T(1024)S(1)} %broadcast_clamp_fusion.3), kind=kCustom, calls=%fused_computation.2 | custom fusion | bytes 266240 | tf_op jit(solution)/shard_map/jit(_take)/gather | solution.py:68
  72.0 7.2 %all_gather.7 = bf16[256,1024]{1,0:T(8,128)(2,1)S(1)} all-gather(bf16[64,1024]{1,0:T(8,128)(2,1)S(1)} %copy.93), channel_id=1, replica_groups=mesh['dom'=8,'feat'=4] {'feat'}, dimensions={0}, use_global_device_ids=true | all-gather | bytes 655360 | tf_op jit(solution)/shard_map/all_gather | solution.py:70
  79.2 3.9 %while.31 = (s32[]{:T(128)}, bf16[64,1024]{1,0:T(8,128)(2,1)S(1)}, pred[1024]{0:T(1024)(128)(4,1)S(1)}, bf16[256,1024]{1,0:T(8,128)(2,1)S(1)}, bf16[1920,256]{1,...) while((s32[]{:T(128)}, bf16[64,1024]{1,0:T(8,128)(2,1)S(1)}, ...), condition=%wide.region_9.11_spmd, body=%wide.region_8.10_spmd.sunk | while | flops 549087744 | bytes 9465283 | solution.py:104
  83.2 0.8 scatter_fusion
  84.2 0.8 copy.96
  85.0 6.0 %all-to-all-start.3 = ((bf16[64,8,256]{2,0,1:T(8,128)(2,1)}), bf16[64,8,256]{2,0,1:T(8,128)(2,1)S(1)}, u32[]{:S(2)}, u32[]{:S(2)}) async-start(bf16[64,8,256]{2,0,1:T(8,128)(2,1)} %copy.96), calls=%async_computation.3 | async-start | bytes 524288 | tf_op jit(solution)/shard_map/all_to_all | solution.py:112
  91.0 13.2 %gather_fusion.1 = f32[2048]{0:T(1024)S(1)} fusion(f32[512]{0:T(512)S(1)} %maximum_divide_fusion, s32[2048]{0:T(1024)S(1)} %broadcast_clamp_fusion), kind=kCustom, calls=%fused_computation.3 | custom fusion | bytes 24576 | tf_op jit(solution)/shard_map/jit(_take)/gather | solution.py:131
  104.6 11.5 %scatter_custom_fusion.4 = f32[64,512]{0,1:T(8,128)S(1)} fusion(s32[2048]{0:T(1024)S(1)} %bitcast.171, f32[2048,64]{1,0:T(8,128)S(1)} %bitcast.167, f32[]{:T(128)} %constant.134.clone.1), kind=kCustom, calls=%fused_computation.59 | custom fusion | flops 131072 | bytes 131076 | tf_op jit(solution)/shard_map/scatter-add | solution.py:116
  116.3 0.9 multiply_convert_fusion.2
  117.9 6.2 %gather_fusion.4 = bf16[2048,64]{1,0:T(8,128)(2,1)S(1)} fusion(bf16[64,512]{0,1:T(8,128)(2,1)S(1)} %copy.100, s32[2048]{0:T(1024)S(1)} %broadcast_clamp_fusion.1), kind=kCustom, calls=%fused_computation.1.clone | custom fusion | bytes 532480 | tf_op jit(solution)/shard_map/jit(_take)/gather | solution.py:129
  124.3 0.8 multiply_convert_fusion.1
  125.1 6.0 %all-to-all-start.4 = ((bf16[64,8,256]{2,0,1:T(8,128)(2,1)}), bf16[64,8,256]{2,0,1:T(8,128)(2,1)}, u32[]{:S(2)}, u32[]{:S(2)}) async-start(bf16[64,8,256]{2,0,1:T(8,128)(2,1)} %multiply_convert_fusion.1), calls=%async_computation.4 | async-start | bytes 524288 | tf_op jit(solution)/shard_map/all_to_all | solution.py:133
  132.0 8.1 %all-to-all-done.4 = bf16[64,8,256]{2,0,1:T(8,128)(2,1)} async-done(((bf16[64,8,256]{2,0,1:T(8,128)(2,1)}), bf16[64,8,256]{2,0,1:T(8,128)(2,1)}, u32[]{:S(2)}, u32[]{:S(2)}) %all-to-all-start.4) | async-done | bytes 262176 | tf_op jit(solution)/shard_map/all_to_all | solution.py:133
  140.1 1.8 copy.102
  141.9 1.7 reshape.216
  143.6 1.7 copy.103
  145.3 2.1 gather_fusion.2
  147.5 1.6 copy_bitcast_fusion
  149.0 1.1 broadcast_in_dim.132.clone
  150.1 21.8 %while.32 = (s32[]{:T(128)}, f32[1920,256]{1,0:T(8,128)S(1)}, f32[237,30]{0,1:T(8,128)S(1)}, f32[256,1024]{1,0:T(8,128)}, s32[1024]{0:T(1024)S(1)}, /*index=5*/f...) while((s32[]{:T(128)}, f32[1920,256]{1,0:T(8,128)S(1)}, ...), condition=%wide.region_14.16_spmd.clone, body=%wide.region_13.15_spmd.clone.sunk | while | flops 1602539392 | bytes 28454508 | solution.py:165
  150.2 1.2 fusion.87
  151.4 1.5 bitcast_convert_fusion.2
  153.5 1.5 convolution_bitcast_fusion.4
  155.0 1.2 convolution_add_fusion.6
  156.2 1.2 copy.156
  157.4 0.9 constant_dynamic-update-slice_fusion.2
  158.3 1.6 fusion.88
  161.1 1.2 fusion.87
  162.3 1.5 bitcast_convert_fusion.2
  164.4 1.5 convolution_bitcast_fusion.4
  165.9 1.2 convolution_add_fusion.6
  167.1 1.2 copy.156
  168.3 0.9 constant_dynamic-update-slice_fusion.2
  169.2 1.7 fusion.88
  172.0 1.4 convolution_bitcast_fusion.1
  173.4 1.0 copy.123
  174.5 0.8 convolution_bitcast_fusion.2
  175.4 41.2 %psum.23 = f32[237,30]{0,1:T(8,128)S(1)} all-reduce(f32[237,30]{0,1:T(8,128)S(1)} %get-tuple-element.289), channel_id=1, replica_groups=mesh['dom'=8,'feat'=4] {'dom','feat'}, use_global_device_ids=true, to_apply=%region_20.22 | all-reduce | flops 7110 | bytes 56880 | tf_op jit(solution)/shard_map/psum | solution.py:187
  216.6 1.1 copy.126
  217.8 3.5 %scatter_custom_fusion.5 = f32[64,2048]{0,1:T(8,128)S(1)} fusion(s32[1024]{0:T(1024)} %bitcast.178, f32[64,1024]{0,1:T(8,128)S(1)} %copy.126, f32[]{:T(128)} %constant.134.clone.1), kind=kCustom, calls=%fused_computation.47 | custom fusion | bytes 786944 | tf_op jit(solution)/shard_map/scatter | solution.py:172
  221.3 1.1 copy.105
  222.4 4.8 %all-to-all-start.5 = ((f32[64,8,256]{2,0,1:T(8,128)}), f32[64,8,256]{2,0,1:T(8,128)S(1)}, u32[]{:S(2)}, u32[]{:S(2)}) async-start(f32[64,8,256]{2,0,1:T(8,128)} %copy.105), calls=%async_computation.5 | async-start | bytes 1048576 | tf_op jit(solution)/shard_map/all_to_all | solution.py:175
  227.9 1.0 copy.124
  228.9 51.5 %all-reduce.3.cloned.1.call-done = (f32[1920,256]{1,0:T(8,128)}, f32[256,64]{0,1:T(8,128)}) async-done(((f32[1920,256]{1,0:T(8,128)}, f32[256,64]{0,1:T(8,128)}), (f32[1920,256]{1,0:T(8,128)}, f32[256,64]{0,1:T(8,128)})) %all-reduce.3.cloned.1.call-update) | async-done | bytes 2031632 | tf_op jit(solution)/shard_map/psum | solution.py:186
  280.4 1.5 broadcast_multiply_fusion.1
  281.9 3.0 broadcast_multiply_fusion
  285.2 11.6 %scatter_fusion.1 = f32[64,512]{0,1:T(8,128)S(1)} fusion(f32[64,512]{0,1:T(8,128)S(1)} %copy.124, s32[2048]{0:T(1024)S(1)} %bitcast.168, f32[2048,64]{1,0:T(8,128)S(1)} %bitcast.162), kind=kCustom, calls=%fused_computation.11 | custom fusion | flops 131072 | bytes 1581056 | tf_op jit(solution)/shard_map/scatter-add | solution.py:179
  296.8 0.7 copy.107
  (109 shorter events, 12.5 us)
Async XLA Ops:
  8.0 108.3 %copy-start = (bf16[256,64]{0,1:T(8,128)(2,1)S(1)}, bf16[256,64]{0,1:T(8,128)(2,1)}, u32[]{:S(2)}) copy-start(bf16[256,64]{0,1:T(8,128)(2,1)} %param.18) | copy-start | bytes 98308
  10.5 13.1 %copy-start.11 = (s32[1024,1]{0,1:T(1,128)}, s32[1024,1]{0,1:T(1,128)S(1)}, u32[]{:S(2)}) copy-start(s32[1024,1]{0,1:T(1,128)S(1)} %get-tuple-element.435) | copy-start | bytes 12292
  15.5 18.6 %all-to-all-start.1 = ((s32[8,1,256]{2,1,0:T(1,128)}), s32[8,1,256]{2,1,0:T(1,128)S(1)}, u32[]{:S(2)}, u32[]{:S(2)}) async-start(s32[8,1,256]{2,1,0:T(1,128)} %bitcast.18), calls=%async_computation.1 | async-start | bytes 16384 | tf_op jit(solution)/shard_map/all_to_all | solution.py:61
  25.8 57.4 %copy-start.12 = (s32[8]{0:T(128)}, s32[8]{0:T(128)S(1)}, u32[]{:S(2)}) copy-start(s32[8]{0:T(128)S(1)} %fusion.39) | copy-start | bytes 100
  31.8 84.5 %copy-start.6 = (bf16[256,512]{1,0:T(8,128)(2,1)}, bf16[256,512]{1,0:T(8,128)(2,1)S(1)}, u32[]{:S(2)}) copy-start(bf16[256,512]{1,0:T(8,128)(2,1)S(1)} %all_gather.6) | copy-start | bytes 786436
  34.2 13.2 %all-to-all-start = ((s32[8,1,256]{2,1,0:T(1,128)}), s32[8,1,256]{2,1,0:T(1,128)S(1)}, u32[]{:S(2)}, u32[]{:S(2)}) async-start(s32[8,1,256]{2,1,0:T(1,128)} %bitcast.10), calls=%async_computation | async-start | bytes 16384 | tf_op jit(solution)/shard_map/all_to_all | solution.py:62
  47.4 20.7 %all-to-all-start.2 = ((bf16[64,8,256]{2,0,1:T(8,128)(2,1)}), bf16[64,8,256]{2,0,1:T(8,128)(2,1)S(1)}, u32[]{:S(2)}, u32[]{:S(2)}) async-start(bf16[64,8,256]{2,0,1:T(8,128)(2,1)} %select_bitcast_fusion), calls=%async_computation.2 | async-start | bytes 524288 | tf_op jit(solution)/shard_map/all_to_all | solution.py:65
  53.3 25.8 %copy-start.1 = (bf16[30,64,256]{2,1,0:T(8,128)(2,1)S(1)}, bf16[30,64,256]{2,1,0:T(8,128)(2,1)}, u32[]{:S(2)}) copy-start(bf16[30,64,256]{2,1,0:T(8,128)(2,1)} %param.19) | copy-start | bytes 2949124
  53.4 25.8 %copy-start.10 = (s32[1024]{0:T(1024)S(1)}, s32[1024]{0:T(1024)}, u32[]{:S(2)}) copy-start(s32[1024]{0:T(1024)} %param.24) | copy-start | bytes 12292
  53.4 25.8 %copy-start.14 = (f32[237,30]{0,1:T(8,128)S(1)}, f32[237,30]{0,1:T(8,128)}, u32[]{:S(2)}) copy-start(f32[237,30]{0,1:T(8,128)} %param.20) | copy-start | bytes 85324
  85.0 19.3 %all-to-all-start.3 = ((bf16[64,8,256]{2,0,1:T(8,128)(2,1)}), bf16[64,8,256]{2,0,1:T(8,128)(2,1)S(1)}, u32[]{:S(2)}, u32[]{:S(2)}) async-start(bf16[64,8,256]{2,0,1:T(8,128)(2,1)} %copy.96), calls=%async_computation.3 | async-start | bytes 524288 | tf_op jit(solution)/shard_map/all_to_all | solution.py:112
  104.2 12.1 %copy-start.13 = (bf16[64,512]{1,0:T(8,128)(2,1)S(1)}, bf16[64,512]{1,0:T(8,128)(2,1)}, u32[]{:S(2)}) copy-start(bf16[64,512]{1,0:T(8,128)(2,1)} %param.27) | copy-start | bytes 196612
  117.2 0.6 copy-start.8
  125.1 15.0 %all-to-all-start.4 = ((bf16[64,8,256]{2,0,1:T(8,128)(2,1)}), bf16[64,8,256]{2,0,1:T(8,128)(2,1)}, u32[]{:S(2)}, u32[]{:S(2)}) async-start(bf16[64,8,256]{2,0,1:T(8,128)(2,1)} %multiply_convert_fusion.1), calls=%async_computation.4 | async-start | bytes 524288 | tf_op jit(solution)/shard_map/all_to_all | solution.py:133
  131.1 85.5 %reduce-scatter.9.cloned.1.call-start = ((), (), s32[]{:S(2)}) async-start(), calls=%async_computation.9 | async-start | bytes 1310720
  150.1 4.9 %copy-start.3 = (bf16[256,1024]{1,0:T(8,128)(2,1)}, bf16[256,1024]{1,0:T(8,128)(2,1)S(1)}, u32[]{:S(2)}) copy-start(bf16[256,1024]{1,0:T(8,128)(2,1)S(1)} %get-tuple-element.608) | copy-start | bytes 1572868 | tf_op jit(solution)/shard_map/while
  158.3 1.7 copy-start.5
  160.0 1.0 copy-start.4
  161.0 4.9 %copy-start.3 = (bf16[256,1024]{1,0:T(8,128)(2,1)}, bf16[256,1024]{1,0:T(8,128)(2,1)S(1)}, u32[]{:S(2)}) copy-start(bf16[256,1024]{1,0:T(8,128)(2,1)S(1)} %get-tuple-element.608) | copy-start | bytes 1572868 | tf_op jit(solution)/shard_map/while
  169.2 1.7 copy-start.5
  170.9 1.0 copy-start.4
  171.9 3.4 %copy-start.2 = (f32[1920,256]{1,0:T(8,128)}, f32[1920,256]{1,0:T(8,128)S(1)}, u32[]{:S(2)}) copy-start(f32[1920,256]{1,0:T(8,128)S(1)} %get-tuple-element.288) | copy-start | bytes 5898244
  171.9 2.6 copy-start.7
  171.9 2.6 copy-start.9
  171.9 56.0 %reduce-scatter.7.cloned.1.call-start = ((), (), s32[]{:S(2)}) async-start(), calls=%async_computation.8 | async-start | bytes 655360
  174.4 106.0 %all-reduce.3.cloned.1.call-start = ((), (), s32[]{:S(2)}) async-start(), calls=%async_computation.10 | async-start | bytes 4063232 | tf_op jit(solution)/shard_map/psum | solution.py:186
  222.4 62.4 %all-to-all-start.5 = ((f32[64,8,256]{2,0,1:T(8,128)}), f32[64,8,256]{2,0,1:T(8,128)S(1)}, u32[]{:S(2)}, u32[]{:S(2)}) async-start(f32[64,8,256]{2,0,1:T(8,128)} %copy.105), calls=%async_computation.5 | async-start | bytes 1048576 | tf_op jit(solution)/shard_map/all_to_all | solution.py:175
Sparse Core Ops, SparseCore 0:
  172.1 23.2 reduce-scatter.8
  197.8 21.6 reduce-scatter.6
Sparse Core Ops, SparseCore 1:
  179.1 101.2 all-reduce.2
where the time goes:
time: 307 us; the launch traced here: 305 us
  local copies, waits for them, and re-layouts  62.4 us (20%)
  waiting for transfers between devices  59.6 us (19%)
  other arithmetic  57.8 us (19%)
  blocking collectives  54.4 us (18%)
  starting transfers between devices  36.4 us (12%)
  matrix products  18.1 us (6%)
  between operations  16 us (5%)
    psum x1, waiting for transfers between devices, body(): bases_total, self_total = lax.psum((grad_bases, self_term), 'dom')  51.5 us
    psum x1, blocking collectives, body(): coef_total = lax.psum(grad_coef, ('dom', 'feat'))  41.2 us
    scatter-add x1, other arithmetic, body(): jnp.zeros((entities,), jnp.float32).at[arriving].add(1.0, mode='drop')  14.7 us
    gather x2, local copies, waits for them, and re-layouts, body(): jnp.take(inverse_degree, arriving, mode='fill', fill_value=0.0)[None]  13.2 us
    scatter-add x1, other arithmetic, body(): source_sum = jnp.zeros((quarter, entities), jnp.float32).at[:, asked_rows...  11.6 us
    scatter-add x1, other arithmetic, body(): aggregate = jnp.zeros((quarter, entities), jnp.float32).at[:, arriving].a...  11.5 us
    all_to_all x1, waiting for transfers between devices, body(): lax.all_to_all(sent_back, 'dom', split_axis=1, concat_axis=1, tiled=True)  8.05 us
    all_to_all x1, starting transfers between devices, body(): lax.all_to_all(requests, 'dom', split_axis=0, concat_axis=0, tiled=True)  7.28 us
  transfers between devices with their start and end apart: 9, of which 2 were waited for; matrix products, arithmetic and copies ran while one was open for 18% of the time, Pallas kernels for 0%

commit v1 on v0

v1 whole, which is shorter than its diff:
```python
import functools

import jax
import jax.numpy as jnp
from jax import lax
from jax.experimental import pallas as pl
from jax.experimental.pallas import tpu as pltpu
from jax.sharding import PartitionSpec as P

BF = jnp.bfloat16
F32 = jnp.float32
I32 = jnp.int32
LANES = 128
NN = (((1,), (0,)), ((), ()))
NT = (((1,), (1,)), ((), ()))


def iota(shape, dim):
    return lax.broadcasted_iota(I32, shape, dim)


def hot(mask):
    return jnp.where(mask, 1.0, 0.0).astype(BF)


def dot(left, right, dims=NN):
    return lax.dot_general(left, right, dims, preferred_element_type=F32)


def call(kernel, out_shape, smem=(), scratch=(), count=0):
    specs = [
        pl.BlockSpec(memory_space=pltpu.SMEM if k in smem else pltpu.VMEM) for k in range(count)
    ]
    single = not isinstance(out_shape, (tuple, list))
    outs = pl.BlockSpec(memory_space=pltpu.VMEM)
    return pl.pallas_call(
        kernel,
        out_shape=out_shape,
        in_specs=specs,
        out_specs=outs if single else tuple(outs for _ in out_shape),
        scratch_shapes=scratch,
    )


def block_slots(owners, block_count, block_cap):
    slots = []
    for j in range(block_count):
        rank = jnp.int32(0)
        for k in range(j):
            rank = rank + jnp.where(owners[k] == owners[j], 1, 0)
        slots.append(owners[j] * block_cap + rank)
    return slots


def each(count, step):
    if count <= 8:
        for k in range(count):
            step(k)
    else:
        lax.fori_loop(0, count, lambda k, c: (step(k), c)[1], 0)


def plan_kernel(
    entities, slot_cap, block_cap, owners, valid, part, row, dst, send, slot_out, hot_scratch
):
    dom_count = send.shape[0]
    edge_count = part.shape[1]
    block_count = dst.shape[0]
    chunks = slot_cap // LANES
    before = hot(iota((LANES, LANES), 0) < iota((LANES, LANES), 1))
    ones = jnp.ones((LANES, LANES), BF)
    offset = jnp.zeros((dom_count, LANES), F32)
    for c in range(edge_count // LANES):
        lanes = slice(c * LANES, (c + 1) * LANES)
        here = part[:, lanes]
        mask = iota((dom_count, LANES), 0) == here
        chosen = hot(mask)
        rank = jnp.sum(jnp.where(mask, dot(chosen, before) + offset, 0.0), axis=0, keepdims=True)
        offset = offset + dot(chosen, ones)
        slot_out[:, lanes] = here * slot_cap + rank.astype(I32)
    rows = row[...]
    digits = jnp.concatenate(
        [
            (rows >> 8).astype(F32),
            (rows & 255).astype(F32),
            jnp.ones((1, edge_count), F32),
            jnp.zeros((13, edge_count), F32),
        ],
        axis=0,
    ).astype(BF)

    def ask(p):
        near = slot_out[...] - p * slot_cap
        hot_scratch[...] = hot(iota((slot_cap, edge_count), 0) == near)
        found = dot(digits, hot_scratch[...], NT)
        wanted = found[0:1] * 256.0 + found[1:2] + (1.0 - found[2:3]) * float(entities)
        wanted = wanted.astype(I32)
        for k in range(chunks):
            send[p, k : k + 1, :] = wanted[:, k * LANES : (k + 1) * LANES]
        for t in range(block_cap):
            send[p, chunks + t : chunks + t + 1, :] = jnp.full((1, LANES), entities, I32)

    each(dom_count, ask)
    for j in range(block_count):
        rank = jnp.int32(0)
        for k in range(j):
            rank = rank + jnp.where(owners[k] == owners[j], 1, 0)
        live = iota((1, LANES), 1) < valid[j]
        send[owners[j], pl.ds(chunks + rank, 1), :] = jnp.where(live, dst[j : j + 1, :], entities)


def asked_row(arrived, g, chunks):
    rows = [arrived[g, k : k + 1, :] for k in range(chunks)]
    return rows[0] if chunks == 1 else jnp.concatenate(rows, axis=1)


def serve_kernel(slot_cap, arrived, feats, served):
    chunks = slot_cap // LANES
    entities = feats.shape[1]

    def step(g):
        asked = asked_row(arrived, g, chunks)
        chosen = hot(iota((entities, slot_cap), 0) == asked)
        served[g] = dot(feats[...], chosen).astype(BF)

    each(served.shape[0], step)


def unslot_kernel(fetched, slot, feats, out, total):
    dom_count, quarter, slot_cap = fetched.shape
    edge_count = slot.shape[1]
    total[...] = jnp.zeros_like(total)

    def step(p):
        near = slot[...] - p * slot_cap
        chosen = hot(iota((slot_cap, edge_count), 0) == near)
        total[...] += dot(fetched[p], chosen)

    each(dom_count, step)
    out[:, :edge_count] = total[...].astype(BF)
    out[:, edge_count:] = feats[...]


def rel_hot(rel, width):
    return hot(iota((width, rel.shape[1]), 0) == rel)


def forward_kernel(block_cap, owners, gathered, bases, coef, rel, send, weights):
    slots, quarter, rows = send.shape
    edge_count = rel.shape[1]
    block_count = edge_count // rows
    basis_count = bases.shape[0] // quarter
    span = 2 * rows if block_count % 2 == 0 else rows
    group = 5
    send[...] = jnp.zeros_like(send)
    table = coef[...]
    high = table.astype(BF)
    rest = table - high.astype(F32)
    middle = rest.astype(BF)
    low = (rest - middle.astype(F32)).astype(BF)
    where = block_slots(owners, block_count, block_cap)
    for t in range(edge_count // span):
        lanes = slice(t * span, (t + 1) * span)
        chosen = rel_hot(rel[:, lanes], coef.shape[1])
        mix = dot(high, chosen) + dot(middle, chosen) + dot(low, chosen)
        weights[:, lanes] = mix
        x = gathered[:, lanes]
        total = jnp.zeros((quarter, span), F32)
        for c in range(0, basis_count, group):
            stop = min(c + group, basis_count)
            products = dot(bases[c * quarter : stop * quarter, :], x)
            for b in range(c, stop):
                part = products[(b - c) * quarter : (b - c + 1) * quarter]
                total = total + mix[b : b + 1, :] * part
        total = total.astype(BF)
        for k in range(span // rows):
            send[where[t * (span // rows) + k]] = total[:, k * rows : (k + 1) * rows]


def owner_kernel(
    slot_cap, block_cap, arrived, received, gathered, weight, cotangent, output, back, grad_pre, hots, flat
):
    slots, quarter, rows = received.shape
    entities = cotangent.shape[1]
    chunks = slot_cap // LANES
    width = slots * rows
    for s in range(slots):
        lanes = slice(s * rows, (s + 1) * rows)
        target = arrived[s // block_cap, chunks + s % block_cap : chunks + s % block_cap + 1, :]
        hots[:, lanes] = hot(iota((entities, rows), 0) == target)
        flat[:quarter, lanes] = received[s]
    flat[quarter:, :] = jnp.ones((16, width), BF)
    own = gathered[:, gathered.shape[1] - entities :]
    own_part = lax.dot_general(
        weight[...], own, (((0,), (0,)), ((), ())), preferred_element_type=F32
    )
    sums = dot(flat[...], hots[...], NT)
    inverse = 1.0 / jnp.maximum(sums[quarter : quarter + 1], 1.0)
    preact = own_part + inverse * sums[:quarter]
    gate = jax.nn.sigmoid(preact)
    output[...] = (preact * gate).astype(BF)
    pre = (cotangent[...].astype(F32) * gate * (1.0 + preact * (1.0 - gate))).astype(BF)
    grad_pre[...] = pre
    scaled = (inverse * pre.astype(F32)).astype(BF)
    for s in range(slots):
        back[s] = dot(scaled, hots[:, s * rows : (s + 1) * rows]).astype(BF)


def fill_combined(where, returned, weights, combined, basis_count):
    quarter, rows = returned.shape[1:]
    for j, slot in enumerate(where):
        lanes = slice(j * rows, (j + 1) * rows)
        grad = returned[slot].astype(F32)
        for b in range(basis_count):
            combined[b * quarter : (b + 1) * quarter, lanes] = (
                weights[b : b + 1, lanes] * grad
            ).astype(BF)


def bases_kernel(block_cap, owners, returned, gathered, weights, grad_pre, out, combined):
    quarter, rows = returned.shape[1:]
    edge_count = weights.shape[1]
    total = combined.shape[0]
    where = block_slots(owners, edge_count // rows, block_cap)
    fill_combined(where, returned, weights, combined, total // quarter)
    x = gathered[:, :edge_count]
    chunk = 5 * quarter
    for start in range(0, total, chunk):
        stop = min(start + chunk, total)
        out[start:stop, :] = dot(combined[start:stop, :], x, NT).astype(BF)
    own = gathered[:, edge_count:]
    out[total : total + quarter, :] = dot(grad_pre[...], own, NT).astype(BF)
    out[total + quarter :, :] = jnp.zeros((out.shape[0] - total - quarter, out.shape[1]), BF)


def edges_kernel(
    block_cap, owners, returned, gathered, weights, grad_pre, bases, bases_t, weight, rel, out, combined, scaled
):
    quarter, rows = returned.shape[1:]
    edge_count = weights.shape[1]
    entities = grad_pre.shape[1]
    total = combined.shape[0]
    basis_count = total // quarter
    padded = weights.shape[0]
    relations = 2 * LANES
    where = block_slots(owners, edge_count // rows, block_cap)
    fill_combined(where, returned, weights, combined, basis_count)
    peers = out.shape[0]
    share = out.shape[1]
    span = 2 * rows if (edge_count // rows) % 2 == 0 else rows
    scaled[...] = jnp.zeros_like(scaled)
    for t in range(edge_count // span):
        lanes = slice(t * span, (t + 1) * span)
        partial = dot(bases_t[...], combined[:, lanes]).astype(BF)
        for f in range(peers):
            out[f, :, lanes] = partial[f * share : (f + 1) * share]
        x = gathered[:, lanes]
        count = span // rows
        grad = [returned[where[t * count + k]].astype(F32) for k in range(count)]
        grad = grad[0] if count == 1 else jnp.concatenate(grad, axis=1)
        group = 5
        for c in range(0, basis_count, group):
            stop = min(c + group, basis_count)
            products = dot(bases[c * quarter : stop * quarter, :], x)
            for b in range(c, stop):
                part = products[(b - c) * quarter : (b - c + 1) * quarter]
                scaled[b : b + 1, lanes] = jnp.sum(part * grad, axis=0, keepdims=True)
    high = scaled[...].astype(BF)
    low = (scaled[...] - high.astype(F32)).astype(BF)
    chosen = rel_hot(rel[...], relations)
    coef = (dot(high, chosen, NT) + dot(low, chosen, NT)).astype(BF)
    own = dot(weight[...], grad_pre[...]).astype(BF)
    tail = edge_count + entities
    for f in range(peers):
        out[f, :, edge_count:tail] = own[f * share : (f + 1) * share]
        out[f, :padded, tail:] = coef[:, :LANES]
        out[f, padded : 2 * padded, tail:] = coef[:, LANES:]


def slots_kernel(padded, arrived, slot, out, own):
    peers, share, width = arrived.shape
    dom_count, height, slot_cap = out.shape
    edge_count = slot.shape[1]
    entities = own.shape[1]
    sums = arrived[0].astype(F32)
    for f in range(1, peers):
        sums = sums + arrived[f].astype(F32)
    own[...] = sums[:, edge_count : edge_count + entities]
    edges = sums[:, :edge_count].astype(BF)
    coef = sums[: 2 * padded, edge_count + entities :].astype(BF)

    def step(p):
        near = slot[...] - p * slot_cap
        chosen = hot(iota((slot_cap, edge_count), 0) == near)
        out[p, :share, :] = dot(edges, chosen, NT).astype(BF)
        if slot_cap >= 2 * LANES:
            out[p, share:, :LANES] = coef[:padded]
            out[p, share:, LANES : 2 * LANES] = coef[padded:]
        else:
            out[p, share:, :] = coef

    each(dom_count, step)


def feats_kernel(slot_cap, padded, scale, arrived, asked, own, out, coef, total):
    dom_count, height, _ = arrived.shape
    share, entities = own.shape
    chunks = slot_cap // LANES
    total[...] = own[...]
    coef[...] = jnp.zeros_like(coef)

    def step(g):
        chosen = hot(iota((entities, slot_cap), 0) == asked_row(asked, g, chunks))
        total[...] += dot(arrived[g, :share, :], chosen, NT)
        if slot_cap >= 2 * LANES:
            coef[...] += arrived[g, share:, : 2 * LANES].astype(F32)
        else:
            coef[:, :LANES] += arrived[g, share : share + padded, :].astype(F32)
            coef[:, LANES:] += arrived[g, share + padded :, :].astype(F32)

    each(dom_count, step)
    out[...] = total[...].astype(BF)
    coef[...] = coef[...] * scale


def reduce_kernel(scale, parts, out):
    sums = parts[0].astype(F32)
    for k in range(1, parts.shape[0]):
        sums = sums + parts[k].astype(F32)
    out[...] = (sums * scale).astype(BF)


def body(
    feats,
    self_weight,
    bases,
    coef,
    src_part,
    src_row,
    edge_dst,
    edge_rel,
    block_owner,
    block_valid,
    cotangent,
):
    dom_count = lax.axis_size("dom")
    feat_count = lax.axis_size("feat")
    quarter, entities = feats.shape
    edge_count = src_row.shape[0]
    block_count = block_valid.shape[1]
    rows = edge_count // block_count
    slot_cap = LANES * ((2 * edge_count + LANES * dom_count - 1) // (LANES * dom_count))
    block_cap = (2 * block_count + dom_count - 1) // dom_count
    basis_count, _, model = bases.shape
    relation_count = coef.shape[0]
    flat = basis_count * quarter
    padded = 8 * ((basis_count + 7) // 8)
    padded = 16 * ((padded + 15) // 16)
    shape = jax.ShapeDtypeStruct
    scale = float(edge_count * dom_count) ** (-0.5)

    owners = block_owner[:, 0]
    valid = block_valid[0]
    rel = edge_rel.reshape(1, edge_count)
    bases_flat = bases.reshape(flat, model)
    coef_t = jnp.zeros((padded, 2 * LANES), F32).at[:basis_count, :relation_count].set(coef.T)

    height = slot_cap // LANES + block_cap
    send, slot = call(
        functools.partial(plan_kernel, entities, slot_cap, block_cap),
        (shape((dom_count, height, LANES), I32), shape((1, edge_count), I32)),
        smem=(0, 1),
        scratch=[pltpu.VMEM((slot_cap, edge_count), BF)],
        count=5,
    )(
        owners,
        valid,
        src_part.reshape(1, edge_count),
        src_row.reshape(1, edge_count),
        edge_dst.reshape(block_count, rows),
    )
    arrived = lax.all_to_all(send, "dom", split_axis=0, concat_axis=0, tiled=True)
    served = call(
        functools.partial(serve_kernel, slot_cap),
        shape((dom_count, quarter, slot_cap), BF),
        count=2,
    )(arrived, feats)
    fetched = lax.all_to_all(served, "dom", split_axis=0, concat_axis=0, tiled=True)
    mine = call(
        unslot_kernel,
        shape((quarter, edge_count + entities), BF),
        scratch=[pltpu.VMEM((quarter, edge_count), F32)],
        count=3,
    )(fetched, slot, feats)
    gathered = lax.all_gather(mine, "feat", axis=0, tiled=True)

    messages, weights = call(
        functools.partial(forward_kernel, block_cap),
        (shape((dom_count * block_cap, quarter, rows), BF), shape((padded, edge_count), F32)),
        smem=(0,),
        count=5,
    )(owners, gathered, bases_flat, coef_t, rel)
    received = lax.all_to_all(messages, "dom", split_axis=0, concat_axis=0, tiled=True)
    total_slots = dom_count * block_cap * rows
    output, back, grad_pre = call(
        functools.partial(owner_kernel, slot_cap, block_cap),
        (
            shape((quarter, entities), BF),
            shape((dom_count * block_cap, quarter, rows), BF),
            shape((quarter, entities), BF),
        ),
        scratch=[pltpu.VMEM((entities, total_slots), BF), pltpu.VMEM((quarter + 16, total_slots), BF)],
        count=5,
    )(arrived, received, gathered, self_weight, cotangent)
    returned = lax.all_to_all(back, "dom", split_axis=0, concat_axis=0, tiled=True)

    unit = 16 * dom_count
    tall = unit * ((flat + quarter + unit - 1) // unit)
    bases_part = call(
        functools.partial(bases_kernel, block_cap),
        shape((tall, model), BF),
        smem=(0,),
        scratch=[pltpu.VMEM((flat, edge_count), BF)],
        count=5,
    )(owners, returned, gathered, weights, grad_pre)
    parts = lax.all_to_all(
        bases_part.reshape(dom_count, tall // dom_count, model),
        "dom",
        split_axis=0,
        concat_axis=0,
        tiled=True,
    )
    edge_part = call(
        functools.partial(edges_kernel, block_cap),
        shape((feat_count, quarter, edge_count + entities + LANES), BF),
        smem=(0,),
        scratch=[pltpu.VMEM((flat, edge_count), BF), pltpu.VMEM((padded, edge_count), F32)],
        count=9,
    )(owners, returned, gathered, weights, grad_pre, bases_flat, bases_flat.T, self_weight, rel)
    edge_sum = lax.all_to_all(edge_part, "feat", split_axis=0, concat_axis=0, tiled=True)
    extra = padded * 2 * LANES // min(slot_cap, 2 * LANES)
    slot_grads, own_grads = call(
        functools.partial(slots_kernel, padded),
        (shape((dom_count, quarter + extra, slot_cap), BF), shape((quarter, entities), F32)),
        count=2,
    )(edge_sum, slot)
    arrived_grads = lax.all_to_all(slot_grads, "dom", split_axis=0, concat_axis=0, tiled=True)
    reduced = call(
        functools.partial(reduce_kernel, scale), shape((tall // dom_count, model), BF), count=1
    )(parts)
    near = [[2 * k, 2 * k + 1] for k in range(dom_count // 2)]
    far = [[2 * k + side for k in range(dom_count // 2)] for side in range(2)]
    pair = lax.all_gather(reduced, "dom", axis=0, tiled=True, axis_index_groups=near)
    whole = lax.all_gather(pair, "dom", axis=0, tiled=True, axis_index_groups=far)
    grad_feats, coef_total = call(
        functools.partial(feats_kernel, slot_cap, padded, scale),
        (shape((quarter, entities), BF), shape((padded, 2 * LANES), F32)),
        scratch=[pltpu.VMEM((quarter, entities), F32)],
        count=3,
    )(arrived_grads, arrived, own_grads)
    return (
        output,
        grad_feats,
        whole[:flat].astype(F32).reshape(basis_count, quarter, model),
        whole[flat : flat + quarter].astype(F32).T,
        coef_total[:basis_count, :relation_count].T,
    )


def solution(mesh):
    return jax.shard_map(
        body,
        mesh=mesh,
        in_specs=(
            P("feat", "dom"),
            P(None, "feat"),
            P(None, "feat", None),
            P(),
            P("dom", None),
            P("dom"),
            P("dom"),
            P("dom"),
            P("dom", None),
            P("dom", None),
            P("feat", "dom"),
        ),
        out_specs=(P("feat", "dom"), P("feat", "dom"), P(None, "feat", None), P(None, "feat"), P()),
        check_vma=False,
    )
```

time: 307 us -> 184 us (0.60)
  other arithmetic: 57.8 us -> 2.14 us
  local copies, waits for them, and re-layouts: 62.4 us -> 7.51 us
  blocking collectives: 54.4 us -> 105 us
  waiting for transfers between devices: 59.6 us -> 15.6 us
  Pallas kernels: 0 us -> 31.2 us
  starting transfers between devices: 36.4 us -> 6.87 us
  matrix products: 18.1 us -> 0 us
    all_to_all x0 -> x5, blocking collectives: none -> 89.1 us  [the longest x1 29.3 us: body(): lax.all_to_all(bases_part.reshape(dom_count, tall // dom_count, model), '...]
    psum x1 -> x0, waiting for transfers between devices: 51.5 us -> none  [body(): bases_total, self_total = lax.psum((grad_bases, self_term), 'dom')]
    psum x1 -> x0, blocking collectives: 41.2 us -> none  [body(): coef_total = lax.psum(grad_coef, ('dom', 'feat'))]
    scatter-add x3 -> x0, other arithmetic: 37.8 us -> none  [the longest x1 14.7 us: body(): jnp.zeros((entities,), jnp.float32).at[arriving].add(1.0, mode='drop')]
    gather x8 -> x0, local copies, waits for them, and re-layouts: 31.3 us -> none  [the longest x2 13.2 us: body(): jnp.take(inverse_degree, arriving, mode='fill', fill_value=0.0)[None]]
    pallas_call x0 -> x10, Pallas kernels: none -> 31.2 us  [the longest x1 5.56 us: body(): call(functools.partial(edges_kernel, block_cap), shape((feat_count, quart...]
    all_to_all x6 -> x2, starting transfers between devices: 36.1 us -> 6.83 us  [the longest x1 3.41 us: body(): lax.all_to_all(messages, 'dom', split_axis=0, concat_axis=0, tiled=True)]
    dot_general x18 -> x0, matrix products: 18.1 us -> none  [the longest x4 4.66 us: block_terms(): lax.dot_general(source_block, bases_flat, (((0,), (1,)), ((), ())), prefe...]
  transfers between devices with their start and end apart: 9 -> 3, of which waited for: 2 -> 2; matrix products, arithmetic and copies ran while one was open for 18% -> 3% of each run, Pallas kernels for 0% -> 6%
where the time goes in v1:
time: 184 us; the launch traced here: 183 us
  blocking collectives  105 us (57%)
  Pallas kernels  31.2 us (17%)
  waiting for transfers between devices  15.6 us (8%)
  between operations  14.1 us (8%)
  local copies, waits for them, and re-layouts  7.51 us (4%)
  starting transfers between devices  6.87 us (4%)
  other arithmetic  2.14 us (1%)
    all_to_all x1, blocking collectives, body(): lax.all_to_all(bases_part.reshape(dom_count, tall // dom_count, model), '...  29.3 us
    all_to_all x1, blocking collectives, body(): lax.all_to_all(edge_part, 'feat', split_axis=0, concat_axis=0, tiled=True)  16.6 us
    all_to_all x1, blocking collectives, body(): lax.all_to_all(slot_grads, 'dom', split_axis=0, concat_axis=0, tiled=True)  16.5 us
    all_to_all x1, blocking collectives, body(): lax.all_to_all(send, 'dom', split_axis=0, concat_axis=0, tiled=True)  14 us
    all_to_all x1, blocking collectives, body(): lax.all_to_all(back, 'dom', split_axis=0, concat_axis=0, tiled=True)  12.8 us
    all_gather x1, blocking collectives, body(): gathered = lax.all_gather(mine, 'feat', axis=0, tiled=True)  9.27 us
    all_to_all x1, waiting for transfers between devices, body(): lax.all_to_all(messages, 'dom', split_axis=0, concat_axis=0, tiled=True)  8.85 us
    all_gather x1, blocking collectives, body(): lax.all_gather(reduced, 'dom', axis=0, tiled=True, axis_index_groups=near)  6.86 us
  transfers between devices with their start and end apart: 3, of which 2 were waited for; matrix products, arithmetic and copies ran while one was open for 3% of the time, Pallas kernels for 6%

profile of v1, /device:TPU:0, one launch (start us, length us, event | category | flops | bytes accessed | tf_op | source)
XLA Modules:
  0.0 182.7 jit_solution(10623528867236108918)
XLA Ops:
  7.2 2.9 %shard_map.146 = (s32[8,4,128]{2,1,0:T(4,128)}, s32[1,1024]{1,0:T(1,128)}) custom-call(s32[8]{0:T(128)} %bitcast.25, s32[8]{0:T(128)} %bitcast.32, s32[1,1024]{1,0:T(1,128)} %bitcast.29, s32[1,1024]{1,0:T(1,128)} %bitcast.30, s32[8,128]{1,0:T(8,128)} %bitcast.31), custom_call_target="tpu_custom_call" | custom-call | tf_op jit(solution)/shard_map/pallas_call | solution.py:369
  10.1 14.0 %all_to_all.35.arrived.asked = s32[8,4,128]{2,1,0:T(4,128)} all-to-all(s32[8,4,128]{2,1,0:T(4,128)} %get-tuple-element.28), channel_id=1, replica_groups=mesh['dom'=8,'feat'=4] {'dom'}, dimensions={0} | all-to-all | bytes 32768 | tf_op jit(solution)/shard_map/all_to_all | solution.py:382
  24.0 2.0 %shard_map.147 = bf16[8,64,256]{2,1,0:T(8,128)(2,1)} custom-call(s32[8,4,128]{2,1,0:T(4,128)} %all_to_all.35.arrived.asked, bf16[64,512]{1,0:T(8,128)(2,1)} %feats.3), custom_call_target="tpu_custom_call" | custom-call | tf_op jit(solution)/shard_map/pallas_call | solution.py:383
  26.1 3.4 %all-to-all-start.1 = ((bf16[8,64,256]{2,1,0:T(8,128)(2,1)}), bf16[8,64,256]{2,1,0:T(8,128)(2,1)S(1)}, u32[]{:S(2)}, u32[]{:S(2)}) async-start(bf16[8,64,256]{2,1,0:T(8,128)(2,1)} %shard_map.147), calls=%async_computation.1 | async-start | bytes 524288 | tf_op jit(solution)/shard_map/all_to_all | solution.py:388
  29.5 0.0 copy-start.4
  29.5 1.4 scatter.4.coef
  30.9 6.8 %all-to-all-done.1.fetched = bf16[8,64,256]{2,1,0:T(8,128)(2,1)S(1)} async-done(((bf16[8,64,256]{2,1,0:T(8,128)(2,1)}), bf16[8,64,256]{2,1,0:T(8,128)(2,1)S(1)}, u32[]{:S(2)}, u32[]{:S(2)}) %all-to-all-start.1) | async-done | bytes 262176 | tf_op jit(solution)/shard_map/all_to_all | solution.py:388
  37.6 0.0 copy-start.2
  37.7 0.7 copy-done.2
  38.4 2.5 %shard_map.148 = bf16[64,1536]{1,0:T(8,128)(2,1)} custom-call(bf16[8,64,256]{2,1,0:T(8,128)(2,1)} %copy-done.2, s32[1,1024]{1,0:T(1,128)} %get-tuple-element.29.slot, bf16[64,512]{1,0:T(8,128)(2,1)} %feats.3), custom_call_target="tpu_custom_call" | custom-call | tf_op jit(solution)/shard_map/pallas_call | solution.py:389
  40.8 9.3 %all_gather.9.gathered = bf16[256,1536]{1,0:T(8,128)(2,1)} all-gather(bf16[64,1536]{1,0:T(8,128)(2,1)} %shard_map.148), channel_id=1, replica_groups=mesh['dom'=8,'feat'=4] {'feat'}, dimensions={0}, use_global_device_ids=true | all-gather | bytes 983040 | tf_op jit(solution)/shard_map/all_gather | solution.py:395
  50.1 3.6 %shard_map.149 = (bf16[16,64,128]{2,1,0:T(8,128)(2,1)}, f32[32,1024]{1,0:T(8,128)}) custom-call(s32[8]{0:T(128)} %bitcast.26, bf16[256,1536]{1,0:T(8,128)(2,1)} %all_gather.9.gathered, bf16[1920,256]{1,0:T(8,128)(2,1)} %bitcast.16, f32[32,256]{1,0:T(8,128)} %scatter.4.coef, s32[1,1024]{1,0:T(1,128)} %bitcast.23), custom_call_target="tpu_custom_call" | custom-call | tf_op jit(solution)/shard_map/pallas_call | solution.py:397
  53.7 3.4 %all-to-all-start.2 = ((bf16[16,64,128]{2,1,0:T(8,128)(2,1)}), bf16[16,64,128]{2,1,0:T(8,128)(2,1)S(1)}, u32[]{:S(2)}, u32[]{:S(2)}) async-start(bf16[16,64,128]{2,1,0:T(8,128)(2,1)} %get-tuple-element.30), calls=%async_computation.2 | async-start | bytes 524288 | tf_op jit(solution)/shard_map/all_to_all | solution.py:403
  57.1 0.0 all-gather.2.cloned.1.call-start
  57.1 0.0 copy-done.4
  57.1 0.7 copy.21.weight
  57.9 8.9 %all-to-all-done.2.received = bf16[16,64,128]{2,1,0:T(8,128)(2,1)S(1)} async-done(((bf16[16,64,128]{2,1,0:T(8,128)(2,1)}), bf16[16,64,128]{2,1,0:T(8,128)(2,1)S(1)}, u32[]{:S(2)}, u32[]{:S(2)}) %all-to-all-start.2) | async-done | bytes 262176 | tf_op jit(solution)/shard_map/all_to_all | solution.py:403
  66.7 0.0 copy-start.3
  66.7 0.7 copy-done.3
  67.4 3.4 %shard_map.150 = (bf16[64,512]{1,0:T(8,128)(2,1)}, bf16[16,64,128]{2,1,0:T(8,128)(2,1)}, bf16[64,512]{1,0:T(8,128)(2,1)}) custom-call(s32[8,4,128]{2,1,0:T(4,128)} %all_to_all.35.arrived.asked, bf16[16,64,128]{2,1,0:T(8,128)(2,1)} %copy-done.3, bf16[256,1536]{1,0:T(8,128)(2,1)} %all_gather.9.gathered, bf16[256,64]{1,0:T(8,128)(2,1)} %copy.21.weight, ...), custom_call_target="tpu_custom_call" | custom-call | tf_op jit(solution)/shard_map/pallas_call | solution.py:405
  70.8 12.8 %all_to_all.36.returned = bf16[16,64,128]{2,1,0:T(8,128)(2,1)} all-to-all(bf16[16,64,128]{2,1,0:T(8,128)(2,1)} %get-tuple-element.32), channel_id=1, replica_groups=mesh['dom'=8,'feat'=4] {'dom'}, dimensions={0} | all-to-all | bytes 524288 | tf_op jit(solution)/shard_map/all_to_all | solution.py:415
  83.6 3.5 %shard_map.154 = bf16[2048,256]{1,0:T(8,128)(2,1)} custom-call(s32[8]{0:T(128)} %bitcast.27, bf16[16,64,128]{2,1,0:T(8,128)(2,1)} %all_to_all.36.returned, bf16[256,1536]{1,0:T(8,128)(2,1)} %all_gather.9.gathered, f32[32,1024]{1,0:T(8,128)} %get-tuple-element.33.weights, bf16[64,512]{1,0:T(8,128)(2,1)} %get-tuple-element.34.grad_pre), custom_call_target="tpu_custom_call" | custom-call | tf_op jit(solution)/shard_map/pallas_call | solution.py:419
  87.1 0.0 copy-start
  87.1 29.3 %all_to_all.37.parts = bf16[8,256,256]{2,1,0:T(8,128)(2,1)} all-to-all(bf16[8,256,256]{2,1,0:T(8,128)(2,1)} %bitcast.19), channel_id=1, replica_groups=mesh['dom'=8,'feat'=4] {'dom'}, dimensions={0} | all-to-all | bytes 2097152 | tf_op jit(solution)/shard_map/all_to_all | solution.py:426
  116.4 2.0 %shard_map.155 = bf16[256,256]{1,0:T(8,128)(2,1)} custom-call(bf16[8,256,256]{2,1,0:T(8,128)(2,1)} %all_to_all.37.parts), custom_call_target="tpu_custom_call" | custom-call | tf_op jit(solution)/shard_map/pallas_call | solution.py:448
  118.4 6.9 %all_gather.10 = bf16[512,256]{1,0:T(8,128)(2,1)} all-gather(bf16[256,256]{1,0:T(8,128)(2,1)} %shard_map.155), channel_id=1, replica_groups={{0,4},{8,12},{16,20},{24,28},{1,5},{9,13},{17,21},{25,29},{2,6},{10,14}..., dimensions={0}, use_global_device_ids=true | all-gather | bytes 393216 | tf_op jit(solution)/shard_map/all_gather | solution.py:453
  125.3 0.0 all-gather.2.cloned.1.call-update
  125.3 0.0 copy-done
  125.3 1.4 copy.22
  126.7 5.6 %shard_map.151 = bf16[4,64,1664]{2,1,0:T(8,128)(2,1)} custom-call(s32[8]{0:T(128)} %bitcast.28, bf16[16,64,128]{2,1,0:T(8,128)(2,1)} %all_to_all.36.returned, bf16[256,1536]{1,0:T(8,128)(2,1)} %all_gather.9.gathered, f32[32,1024]{1,0:T(8,128)} %get-tuple-element.33.weights, bf16[64,512]{1,0:T(8,128)(2,1)} %get-tuple-element.34.grad_pre, ...), custom_call_target="tpu_custom_call" | custom-call | tf_op jit(solution)/shard_map/pallas_call | solution.py:433
  132.3 16.6 %all_to_all.38.arrived = bf16[4,64,1664]{2,1,0:T(8,128)(2,1)} all-to-all(bf16[4,64,1664]{2,1,0:T(8,128)(2,1)} %shard_map.151), channel_id=1, replica_groups=mesh['dom'=8,'feat'=4] {'feat'}, dimensions={0} | all-to-all | bytes 1703936 | tf_op jit(solution)/shard_map/all_to_all | solution.py:440
  148.9 3.3 %shard_map.152 = (bf16[8,96,256]{2,1,0:T(8,128)(2,1)}, f32[64,512]{1,0:T(8,128)}) custom-call(bf16[4,64,1664]{2,1,0:T(8,128)(2,1)} %all_to_all.38.arrived, s32[1,1024]{1,0:T(1,128)} %get-tuple-element.29.slot), custom_call_target="tpu_custom_call" | custom-call | tf_op jit(solution)/shard_map/pallas_call | solution.py:442
  152.2 16.5 %all_to_all.39.arrived = bf16[8,96,256]{2,1,0:T(8,128)(2,1)} all-to-all(bf16[8,96,256]{2,1,0:T(8,128)(2,1)} %get-tuple-element.35), channel_id=1, replica_groups=mesh['dom'=8,'feat'=4] {'dom'}, dimensions={0} | all-to-all | bytes 786432 | tf_op jit(solution)/shard_map/all_to_all | solution.py:447
  168.7 2.4 %shard_map.153 = (bf16[64,512]{1,0:T(8,128)(2,1)}, f32[32,256]{1,0:T(8,128)}) custom-call(bf16[8,96,256]{2,1,0:T(8,128)(2,1)} %all_to_all.39.arrived, s32[8,4,128]{2,1,0:T(4,128)} %all_to_all.35.arrived.asked, f32[64,512]{1,0:T(8,128)} %get-tuple-element.36.own), custom_call_target="tpu_custom_call" | custom-call | tf_op jit(solution)/shard_map/pallas_call | solution.py:455
  171.1 1.4 slice_bitcast_fusion
  172.5 0.0 all-gather.2.cloned.1.call-done
  172.5 0.0 slice-start
  172.5 0.0 copy-start.1
  172.5 1.2 slice-done
  173.7 1.5 convert.2
  175.2 0.0 copy-done.1
  175.2 0.6 convert_bitcast_fusion
Async XLA Ops:
  26.1 11.6 %all-to-all-start.1 = ((bf16[8,64,256]{2,1,0:T(8,128)(2,1)}), bf16[8,64,256]{2,1,0:T(8,128)(2,1)S(1)}, u32[]{:S(2)}, u32[]{:S(2)}) async-start(bf16[8,64,256]{2,1,0:T(8,128)(2,1)} %shard_map.147), calls=%async_computation.1 | async-start | bytes 524288 | tf_op jit(solution)/shard_map/all_to_all | solution.py:388
  29.5 27.7 %copy-start.4 = (bf16[256,64]{0,1:T(8,128)(2,1)S(1)}, bf16[256,64]{0,1:T(8,128)(2,1)}, u32[]{:S(2)}) copy-start(bf16[256,64]{0,1:T(8,128)(2,1)} %param.14) | copy-start | bytes 98308
  37.6 0.7 copy-start.2
  53.7 13.1 %all-to-all-start.2 = ((bf16[16,64,128]{2,1,0:T(8,128)(2,1)}), bf16[16,64,128]{2,1,0:T(8,128)(2,1)S(1)}, u32[]{:S(2)}, u32[]{:S(2)}) async-start(bf16[16,64,128]{2,1,0:T(8,128)(2,1)} %get-tuple-element.30), calls=%async_computation.2 | async-start | bytes 524288 | tf_op jit(solution)/shard_map/all_to_all | solution.py:403
  57.1 115.4 %all-gather.2.cloned.1.call-start = ((), (), s32[]{:S(2)}) async-start(), calls=%async_computation.7 | async-start | bytes 1310720 | tf_op jit(solution)/shard_map/all_gather | solution.py:454
  66.7 0.7 copy-start.3
  87.1 38.2 %copy-start = (bf16[30,64,256]{2,1,0:T(8,128)(2,1)S(1)}, bf16[30,64,256]{2,1,0:T(8,128)(2,1)}, u32[]{:S(2)}) copy-start(bf16[30,64,256]{2,1,0:T(8,128)(2,1)} %param.15) | copy-start | bytes 2949124
  172.5 1.2 slice-start
  172.5 2.7 %copy-start.1 = (bf16[2048,256]{1,0:T(8,128)(2,1)S(1)}, bf16[2048,256]{1,0:T(8,128)(2,1)}, u32[]{:S(2)}) copy-start(bf16[2048,256]{1,0:T(8,128)(2,1)} %all-gather.2.cloned.1.call-done) | copy-start | bytes 3145732
Sparse Core Ops, SparseCore 0:
  125.4 25.3 all-gather.1

commit v2 on v1

--- a/solution.py
+++ b/solution.py
@@ -7,6 +7,7 @@
 from jax.experimental.pallas import tpu as pltpu
 from jax.sharding import PartitionSpec as P
 
+
 BF = jnp.bfloat16
 F32 = jnp.float32
 I32 = jnp.int32
@@ -27,7 +28,7 @@
     return lax.dot_general(left, right, dims, preferred_element_type=F32)
 
 
-def call(kernel, out_shape, smem=(), scratch=(), count=0):
+def call(kernel, out_shape, smem=(), scratch=(), count=0, us=4):
     specs = [
         pl.BlockSpec(memory_space=pltpu.SMEM if k in smem else pltpu.VMEM) for k in range(count)
     ]
@@ -39,6 +40,9 @@
         in_specs=specs,
         out_specs=outs if single else tuple(outs for _ in out_shape),
         scratch_shapes=scratch,
+        cost_estimate=pl.CostEstimate(
+            flops=us * 1_000_000_000, bytes_accessed=1 << 20, transcendentals=0
+        ),
     )
 
 
@@ -127,7 +131,7 @@
 
 
 def unslot_kernel(fetched, slot, feats, out, total):
-    dom_count, quarter, slot_cap = fetched.shape
+    dom_count, _, slot_cap = fetched.shape
     edge_count = slot.shape[1]
     total[...] = jnp.zeros_like(total)
 
@@ -146,7 +150,7 @@
 
 
 def forward_kernel(block_cap, owners, gathered, bases, coef, rel, send, weights):
-    slots, quarter, rows = send.shape
+    _, quarter, rows = send.shape
     edge_count = rel.shape[1]
     block_count = edge_count // rows
     basis_count = bases.shape[0] // quarter
@@ -278,8 +282,8 @@
 
 
 def slots_kernel(padded, arrived, slot, out, own):
-    peers, share, width = arrived.shape
-    dom_count, height, slot_cap = out.shape
+    peers, share, _ = arrived.shape
+    dom_count, _, slot_cap = out.shape
     edge_count = slot.shape[1]
     entities = own.shape[1]
     sums = arrived[0].astype(F32)
@@ -303,7 +307,7 @@
 
 
 def feats_kernel(slot_cap, padded, scale, arrived, asked, own, out, coef, total):
-    dom_count, height, _ = arrived.shape
+    dom_count, _, _ = arrived.shape
     share, entities = own.shape
     chunks = slot_cap // LANES
     total[...] = own[...]
@@ -330,7 +334,7 @@
     out[...] = (sums * scale).astype(BF)
 
 
-def body(
+def body_many(
     feats,
     self_weight,
     bases,
@@ -467,7 +471,543 @@
     )
 
 
+def pack_kernel(owners, valid, feats, part, row, dst, rel, out):
+    copies = out.shape[0]
+    quarter, entities = feats.shape
+    blocks = part.shape[0]
+    owner = jnp.zeros((blocks, LANES), I32)
+    live = jnp.zeros((blocks, LANES), I32)
+    for j in range(blocks):
+        here = iota((blocks, LANES), 0) == j
+        owner = jnp.where(here, owners[j], owner)
+        live = jnp.where(here, valid[j], live)
+    target = jnp.where(iota((blocks, LANES), 1) < live, dst[...], entities)
+    digits = [
+        part[...],
+        row[...] >> 8,
+        row[...] & 255,
+        owner,
+        target >> 8,
+        target & 255,
+        rel[...] >> 8,
+        rel[...] & 255,
+    ]
+    digits = jnp.concatenate([d.astype(F32) for d in digits], axis=0).astype(BF)
+    chunks = entities // LANES
+    for k in range(copies):
+        for c in range(chunks):
+            out[k, c * quarter : (c + 1) * quarter, :] = feats[:, c * LANES : (c + 1) * LANES]
+        out[k, chunks * quarter :, :] = digits
+
+
+def source_kernel(
+    shared, feats, part, row, mine, wide, ids, spans, targets, rels, owners, total, hots
+):
+    dom_count = shared.shape[0]
+    quarter, entities = feats.shape
+    blocks = part.shape[0]
+    chunks = entities // LANES
+    edge_count = blocks * LANES
+    for g in range(dom_count):
+        for c in range(chunks):
+            start = g * entities + c * LANES
+            wide[:, start : start + LANES] = shared[g, c * quarter : (c + 1) * quarter, :]
+        digits = shared[g, chunks * quarter :, :].astype(F32).astype(I32)
+        piece = [digits[d * blocks : (d + 1) * blocks] for d in range(8)]
+        at = piece[0] * entities + piece[1] * 256 + piece[2]
+        ids[g] = at
+        for t in range(blocks // 2):
+            spans[g * (blocks // 2) + t] = jnp.concatenate(
+                [at[2 * t : 2 * t + 1], at[2 * t + 1 : 2 * t + 2]], axis=1
+            )
+        owners[g] = piece[3]
+        targets[g] = piece[4] * 256 + piece[5]
+        rels[g] = piece[6] * 256 + piece[7]
+    total[...] = jnp.zeros_like(total)
+    for p in range(dom_count):
+        near = jnp.where(part[...] == p, row[...], -1)
+        for j in range(blocks):
+            hots[:, j * LANES : (j + 1) * LANES] = hot(
+                iota((entities, LANES), 0) == near[j : j + 1, :]
+            )
+        total[...] += dot(wide[:, p * entities : (p + 1) * entities], hots[...])
+    mine[:, :edge_count] = total[...].astype(BF)
+    mine[:, edge_count:] = feats[...]
+
+
+def split3(table):
+    high = table.astype(BF)
+    rest = table - high.astype(F32)
+    middle = rest.astype(BF)
+    low = (rest - middle.astype(F32)).astype(BF)
+    return high, middle, low
+
+
+def message_kernel(block_cap, entities, owners, valid, gathered, bases, coef, rel, dst, send):
+    slots, tall, rows = send.shape
+    blocks = rel.shape[0]
+    quarter = tall - 16
+    basis_count = bases.shape[0] // quarter
+    group = 5
+    first = iota((16, rows), 0)
+    empty = jnp.where(first == 0, entities >> 8, jnp.where(first == 1, entities & 255, 0))
+    empty = empty.astype(F32).astype(BF)
+    for s in range(slots):
+        send[s, :quarter, :] = jnp.zeros((quarter, rows), BF)
+        send[s, quarter:, :] = empty
+    parts = split3(coef[...])
+    where = block_slots(owners, blocks, block_cap)
+    for t in range(blocks // 2):
+        lanes = slice(2 * t * rows, 2 * (t + 1) * rows)
+        both = jnp.concatenate([rel[2 * t : 2 * t + 1, :], rel[2 * t + 1 : 2 * t + 2, :]], axis=1)
+        chosen = rel_hot(both, coef.shape[1])
+        mix = sum(dot(p, chosen) for p in parts)
+        x = gathered[:, lanes]
+        total = jnp.zeros((quarter, 2 * rows), F32)
+        for c in range(0, basis_count, group):
+            stop = min(c + group, basis_count)
+            products = dot(bases[c * quarter : stop * quarter, :], x)
+            for b in range(c, stop):
+                part = products[(b - c) * quarter : (b - c + 1) * quarter]
+                total = total + mix[b : b + 1, :] * part
+        total = total.astype(BF)
+        for k in range(2):
+            j = 2 * t + k
+            slot = where[j]
+            live = iota((1, rows), 1) < valid[j]
+            target = jnp.where(live, dst[j : j + 1, :], entities)
+            code = jnp.where(first == 0, target >> 8, jnp.where(first == 1, target & 255, 0))
+            send[slot, :quarter, :] = total[:, k * rows : (k + 1) * rows]
+            send[slot, quarter:, :] = code.astype(F32).astype(BF)
+
+
+def node_kernel(received, gathered, weight, cotangent, output, share, grad_pre, hots, flat):
+    slots, _, rows = received.shape
+    quarter, entities = cotangent.shape
+    copies = share.shape[0]
+    for s in range(slots):
+        lanes = slice(s * rows, (s + 1) * rows)
+        code = received[s, quarter:, :].astype(F32).astype(I32)
+        target = code[0:1] * 256 + code[1:2]
+        hots[:, lanes] = hot(iota((entities, rows), 0) == target)
+        flat[:quarter, lanes] = received[s, :quarter, :]
+    flat[quarter:, :] = jnp.ones((16, slots * rows), BF)
+    own = gathered[:, gathered.shape[1] - entities :]
+    own_part = dot(weight[...], own)
+    sums = dot(flat[...], hots[...], NT)
+    count = sums[quarter : quarter + 1]
+    inverse = 1.0 / jnp.maximum(count, 1.0)
+    preact = own_part + inverse * sums[:quarter]
+    gate = jax.nn.sigmoid(preact)
+    output[...] = (preact * gate).astype(BF)
+    pre = (cotangent[...].astype(F32) * gate * (1.0 + preact * (1.0 - gate))).astype(BF)
+    grad_pre[...] = pre
+    whole = count.astype(I32)
+    first = iota((16, entities), 0)
+    code = jnp.where(first == 0, whole >> 8, jnp.where(first == 1, whole & 255, 0))
+    code = code.astype(F32).astype(BF)
+    for k in range(copies):
+        share[k, :quarter, :] = pre
+        share[k, quarter:, :] = code
+
+
+def scaled_grad(shared, q, quarter):
+    code = shared[q, quarter:, :].astype(F32)
+    count = code[0:1] * 256.0 + code[1:2]
+    inverse = 1.0 / jnp.maximum(count, 1.0)
+    return (inverse * shared[q, :quarter, :].astype(F32)).astype(BF)
+
+
+def rows_of_edges_kernel(entities, place, spans, *refs):
+    pieces, out, full = refs[:-2], refs[-2], refs[-1]
+    count, width, model = out.shape
+    quarter = pieces[0].shape[0]
+    for k, piece in enumerate(pieces):
+        full[pl.ds(pl.multiple_of(place[k] * quarter, quarter), quarter), :] = piece[...]
+
+    def step(n, carry):
+        row = spans[place[0] * count + n]
+        total = jnp.zeros((model, width), F32)
+        for start in range(0, full.shape[1], entities):
+            chosen = hot(iota((entities, width), 0) == row - start)
+            total = total + dot(full[:, start : start + entities], chosen)
+        out[n] = total.T.astype(BF)
+        return carry
+
+    lax.fori_loop(0, count, step, 0)
+
+
+def rank_kernel(
+    slot_cap, entities, me, ids, rels, coef, ranks, slot_rows, slot_mix, mix, comp, digits, hots
+):
+    dom_count, blocks, _ = ids.shape
+    before = hot(iota((LANES, LANES), 0) < iota((LANES, LANES), 1))
+    ones = jnp.ones((LANES, LANES), BF)
+    table = coef[...].astype(BF)
+
+    def step(g, carry):
+        near = ids[g] - me[0] * entities
+        mask = (near >= 0) & (near < entities)
+        chosen = jnp.where(mask, 1.0, 0.0)
+        chosen = jnp.concatenate([chosen, jnp.zeros_like(chosen)], axis=0).astype(BF)
+        inside = dot(chosen, before)[:blocks]
+        totals = dot(chosen, ones)[:blocks]
+        offset = jnp.zeros((1, LANES), F32)
+        offsets = []
+        for j in range(blocks):
+            offsets.append(offset)
+            offset = offset + totals[j : j + 1]
+        rank = inside + jnp.concatenate(offsets, axis=0)
+        rank = jnp.where(mask, rank.astype(I32), -1)
+        ranks[g] = rank
+        rel = rels[g]
+        rows = jnp.where(mask, near, 0)
+        first = iota((16, LANES), 0)
+        for j in range(blocks):
+            lanes = slice(j * LANES, (j + 1) * LANES)
+            comp[:, lanes] = hot(iota((slot_cap, LANES), 0) == rank[j : j + 1, :])
+            at, kind = rows[j : j + 1, :], rel[j : j + 1, :]
+            code = jnp.where(first == 0, at >> 8, jnp.where(first == 1, at & 255, 0))
+            code = code + jnp.where(first == 2, kind >> 8, jnp.where(first == 3, kind & 255, 0))
+            digits[:, lanes] = code.astype(F32).astype(BF)
+            hots[:, lanes] = rel_hot(kind, coef.shape[1])
+        mix[g] = dot(table, hots[...])
+        found = dot(digits[...], comp[...], NT)
+        slot_rows[g] = (found[0:1] * 256.0 + found[1:2]).astype(I32)
+        kind = (found[2:3] * 256.0 + found[3:4]).astype(I32)
+        slot_mix[g] = dot(table, rel_hot(kind, coef.shape[1]))
+        return carry
+
+    lax.fori_loop(0, dom_count, step, 0)
+
+
+def coef_kernel(owners, valid, shared, gathered, bases, rel, dst, out, scaled, grads):
+    blocks = rel.shape[0]
+    copies, padded, relations = out.shape
+    entities = shared.shape[2]
+    quarter = shared.shape[1] - 16
+    basis_count = bases.shape[0] // quarter
+    group = 5
+    scaled[...] = jnp.zeros_like(scaled)
+    total = jnp.zeros((padded, relations), F32)
+    for j in range(blocks):
+        live = iota((1, LANES), 1) < valid[j]
+        target = jnp.where(live, dst[j : j + 1, :], entities)
+        chosen = hot(iota((entities, LANES), 0) == target)
+        grads[:, j * LANES : (j + 1) * LANES] = dot(scaled_grad(shared, owners[j], quarter), chosen)
+    for t in range(blocks // 2):
+        lanes = slice(2 * t * LANES, 2 * (t + 1) * LANES)
+        both = jnp.concatenate([rel[2 * t : 2 * t + 1, :], rel[2 * t + 1 : 2 * t + 2, :]], axis=1)
+        x = gathered[:, lanes]
+        grad = grads[:, lanes]
+        for c in range(0, basis_count, group):
+            stop = min(c + group, basis_count)
+            products = dot(bases[c * quarter : stop * quarter, :], x)
+            for b in range(c, stop):
+                part = products[(b - c) * quarter : (b - c + 1) * quarter]
+                scaled[b : b + 1, :] = jnp.sum(part * grad, axis=0, keepdims=True)
+        high = scaled[...].astype(BF)
+        low = (scaled[...] - high.astype(F32)).astype(BF)
+        chosen = rel_hot(both, relations)
+        total = total + dot(high, chosen, NT) + dot(low, chosen, NT)
+    total = total.astype(BF)
+    for k in range(copies):
+        out[k] = total
+
+
+def grads_kernel(owners, targets, ranks, shared, grads, slot_grads, scaled, comp):
+    dom_count, blocks, _ = targets.shape
+    slot_cap = comp.shape[1]
+    entities = shared.shape[2]
+    quarter = shared.shape[1] - 16
+    for q in range(dom_count):
+        scaled[q] = scaled_grad(shared, q, quarter)
+
+    def step(g, carry):
+        rows = targets[g]
+        rank = ranks[g]
+        for j in range(blocks):
+            lanes = slice(j * LANES, (j + 1) * LANES)
+            chosen = hot(iota((entities, LANES), 0) == rows[j : j + 1, :])
+            grads[g, :, lanes] = dot(scaled[owners[g * blocks + j]], chosen).astype(BF)
+            comp[g % 2, :, lanes] = hot(iota((slot_cap, LANES), 0) == rank[j : j + 1, :])
+        slot_grads[g] = dot(grads[g], comp[g % 2], NT).astype(BF)
+        return carry
+
+    for g in range(dom_count):
+        step(g, 0)
+
+
+def mix_rows(mix, grad, quarter):
+    pieces = []
+    for b in range(mix.shape[0]):
+        wide = jnp.broadcast_to(mix[b : b + 1, :], (16, mix.shape[1])).astype(BF)
+        for r in range(0, quarter, 16):
+            pieces.append(wide * grad[r : r + 16])
+    return jnp.concatenate(pieces, axis=0)
+
+
+def scatter_kernel(slot_grads, slot_rows, slot_mix, bases_t, weight, grad_pre, coefs, out, total):
+    dom_count, quarter, slot_cap = slot_grads.shape
+    padded = slot_mix.shape[1]
+    basis_count = bases_t.shape[1] // quarter
+    entities = grad_pre.shape[1]
+    peers = out.shape[0]
+    total[...] = lax.dot_general(
+        weight[...], grad_pre[...], (((0,), (0,)), ((), ())), preferred_element_type=F32
+    )
+
+    def step(g, carry):
+        combined = mix_rows(slot_mix[g][:basis_count], slot_grads[g], quarter)
+        partial = dot(bases_t[...], combined).astype(BF)
+        chosen = hot(iota((entities, slot_cap), 0) == slot_rows[g])
+        total[...] += dot(partial, chosen, NT)
+        return carry
+
+    for g in range(dom_count):
+        step(g, 0)
+    coef = coefs[0].astype(F32)
+    for g in range(1, dom_count):
+        coef = coef + coefs[g].astype(F32)
+    coef = coef.astype(BF)
+    for f in range(peers):
+        out[f, :, :entities] = total[f * quarter : (f + 1) * quarter].astype(BF)
+        out[f, :padded, entities:] = coef[:, :LANES]
+        out[f, padded : 2 * padded, entities:] = coef[:, LANES:]
+
+
+def weights_kernel(scale, place, mix, grads, full, shared, *refs):
+    rows, out, own_out = refs[:-2], refs[-2], refs[-1]
+    dom_count, quarter, _ = grads.shape
+    entities = shared.shape[2]
+    basis_count = out.shape[0] // quarter
+    group = 5
+    own = jnp.zeros(own_out.shape, F32)
+    for q in range(dom_count):
+        lanes = slice(q * entities, (q + 1) * entities)
+        own = own + dot(shared[q, :quarter, :], full[:, lanes], NT)
+    own_out[...] = own * scale
+    out[...] = jnp.zeros_like(out)
+    for part, piece in enumerate(rows):
+        count = piece.shape[0]
+
+        def step(k, carry):
+            g = place[part] * count + k
+            grad = grads[g]
+            for c in range(0, basis_count, group):
+                stop = min(c + group, basis_count)
+                combined = mix_rows(mix[g, c:stop, :], grad, quarter)
+                out[c * quarter : stop * quarter, :] += dot(combined, piece[k])
+            return carry
+
+        lax.fori_loop(0, count, step, 0)
+    out[...] = out[...] * scale
+
+
+def finish_kernel(padded, scale, arrived, after, grad_feats, coef_out):
+    peers, _, _ = arrived.shape
+    entities = grad_feats.shape[1]
+    sums = arrived[0].astype(F32)
+    for f in range(1, peers):
+        sums = sums + arrived[f].astype(F32)
+    grad_feats[...] = sums[:, :entities].astype(BF)
+    coef = jnp.concatenate([sums[:padded, entities:], sums[padded : 2 * padded, entities:]], axis=1)
+    coef_out[...] = coef[: coef_out.shape[0], : coef_out.shape[1]] * scale
+
+
+def body_few(
+    feats,
+    self_weight,
+    bases,
+    coef,
+    src_part,
+    src_row,
+    edge_dst,
+    edge_rel,
+    block_owner,
+    block_valid,
+    cotangent,
+):
+    dom_count = lax.axis_size("dom")
+    feat_count = lax.axis_size("feat")
+    quarter, entities = feats.shape
+    edge_count = src_row.shape[0]
+    blocks = block_valid.shape[1]
+    slot_cap = LANES * ((2 * edge_count + LANES * dom_count - 1) // (LANES * dom_count))
+    block_cap = (2 * blocks + dom_count - 1) // dom_count
+    basis_count, _, model = bases.shape
+    relation_count = coef.shape[0]
+    flat = basis_count * quarter
+    padded = 16 * ((basis_count + 15) // 16)
+    relations = 2 * LANES
+    shape = jax.ShapeDtypeStruct
+    scale = float(edge_count * dom_count) ** (-0.5)
+    owners = block_owner[:, 0]
+    valid = block_valid[0]
+    part = src_part.reshape(blocks, LANES)
+    row = src_row.reshape(blocks, LANES)
+    dst = edge_dst.reshape(blocks, LANES)
+    rel = edge_rel.reshape(blocks, LANES)
+    bases_flat = bases.reshape(flat, model)
+    bases_t = bases_flat.T
+    weight_t = self_weight.T
+    coef_t = jnp.zeros((padded, relations), F32).at[:basis_count, :relation_count].set(coef.T)
+    feat_place = lax.axis_index("feat").astype(I32)
+
+    tall = (entities // LANES) * quarter + 8 * blocks
+    packed = call(pack_kernel, shape((dom_count, tall, LANES), BF), smem=(0, 1), count=7, us=1)(
+        owners, valid, feats, part, row, dst, rel
+    )
+    shared = lax.all_to_all(packed, "dom", split_axis=0, concat_axis=0, tiled=True)
+    ints = shape((dom_count, blocks, LANES), I32)
+    mine, wide, ids, spans, targets, rels, all_owners = call(
+        source_kernel,
+        (
+            shape((quarter, edge_count + entities), BF),
+            shape((quarter, dom_count * entities), BF),
+            ints,
+            shape((dom_count * blocks // 2, 1, 2 * LANES), I32),
+            ints,
+            ints,
+            ints,
+        ),
+        scratch=[pltpu.VMEM((quarter, edge_count), F32), pltpu.VMEM((entities, edge_count), BF)],
+        count=4,
+        us=4,
+    )(shared, feats, part, row)
+    gathered = lax.all_gather(mine, "feat", axis=0, tiled=True)
+    owner_list = all_owners[:, :, 0].reshape(dom_count * blocks)
+
+    def doubled(piece):
+        pieces, bit, stage = [piece], feat_count // 2, 0
+        while bit >= 1:
+            links = [(f, f ^ bit) for f in range(feat_count)]
+            pieces = pieces + [lax.ppermute(piece, "feat", links) for piece in pieces]
+            bit //= 2
+            stage += 1
+        return pieces
+
+    places, bit = [0], feat_count // 2
+    while bit >= 1:
+        places = places + [place ^ bit for place in places]
+        bit //= 2
+    place = jnp.stack([feat_place ^ k for k in places])
+    wide, gathered = lax.optimization_barrier((wide, gathered))
+    part_count = dom_count // feat_count
+    rows, full = call(
+        functools.partial(rows_of_edges_kernel, entities),
+        (
+            shape((part_count * blocks // 2, 2 * LANES, model), BF),
+            shape((model, dom_count * entities), BF),
+        ),
+        smem=(0,),
+        count=2 + feat_count,
+        us=10,
+    )(place, spans, *doubled(wide))
+    rows = doubled(rows.reshape(part_count, edge_count, model))
+    ranks, slot_rows, slot_mix, mix = call(
+        functools.partial(rank_kernel, slot_cap, entities),
+        (
+            ints,
+            shape((dom_count, 1, slot_cap), I32),
+            shape((dom_count, padded, slot_cap), F32),
+            shape((dom_count, padded, edge_count), F32),
+        ),
+        smem=(0,),
+        scratch=[
+            pltpu.VMEM((slot_cap, edge_count), BF),
+            pltpu.VMEM((16, edge_count), BF),
+            pltpu.VMEM((relations, edge_count), BF),
+        ],
+        count=4,
+        us=4,
+    )(lax.axis_index("dom").astype(I32).reshape(1), ids, rels, coef_t)
+
+    messages = call(
+        functools.partial(message_kernel, block_cap, entities),
+        shape((dom_count * block_cap, quarter + 16, LANES), BF),
+        smem=(0, 1),
+        count=7,
+        us=4,
+    )(owners, valid, gathered, bases_flat, coef_t, rel, dst)
+    received = lax.all_to_all(messages, "dom", split_axis=0, concat_axis=0, tiled=True)
+    slots = dom_count * block_cap
+    output, share, grad_pre = call(
+        node_kernel,
+        (
+            shape((quarter, entities), BF),
+            shape((dom_count, quarter + 16, entities), BF),
+            shape((quarter, entities), BF),
+        ),
+        scratch=[
+            pltpu.VMEM((entities, slots * LANES), BF),
+            pltpu.VMEM((quarter + 16, slots * LANES), BF),
+        ],
+        count=4,
+        us=4,
+    )(received, gathered, weight_t, cotangent)
+    nodes = lax.all_to_all(share, "dom", split_axis=0, concat_axis=0, tiled=True)
+
+    coef_part = call(
+        coef_kernel,
+        shape((dom_count, padded, relations), BF),
+        smem=(0, 1),
+        scratch=[pltpu.VMEM((padded, 2 * LANES), F32), pltpu.VMEM((quarter, edge_count), F32)],
+        count=7,
+        us=4,
+    )(owners, valid, nodes, gathered, bases_flat, rel, dst)
+    coefs = lax.all_to_all(coef_part, "dom", split_axis=0, concat_axis=0, tiled=True)
+    grads, slot_grads = call(
+        grads_kernel,
+        (shape((dom_count, quarter, edge_count), BF), shape((dom_count, quarter, slot_cap), BF)),
+        smem=(0,),
+        scratch=[
+            pltpu.VMEM((dom_count, quarter, entities), BF),
+            pltpu.VMEM((2, slot_cap, edge_count), BF),
+        ],
+        count=4,
+        us=6,
+    )(owner_list, targets, ranks, nodes)
+    sent = call(
+        scatter_kernel,
+        shape((feat_count, quarter, entities + LANES), BF),
+        scratch=[pltpu.VMEM((model, entities), F32)],
+        count=7,
+        us=5,
+    )(slot_grads, slot_rows, slot_mix, bases_t, weight_t, grad_pre, coefs)
+    arrived = lax.all_to_all(sent, "feat", split_axis=0, concat_axis=0, tiled=True)
+    grad_bases, grad_self = call(
+        functools.partial(weights_kernel, scale),
+        (shape((flat, model), F32), shape((quarter, model), F32)),
+        smem=(0,),
+        count=5 + feat_count,
+        us=12,
+    )(place, mix, grads, full, nodes, *rows)
+    grad_feats, coef_total = call(
+        functools.partial(finish_kernel, padded, scale),
+        (shape((quarter, entities), BF), shape((basis_count, relation_count), F32)),
+        count=2,
+        us=1,
+    )(arrived, grad_self)
+    return (
+        output,
+        grad_feats,
+        grad_bases.reshape(basis_count, quarter, model),
+        grad_self.T,
+        coef_total.T,
+    )
+
+
 def solution(mesh):
+    def body(*arrays):
+        dom_count = lax.axis_size("dom")
+        edge_count = arrays[5].shape[0]
+        feat_count = lax.axis_size("feat")
+        few = dom_count * edge_count <= 1 << 14 and dom_count % feat_count == 0
+        if not few:
+            return body_many(*arrays)
+        return body_few(*arrays)
+
     return jax.shard_map(
         body,
         mesh=mesh,

time: 184 us -> 153 us (0.83)
  blocking collectives: 105 us -> 9.27 us
  Pallas kernels: 31.2 us -> 66.2 us
  waiting for transfers between devices: 15.6 us -> 41 us
  starting transfers between devices: 6.87 us -> 27 us
  between operations: 14.1 us -> 0.75 us
    all_to_all x5 -> x0, blocking collectives: 89.1 us -> none  [the longest x1 29.3 us: body(): lax.all_to_all(bases_part.reshape(dom_count, tall // dom_count, model), '...]
    pallas_call x10 -> x11, Pallas kernels: 31.2 us -> 66.2 us  [the longest x1 15.3 us: body_few(): call(functools.partial(weights_kernel, scale), (shape((flat, model), F32)...]
    ppermute x0 -> x6, waiting for transfers between devices: none -> 18.6 us  [doubled(): pieces = pieces + [lax.ppermute(piece, 'feat', links) for piece in pieces]]
    all_to_all x2 -> x5, starting transfers between devices: 6.83 us -> 24.9 us  [the longest x1 7.28 us: body_few(): lax.all_to_all(packed, 'dom', split_axis=0, concat_axis=0, tiled=True)]
    all_gather x2 -> x1, blocking collectives: 16.1 us -> 9.27 us  [body_few(): gathered = lax.all_gather(mine, 'feat', axis=0, tiled=True)]
    all_to_all x2 -> x5, waiting for transfers between devices: 15.6 us -> 22.4 us  [the longest x1 16.7 us: body_few(): lax.all_to_all(packed, 'dom', split_axis=0, concat_axis=0, tiled=True)]
    unnamed x11 -> x28, local copies, waits for them, and re-layouts: 2.15 us -> 4.86 us
    ppermute x0 -> x6, starting transfers between devices: none -> 2.11 us  [doubled(): pieces = pieces + [lax.ppermute(piece, 'feat', links) for piece in pieces]]
  transfers between devices with their start and end apart: 3 -> 11, of which waited for: 2 -> 5; matrix products, arithmetic and copies ran while one was open for 3% -> 2% of each run, Pallas kernels for 6% -> 38%
where the time goes in v2:
time: 153 us
  Pallas kernels  66.2 us (43%)
  waiting for transfers between devices  41 us (27%)
  starting transfers between devices  27 us (18%)
  blocking collectives  9.27 us (6%)
  local copies, waits for them, and re-layouts  7.7 us (5%)
    ppermute x6, waiting for transfers between devices, doubled(): pieces = pieces + [lax.ppermute(piece, 'feat', links) for piece in pieces]  18.6 us
    all_to_all x1, waiting for transfers between devices, body_few(): lax.all_to_all(packed, 'dom', split_axis=0, concat_axis=0, tiled=True)  16.7 us
    pallas_call x1, Pallas kernels, body_few(): call(functools.partial(weights_kernel, scale), (shape((flat, model), F32)...  15.3 us
    all_gather x1, blocking collectives, body_few(): gathered = lax.all_gather(mine, 'feat', axis=0, tiled=True)  9.27 us
    pallas_call x1, Pallas kernels, body_few(): call(functools.partial(rows_of_edges_kernel, entities), (shape((part_coun...  9.24 us
    pallas_call x1, Pallas kernels, body_few(): call(scatter_kernel, shape((feat_count, quarter, entities + LANES), BF),...  7.84 us
    pallas_call x1, Pallas kernels, body_few(): call(functools.partial(rank_kernel, slot_cap, entities), (ints, shape((do...  7.77 us
    all_to_all x1, starting transfers between devices, body_few(): lax.all_to_all(packed, 'dom', split_axis=0, concat_axis=0, tiled=True)  7.28 us
  transfers between devices with their start and end apart: 11, of which 5 were waited for; matrix products, arithmetic and copies ran while one was open for 2% of the time, Pallas kernels for 38%

profile of v2, /device:TPU:0, one launch (start us, length us, event | category | flops | bytes accessed | tf_op | source)
XLA Modules:
  0.0 152.6 jit_solution(1066446728338008997)
XLA Ops:
  0.6 0.0 copy-start.7
  0.6 1.8 %shard_map.146 = bf16[8,320,128]{2,1,0:T(8,128)(2,1)} custom-call(s32[8]{0:T(128)} %bitcast.39, s32[8]{0:T(128)} %bitcast.42, bf16[64,512]{1,0:T(8,128)(2,1)} %feats.3, s32[8,128]{1,0:T(8,128)} %bitcast.29, s32[8,128]{1,0:T(8,128)} %bitcast.31, s32[8,128]{1,0:T(8,128)} %bitcast.33, s32[8,128]{1,0:T(8,128)} %bitcast.36), custom_call_target="tpu_custom_call" | custom-call | flops 1000000000 | bytes 1048576 | tf_op jit(solution)/shard_map/pallas_call | solution.py:858
  2.4 7.3 %all-to-all-start = ((bf16[8,320,128]{2,1,0:T(8,128)(2,1)}), bf16[8,320,128]{2,1,0:T(8,128)(2,1)S(1)}, u32[]{:S(2)}, u32[]{:S(2)}) async-start(bf16[8,320,128]{2,1,0:T(8,128)(2,1)} %shard_map.146), calls=%async_computation | async-start | bytes 1310720 | tf_op jit(solution)/shard_map/all_to_all | solution.py:861
  9.7 0.0 copy-done.7
  9.7 0.6 scatter.4.coef
  10.3 16.7 %all-to-all-done.shared = bf16[8,320,128]{2,1,0:T(8,128)(2,1)S(1)} async-done(((bf16[8,320,128]{2,1,0:T(8,128)(2,1)}), bf16[8,320,128]{2,1,0:T(8,128)(2,1)S(1)}, u32[]{:S(2)}, u32[]{:S(2)}) %all-to-all-start) | async-done | bytes 655392 | tf_op jit(solution)/shard_map/all_to_all | solution.py:861
  27.0 0.0 copy-start.2
  27.0 0.8 copy-done.2
  27.9 5.2 %shard_map.147 = (bf16[64,1536]{1,0:T(8,128)(2,1)}, bf16[64,4096]{1,0:T(8,128)(2,1)}, s32[8,8,128]{2,1,0:T(8,128)}, s32[32,1,256]{2,1,0:T(1,128)}, s32[8,8,128]{...) custom-call(bf16[8,320,128]{2,1,0:T(8,128)(2,1)} %copy-done.2, bf16[64,512]{1,0:T(8,128)(2,1)} %feats.3, ...), custom_call_target="tpu_custom_call" | custom-call | flops 4000000000 | bytes 1048576 | tf_op jit(solution)/shard_map/pallas_call | solution.py:863
  33.0 9.3 %all_gather.3.gathered = bf16[256,1536]{1,0:T(8,128)(2,1)} all-gather(bf16[64,1536]{1,0:T(8,128)(2,1)} %get-tuple-element.42), channel_id=1, replica_groups=mesh['dom'=8,'feat'=4] {'feat'}, dimensions={0}, use_global_device_ids=true | all-gather | bytes 983040 | tf_op jit(solution)/shard_map/all_gather | solution.py:878
  42.3 0.5 collective-permute-start
  42.8 0.0 copy-start.10
  42.8 3.7 %shard_map.148 = bf16[16,80,128]{2,1,0:T(8,128)(2,1)} custom-call(s32[8]{0:T(128)} %bitcast.40, s32[8]{0:T(128)} %bitcast.43, bf16[256,1536]{1,0:T(8,128)(2,1)} %all_gather.3.gathered, bf16[1920,256]{1,0:T(8,128)(2,1)} %bitcast.19, f32[32,256]{1,0:T(8,128)} %scatter.4.coef, s32[8,128]{1,0:T(8,128)} %bitcast.37, s32[8,128]{1,0:T(8,128)} %bitcast.34), custom_call_target="tpu_custom_call" | custom-call | flops 4000000000 | bytes 1048576 | tf_op jit(solution)/shard_map/pallas_call | solution.py:926
  46.5 4.8 %all-to-all-start.1 = ((bf16[16,80,128]{2,1,0:T(8,128)(2,1)}), bf16[16,80,128]{2,1,0:T(8,128)(2,1)S(1)}, u32[]{:S(2)}, u32[]{:S(2)}) async-start(bf16[16,80,128]{2,1,0:T(8,128)(2,1)} %shard_map.148), calls=%async_computation.1 | async-start | bytes 655360 | tf_op jit(solution)/shard_map/all_to_all | solution.py:933
  51.3 0.0 copy-done.10
  51.3 0.1 collective-permute-start.1
  51.4 5.3 %collective-permute-done.refs_1_ = bf16[64,4096]{1,0:T(8,128)(2,1)S(1)} collective-permute-done((bf16[64,4096]{1,0:T(8,128)(2,1)}, bf16[64,4096]{1,0:T(8,128)(2,1)S(1)}, u32[]{:S(2)}, u32[]{:S(2)}) %collective-permute-start) | collective-permute-done | bytes 524320 | tf_op jit(solution)/shard_map/ppermute | solution.py:885
  56.7 0.0 copy-start.11
  56.7 0.0 collective-permute-start.2
  56.7 0.7 pad_add_fusion.place
  57.4 4.4 %all-to-all-done.1.received = bf16[16,80,128]{2,1,0:T(8,128)(2,1)S(1)} async-done(((bf16[16,80,128]{2,1,0:T(8,128)(2,1)}), bf16[16,80,128]{2,1,0:T(8,128)(2,1)S(1)}, u32[]{:S(2)}, u32[]{:S(2)}) %all-to-all-start.1) | async-done | bytes 327712 | tf_op jit(solution)/shard_map/all_to_all | solution.py:933
  61.8 0.0 copy-start.3
  61.8 0.7 copy-done.3
  62.5 3.1 %shard_map.149 = (bf16[64,512]{1,0:T(8,128)(2,1)}, bf16[8,80,512]{2,1,0:T(8,128)(2,1)}, bf16[64,512]{1,0:T(8,128)(2,1)}) custom-call(bf16[16,80,128]{2,1,0:T(8,128)(2,1)} %copy-done.3, bf16[256,1536]{1,0:T(8,128)(2,1)} %all_gather.3.gathered, bf16[64,256]{1,0:T(8,128)(2,1)} %bitcast.27, bf16[64,512]{1,0:T(8,128)(2,1)} %cotangent.1), custom_call_target="tpu_custom_call" | custom-call | flops 4000000000 | bytes 1048576 | tf_op jit(solution)/shard_map/pallas_call | solution.py:935
  65.7 0.0 copy-done.11
  65.7 3.6 %all-to-all-start.2 = ((bf16[8,80,512]{2,1,0:T(8,128)(2,1)}), bf16[8,80,512]{2,1,0:T(8,128)(2,1)S(1)}, u32[]{:S(2)}, u32[]{:S(2)}) async-start(bf16[8,80,512]{2,1,0:T(8,128)(2,1)} %get-tuple-element.50), calls=%async_computation.2 | async-start | bytes 1310720 | tf_op jit(solution)/shard_map/all_to_all | solution.py:949
  69.3 0.0 collective-permute-done.1.refs_2_
  69.3 0.0 copy-start.12
  69.3 0.0 collective-permute-done.2.refs_3_
  69.3 0.0 copy-start.13
  69.3 0.8 copy-done.13
  70.2 0.1 copy-done.12
  70.3 0.0 copy-start
  70.3 0.0 copy-start.6
  70.3 9.2 %shard_map.154 = (bf16[8,256,256]{2,1,0:T(8,128)(2,1)}, bf16[256,4096]{1,0:T(8,128)(2,1)}) custom-call(s32[4]{0:T(128)} %pad_add_fusion.place, s32[32,1,256]{2,1,0:T(1,128)} %get-tuple-element.57.spans, bf16[64,4096]{1,0:T(8,128)(2,1)} %get-tuple-element.58.refs_0_, bf16[64,4096]{1,0:T(8,128)(2,1)} %copy-done.11, bf16[64,4096]{1,0:T(8,128)(2,1)} %copy-done.12, ...), custom_call_target="tpu_custom_call" | custom-call | flops 10000000000 | bytes 1048576 | tf_op jit(solution)/shard_map/pallas_call | solution.py:897
  79.5 1.5 %collective-permute-start.3 = (bf16[2,1024,256]{2,1,0:T(8,128)(2,1)}, bf16[2,1024,256]{2,1,0:T(8,128)(2,1)S(1)}, u32[]{:S(2)}, u32[]{:S(2)}) collective-permute-start(bf16[2,1024,256]{2,1,0:T(8,128)(2,1)} %bitcast.24), channel_id=1, source_target_pairs={{0,2},{1,3},{2,0},{3,1},{4,6},{5,7},{6,4},{7,5},{8,10},{9,11},{10,... | collective-permute-start | bytes 3145736 | tf_op jit(solution)/shard_map/ppermute | solution.py:885
  81.1 0.0 copy-done
  81.1 1.4 copy.19
  82.5 0.0 copy-done.6
  82.5 0.2 slice_reduce_fusion
  82.7 0.6 reshape_squeeze.3.owners
  83.3 0.0 copy-start.8
  83.3 7.8 %shard_map.150 = (s32[8,8,128]{2,1,0:T(8,128)}, s32[8,1,256]{2,1,0:T(1,128)}, f32[8,32,256]{2,1,0:T(8,128)}, f32[8,32,1024]{2,1,0:T(8,128)}) custom-call(s32[1]{0:T(128)} %bitcast.9.me, s32[8,8,128]{2,1,0:T(8,128)} %get-tuple-element.47.ids, s32[8,8,128]{2,1,0:T(8,128)} %get-tuple-element.48.rels, f32[32,256]{1,0:T(8,128)} %scatter.4.coef), custom_call_target="tpu_custom_call" | custom-call | flops 4000000000 | bytes 1048576 | tf_op jit(solution)/shard_map/pallas_call | solution.py:908
  91.1 0.0 copy-done.8
  91.1 0.0 collective-permute-start.4
  91.1 13.3 %collective-permute-done.3.refs_1_ = bf16[2,1024,256]{2,1,0:T(8,128)(2,1)S(1)} collective-permute-done((bf16[2,1024,256]{2,1,0:T(8,128)(2,1)}, bf16[2,1024,256]{2,1,0:T(8,128)(2,1)S(1)}, u32[]{:S(2)}, u32[]{:S(2)}) %collective-permute-start.3) | collective-permute-done | bytes 1048608 | tf_op jit(solution)/shard_map/ppermute | solution.py:885
  104.3 0.0 collective-permute-start.5
  104.4 0.0 all-to-all-done.2.shared
  104.4 0.0 copy-start.1
  104.4 0.9 copy-done.1
  105.3 4.4 %shard_map.152 = bf16[8,32,256]{2,1,0:T(8,128)(2,1)} custom-call(s32[8]{0:T(128)} %bitcast.41, s32[8]{0:T(128)} %bitcast.44, bf16[8,80,512]{2,1,0:T(8,128)(2,1)} %copy-done.1, bf16[256,1536]{1,0:T(8,128)(2,1)} %all_gather.3.gathered, bf16[1920,256]{1,0:T(8,128)(2,1)} %bitcast.20, s32[8,128]{1,0:T(8,128)} %bitcast.38, s32[8,128]{1,0:T(8,128)} %bitcast.35), custom_call_target="tpu_custom_call" | custom-call | flops 4000000000 | bytes 1048576 | tf_op jit(solution)/shard_map/pallas_call | solution.py:951
  109.7 0.0 copy-done.9
  109.7 5.7 %all-to-all-start.3 = ((bf16[8,32,256]{2,1,0:T(8,128)(2,1)}), bf16[8,32,256]{2,1,0:T(8,128)(2,1)S(1)}, u32[]{:S(2)}, u32[]{:S(2)}) async-start(bf16[8,32,256]{2,1,0:T(8,128)(2,1)} %shard_map.152), calls=%async_computation.3 | async-start | bytes 262144 | tf_op jit(solution)/shard_map/all_to_all | solution.py:959
  115.4 6.2 %shard_map.151 = (bf16[8,64,1024]{2,1,0:T(8,128)(2,1)}, bf16[8,64,256]{2,1,0:T(8,128)(2,1)}) custom-call(s32[64]{0:T(128)} %reshape_squeeze.3.owners, s32[8,8,128]{2,1,0:T(8,128)} %get-tuple-element.46.targets, s32[8,8,128]{2,1,0:T(8,128)} %get-tuple-element.49.ranks, bf16[8,80,512]{2,1,0:T(8,128)(2,1)} %copy-done.1), custom_call_target="tpu_custom_call" | custom-call | flops 6000000000 | bytes 1048576 | tf_op jit(solution)/shard_map/pallas_call | solution.py:960
  121.6 1.4 all-to-all-done.3.coefs
  123.0 0.7 copy-done.5
  123.7 7.8 %shard_map.153 = bf16[4,64,640]{2,1,0:T(8,128)(2,1)} custom-call(bf16[8,64,256]{2,1,0:T(8,128)(2,1)} %get-tuple-element.51.slot_grads, s32[8,1,256]{2,1,0:T(1,128)} %get-tuple-element.52.slot_rows, f32[8,32,256]{2,1,0:T(8,128)} %get-tuple-element.53.slot_mix, bf16[256,1920]{1,0:T(8,128)(2,1)} %bitcast.22, bf16[64,256]{1,0:T(8,128)(2,1)} %bitcast.28, ...), custom_call_target="tpu_custom_call" | custom-call | flops 5000000000 | bytes 1048576 | tf_op jit(solution)/shard_map/pallas_call | solution.py:971
  131.5 3.5 %all-to-all-start.4 = ((bf16[4,64,640]{2,1,0:T(8,128)(2,1)}), bf16[4,64,640]{2,1,0:T(8,128)(2,1)S(1)}, u32[]{:S(2)}, u32[]{:S(2)}) async-start(bf16[4,64,640]{2,1,0:T(8,128)(2,1)} %shard_map.153), calls=%async_computation.4 | async-start | bytes 655360 | tf_op jit(solution)/shard_map/all_to_all | solution.py:978
  135.0 0.0 collective-permute-done.4.refs_2_
  135.0 0.0 collective-permute-done.5.refs_3_
  135.0 15.3 %shard_map.155 = (f32[1920,256]{1,0:T(8,128)}, f32[64,256]{1,0:T(8,128)}) custom-call(s32[4]{0:T(128)} %pad_add_fusion.place, f32[8,32,1024]{2,1,0:T(8,128)} %get-tuple-element.55.mix, bf16[8,64,1024]{2,1,0:T(8,128)(2,1)} %get-tuple-element.56.grads, bf16[256,4096]{1,0:T(8,128)(2,1)} %get-tuple-element.59.full, bf16[8,80,512]{2,1,0:T(8,128)(2,1)} %copy-done.1, ...), custom_call_target="tpu_custom_call" | custom-call | flops 12000000000 | bytes 1048576 | tf_op jit(solution)/shard_map/pallas_call | solution.py:979
  150.3 0.0 all-to-all-done.4.arrived
  150.3 0.7 copy-done.4
  151.0 1.6 %shard_map.156 = (bf16[64,512]{1,0:T(8,128)(2,1)}, f32[30,237]{1,0:T(8,128)}) custom-call(bf16[4,64,640]{2,1,0:T(8,128)(2,1)} %copy-done.4, f32[64,256]{1,0:T(8,128)} %get-tuple-element.61.after), custom_call_target="tpu_custom_call" | custom-call | flops 1000000000 | bytes 1048576 | tf_op jit(solution)/shard_map/pallas_call | solution.py:986
  (3 shorter events, 0.0 us)
Async XLA Ops:
  0.6 9.1 %copy-start.7 = (f32[237,30]{0,1:T(8,128)S(1)}, f32[237,30]{0,1:T(8,128)}, u32[]{:S(2)}) copy-start(f32[237,30]{0,1:T(8,128)} %param.16) | copy-start | bytes 85324
  2.4 24.6 %all-to-all-start = ((bf16[8,320,128]{2,1,0:T(8,128)(2,1)}), bf16[8,320,128]{2,1,0:T(8,128)(2,1)S(1)}, u32[]{:S(2)}, u32[]{:S(2)}) async-start(bf16[8,320,128]{2,1,0:T(8,128)(2,1)} %shard_map.146), calls=%async_computation | async-start | bytes 1310720 | tf_op jit(solution)/shard_map/all_to_all | solution.py:861
  27.0 0.8 copy-start.2
  42.3 14.4 %collective-permute-start = (bf16[64,4096]{1,0:T(8,128)(2,1)}, bf16[64,4096]{1,0:T(8,128)(2,1)S(1)}, u32[]{:S(2)}, u32[]{:S(2)}) collective-permute-start(bf16[64,4096]{1,0:T(8,128)(2,1)} %get-tuple-element.58.refs_0_), channel_id=1, source_target_pairs={{0,2},{1,3},{2,0},{3,1},{4,6},{5,7},{6,4},{7,5},{8,10},{9,11},{10,... | collective-permute-start | bytes 1572872 | tf_op jit(solution)/shard_map/ppermute | solution.py:885
  42.8 8.5 %copy-start.10 = (bf16[64,4096]{1,0:T(8,128)(2,1)S(1)}, bf16[64,4096]{1,0:T(8,128)(2,1)}, u32[]{:S(2)}) copy-start(bf16[64,4096]{1,0:T(8,128)(2,1)} %get-tuple-element.58.refs_0_) | copy-start | bytes 1572868
  46.5 15.3 %all-to-all-start.1 = ((bf16[16,80,128]{2,1,0:T(8,128)(2,1)}), bf16[16,80,128]{2,1,0:T(8,128)(2,1)S(1)}, u32[]{:S(2)}, u32[]{:S(2)}) async-start(bf16[16,80,128]{2,1,0:T(8,128)(2,1)} %shard_map.148), calls=%async_computation.1 | async-start | bytes 655360 | tf_op jit(solution)/shard_map/all_to_all | solution.py:933
  51.3 18.0 %collective-permute-start.1 = (bf16[64,4096]{1,0:T(8,128)(2,1)S(1)}, bf16[64,4096]{1,0:T(8,128)(2,1)S(1)}, u32[]{:S(2)}, u32[]{:S(2)}) collective-permute-start(bf16[64,4096]{1,0:T(8,128)(2,1)S(1)} %copy-done.10), channel_id=1, source_target_pairs={{0,1},{1,0},{2,3},{3,2},{4,5},{5,4},{6,7},{7,6},{8,9},{9,8},{10,11... | collective-permute-start | bytes 1572872 | tf_op jit(solution)/shard_map/ppermute | solution.py:885
  56.7 9.0 %copy-start.11 = (bf16[64,4096]{1,0:T(8,128)(2,1)}, bf16[64,4096]{1,0:T(8,128)(2,1)S(1)}, u32[]{:S(2)}) copy-start(bf16[64,4096]{1,0:T(8,128)(2,1)S(1)} %collective-permute-done.refs_1_) | copy-start | bytes 1572868
  56.7 12.7 %collective-permute-start.2 = (bf16[64,4096]{1,0:T(8,128)(2,1)S(1)}, bf16[64,4096]{1,0:T(8,128)(2,1)S(1)}, u32[]{:S(2)}, u32[]{:S(2)}) collective-permute-start(bf16[64,4096]{1,0:T(8,128)(2,1)S(1)} %collective-permute-done.refs_1_), channel_id=1, source_target_pairs={{0,1},{1,0},{2,3},{3,2},{4,5},{5,4},{6,7},{7,6},{8,9},{9,8},{10,11... | collective-permute-start | bytes 1572872 | tf_op jit(solution)/shard_map/ppermute | solution.py:885
  61.8 0.7 copy-start.3
  65.7 38.7 %all-to-all-start.2 = ((bf16[8,80,512]{2,1,0:T(8,128)(2,1)}), bf16[8,80,512]{2,1,0:T(8,128)(2,1)S(1)}, u32[]{:S(2)}, u32[]{:S(2)}) async-start(bf16[8,80,512]{2,1,0:T(8,128)(2,1)} %get-tuple-element.50), calls=%async_computation.2 | async-start | bytes 1310720 | tf_op jit(solution)/shard_map/all_to_all | solution.py:949
  69.3 1.0 copy-start.12
  69.3 0.9 copy-start.13
  70.3 10.8 %copy-start = (bf16[30,64,256]{2,1,0:T(8,128)(2,1)S(1)}, bf16[30,64,256]{2,1,0:T(8,128)(2,1)}, u32[]{:S(2)}) copy-start(bf16[30,64,256]{2,1,0:T(8,128)(2,1)} %param.15) | copy-start | bytes 2949124
  70.3 12.2 %copy-start.6 = (s32[8,8,128]{2,1,0:T(8,128)S(1)}, s32[8,8,128]{2,1,0:T(8,128)}, u32[]{:S(2)}) copy-start(s32[8,8,128]{2,1,0:T(8,128)} %get-tuple-element.45) | copy-start | bytes 98308
  79.5 24.8 %collective-permute-start.3 = (bf16[2,1024,256]{2,1,0:T(8,128)(2,1)}, bf16[2,1024,256]{2,1,0:T(8,128)(2,1)S(1)}, u32[]{:S(2)}, u32[]{:S(2)}) collective-permute-start(bf16[2,1024,256]{2,1,0:T(8,128)(2,1)} %bitcast.24), channel_id=1, source_target_pairs={{0,2},{1,3},{2,0},{3,1},{4,6},{5,7},{6,4},{7,5},{8,10},{9,11},{10,... | collective-permute-start | bytes 3145736 | tf_op jit(solution)/shard_map/ppermute | solution.py:885
  83.3 7.8 %copy-start.8 = (bf16[8,256,256]{2,1,0:T(8,128)(2,1)S(1)}, bf16[8,256,256]{2,1,0:T(8,128)(2,1)}, u32[]{:S(2)}) copy-start(bf16[8,256,256]{2,1,0:T(8,128)(2,1)} %get-tuple-element.60) | copy-start | bytes 3145732
  91.1 43.9 %collective-permute-start.4 = (bf16[2,1024,256]{2,1,0:T(8,128)(2,1)S(1)}, bf16[2,1024,256]{2,1,0:T(8,128)(2,1)}, u32[]{:S(2)}, u32[]{:S(2)}) collective-permute-start(bf16[2,1024,256]{2,1,0:T(8,128)(2,1)S(1)} %bitcast.26), channel_id=1, source_target_pairs={{0,1},{1,0},{2,3},{3,2},{4,5},{5,4},{6,7},{7,6},{8,9},{9,8},{10,11... | collective-permute-start | bytes 3145736 | tf_op jit(solution)/shard_map/ppermute | solution.py:885
  104.3 5.3 %copy-start.9 = (bf16[2,1024,256]{2,1,0:T(8,128)(2,1)}, bf16[2,1024,256]{2,1,0:T(8,128)(2,1)S(1)}, u32[]{:S(2)}) copy-start(bf16[2,1024,256]{2,1,0:T(8,128)(2,1)S(1)} %collective-permute-done.3.refs_1_) | copy-start | bytes 3145732
  104.3 30.6 %collective-permute-start.5 = (bf16[2,1024,256]{2,1,0:T(8,128)(2,1)S(1)}, bf16[2,1024,256]{2,1,0:T(8,128)(2,1)}, u32[]{:S(2)}, u32[]{:S(2)}) collective-permute-start(bf16[2,1024,256]{2,1,0:T(8,128)(2,1)S(1)} %collective-permute-done.3.refs_1_), channel_id=1, source_target_pairs={{0,1},{1,0},{2,3},{3,2},{4,5},{5,4},{6,7},{7,6},{8,9},{9,8},{10,11... | collective-permute-start | bytes 3145736 | tf_op jit(solution)/shard_map/ppermute | solution.py:885
  104.4 0.9 copy-start.1
  109.7 13.3 %all-to-all-start.3 = ((bf16[8,32,256]{2,1,0:T(8,128)(2,1)}), bf16[8,32,256]{2,1,0:T(8,128)(2,1)S(1)}, u32[]{:S(2)}, u32[]{:S(2)}) async-start(bf16[8,32,256]{2,1,0:T(8,128)(2,1)} %shard_map.152), calls=%async_computation.3 | async-start | bytes 262144 | tf_op jit(solution)/shard_map/all_to_all | solution.py:959
  123.0 0.7 copy-start.5
  131.5 18.7 %all-to-all-start.4 = ((bf16[4,64,640]{2,1,0:T(8,128)(2,1)}), bf16[4,64,640]{2,1,0:T(8,128)(2,1)S(1)}, u32[]{:S(2)}, u32[]{:S(2)}) async-start(bf16[4,64,640]{2,1,0:T(8,128)(2,1)} %shard_map.153), calls=%async_computation.4 | async-start | bytes 655360 | tf_op jit(solution)/shard_map/all_to_all | solution.py:978
  150.3 0.7 copy-start.4

commit v3 on v2

--- a/solution.py
+++ b/solution.py
@@ -28,22 +28,42 @@
     return lax.dot_general(left, right, dims, preferred_element_type=F32)
 
 
-def call(kernel, out_shape, smem=(), scratch=(), count=0, us=4):
+def call(
+    kernel, out_shape, smem=(), scratch=(), count=0, us=4, far=(), far_out=(), raw=()
+):
     specs = [
-        pl.BlockSpec(memory_space=pltpu.SMEM if k in smem else pltpu.VMEM) for k in range(count)
+        pl.BlockSpec(
+            memory_space=pltpu.SMEM if k in smem else pltpu.HBM if k in raw else pltpu.VMEM
+        )
+        for k in range(count)
     ]
     single = not isinstance(out_shape, (tuple, list))
+    shapes = (out_shape,) if single else tuple(out_shape)
+    shapes = tuple(
+        pltpu.HBM(o.shape, o.dtype) if k in far_out else o for k, o in enumerate(shapes)
+    )
     outs = pl.BlockSpec(memory_space=pltpu.VMEM)
-    return pl.pallas_call(
+    run = pl.pallas_call(
         kernel,
-        out_shape=out_shape,
+        out_shape=shapes[0] if single else shapes,
         in_specs=specs,
-        out_specs=outs if single else tuple(outs for _ in out_shape),
+        out_specs=outs if single else tuple(outs for _ in shapes),
         scratch_shapes=scratch,
+        compiler_params=pltpu.CompilerParams(vmem_limit_bytes=24 << 20),
         cost_estimate=pl.CostEstimate(
             flops=us * 1_000_000_000, bytes_accessed=1 << 20, transcendentals=0
         ),
     )
+
+    def apply(*arrays):
+        return run(
+            *(
+                pltpu.with_memory_space_constraint(a, pltpu.HBM) if k in far or k in raw else a
+                for k, a in enumerate(arrays)
+            )
+        )
+
+    return apply
 
 
 def block_slots(owners, block_count, block_cap):
@@ -594,7 +614,7 @@
     flat[quarter:, :] = jnp.ones((16, slots * rows), BF)
     own = gathered[:, gathered.shape[1] - entities :]
     own_part = dot(weight[...], own)
-    sums = dot(flat[...], hots[...], NT)
+    sums = dot(hots[...], flat[...], NT).T
     count = sums[quarter : quarter + 1]
     inverse = 1.0 / jnp.maximum(count, 1.0)
     preact = own_part + inverse * sums[:quarter]
@@ -681,36 +701,42 @@
     lax.fori_loop(0, dom_count, step, 0)
 
 
-def coef_kernel(owners, valid, shared, gathered, bases, rel, dst, out, scaled, grads):
+def products_kernel(gathered, bases, bases_t, out):
+    edge_count = out.shape[1]
+    bases_t[...] = bases[...].T
+    step = 320
+    for start in range(0, out.shape[0], step):
+        stop = min(start + step, out.shape[0])
+        out[start:stop, :] = dot(bases[start:stop, :], gathered[:, :edge_count]).astype(BF)
+
+
+def coef_kernel(
+    owners, valid, shared, products_far, rel, dst, out, scaled, grads, products, sems
+):
+    fetched = fetch(((products_far, products),), sems)
     blocks = rel.shape[0]
-    copies, padded, relations = out.shape
+    copies, _, relations = out.shape
     entities = shared.shape[2]
     quarter = shared.shape[1] - 16
-    basis_count = bases.shape[0] // quarter
-    group = 5
+    basis_count = products.shape[0] // quarter
     scaled[...] = jnp.zeros_like(scaled)
-    total = jnp.zeros((padded, relations), F32)
     for j in range(blocks):
         live = iota((1, LANES), 1) < valid[j]
         target = jnp.where(live, dst[j : j + 1, :], entities)
         chosen = hot(iota((entities, LANES), 0) == target)
         grads[:, j * LANES : (j + 1) * LANES] = dot(scaled_grad(shared, owners[j], quarter), chosen)
+    fetched[0].wait()
     for t in range(blocks // 2):
         lanes = slice(2 * t * LANES, 2 * (t + 1) * LANES)
-        both = jnp.concatenate([rel[2 * t : 2 * t + 1, :], rel[2 * t + 1 : 2 * t + 2, :]], axis=1)
-        x = gathered[:, lanes]
         grad = grads[:, lanes]
-        for c in range(0, basis_count, group):
-            stop = min(c + group, basis_count)
-            products = dot(bases[c * quarter : stop * quarter, :], x)
-            for b in range(c, stop):
-                part = products[(b - c) * quarter : (b - c + 1) * quarter]
-                scaled[b : b + 1, :] = jnp.sum(part * grad, axis=0, keepdims=True)
-        high = scaled[...].astype(BF)
-        low = (scaled[...] - high.astype(F32)).astype(BF)
-        chosen = rel_hot(both, relations)
-        total = total + dot(high, chosen, NT) + dot(low, chosen, NT)
-    total = total.astype(BF)
+        for b in range(basis_count):
+            part = products[b * quarter : (b + 1) * quarter, lanes].astype(F32)
+            scaled[b : b + 1, lanes] = jnp.sum(part * grad, axis=0, keepdims=True)
+    high = scaled[...].astype(BF)
+    low = (scaled[...] - high.astype(F32)).astype(BF)
+    kinds = jnp.concatenate([rel[j : j + 1, :] for j in range(blocks)], axis=1)
+    chosen = rel_hot(kinds, relations)
+    total = (dot(chosen, high, NT) + dot(chosen, low, NT)).T.astype(BF)
     for k in range(copies):
         out[k] = total
 
@@ -747,7 +773,10 @@
     return jnp.concatenate(pieces, axis=0)
 
 
-def scatter_kernel(slot_grads, slot_rows, slot_mix, bases_t, weight, grad_pre, coefs, out, total):
+def scatter_kernel(
+    slot_grads, slot_rows, slot_mix, bases_far, weight, grad_pre, coefs, out, total, bases_t, sems
+):
+    copies = fetch(((bases_far, bases_t),), sems)
     dom_count, quarter, slot_cap = slot_grads.shape
     padded = slot_mix.shape[1]
     basis_count = bases_t.shape[1] // quarter
@@ -756,6 +785,8 @@
     total[...] = lax.dot_general(
         weight[...], grad_pre[...], (((0,), (0,)), ((), ())), preferred_element_type=F32
     )
+
+    copies[0].wait()
 
     def step(g, carry):
         combined = mix_rows(slot_mix[g][:basis_count], slot_grads[g], quarter)
@@ -776,35 +807,48 @@
         out[f, padded : 2 * padded, entities:] = coef[:, LANES:]
 
 
-def weights_kernel(scale, place, mix, grads, full, shared, *refs):
-    rows, out, own_out = refs[:-2], refs[-2], refs[-1]
+def fetch(pairs, sems):
+    copies = [
+        pltpu.make_async_copy(source, target, sems.at[k]) for k, (source, target) in enumerate(pairs)
+    ]
+    for copy in copies:
+        copy.start()
+    return copies
+
+
+def weights_kernel(scale, place, mix_far, grads_far, full_far, shared, *refs):
+    rows, (out, own_out, mix, grads, full, sems) = refs[:-6], refs[-6:]
+    copies = fetch(((mix_far, mix), (grads_far, grads), (full_far, full)), sems)
     dom_count, quarter, _ = grads.shape
     entities = shared.shape[2]
     basis_count = out.shape[0] // quarter
     group = 5
+    copies[0].wait()
+    copies[1].wait()
+    for part, piece in enumerate(rows):
+        count = piece.shape[0]
+        for k in range(count):
+            g = place[part] * count + k
+            grad = grads[g]
+            for c in range(0, basis_count, group):
+                stop = min(c + group, basis_count)
+                combined = mix_rows(mix[g, c:stop, :], grad, quarter)
+                total = dot(combined, piece[k])
+                lanes = slice(c * quarter, stop * quarter)
+                if part > 0 or k > 0:
+                    total = total + out[lanes, :]
+                if part == len(rows) - 1 and k == count - 1:
+                    total = total * scale
+                out[lanes, :] = total
+    copies[2].wait()
     own = jnp.zeros(own_out.shape, F32)
     for q in range(dom_count):
         lanes = slice(q * entities, (q + 1) * entities)
         own = own + dot(shared[q, :quarter, :], full[:, lanes], NT)
     own_out[...] = own * scale
-    out[...] = jnp.zeros_like(out)
-    for part, piece in enumerate(rows):
-        count = piece.shape[0]
-
-        def step(k, carry):
-            g = place[part] * count + k
-            grad = grads[g]
-            for c in range(0, basis_count, group):
-                stop = min(c + group, basis_count)
-                combined = mix_rows(mix[g, c:stop, :], grad, quarter)
-                out[c * quarter : stop * quarter, :] += dot(combined, piece[k])
-            return carry
-
-        lax.fori_loop(0, count, step, 0)
-    out[...] = out[...] * scale
-
-
-def finish_kernel(padded, scale, arrived, after, grad_feats, coef_out):
+
+
+def finish_kernel(padded, scale, arrived, grad_feats, coef_out):
     peers, _, _ = arrived.shape
     entities = grad_feats.shape[1]
     sums = arrived[0].astype(F32)
@@ -849,16 +893,25 @@
     dst = edge_dst.reshape(blocks, LANES)
     rel = edge_rel.reshape(blocks, LANES)
     bases_flat = bases.reshape(flat, model)
-    bases_t = bases_flat.T
     weight_t = self_weight.T
     coef_t = jnp.zeros((padded, relations), F32).at[:basis_count, :relation_count].set(coef.T)
     feat_place = lax.axis_index("feat").astype(I32)
 
     tall = (entities // LANES) * quarter + 8 * blocks
-    packed = call(pack_kernel, shape((dom_count, tall, LANES), BF), smem=(0, 1), count=7, us=1)(
+    packed = call(
+        pack_kernel,
+        shape((1, tall, LANES), BF),
+        smem=(0, 1),
+        count=7,
+        us=1,
+        far=(0, 1, 2, 3, 4, 5, 6),
+    )(
         owners, valid, feats, part, row, dst, rel
     )
-    shared = lax.all_to_all(packed, "dom", split_axis=0, concat_axis=0, tiled=True)
+    near = [[2 * k, 2 * k + 1] for k in range(dom_count // 2)]
+    far = [[2 * k + side for k in range(dom_count // 2)] for side in range(2)]
+    shared = lax.all_gather(packed, "dom", axis=0, tiled=True, axis_index_groups=near)
+    shared = lax.all_gather(shared, "dom", axis=0, tiled=True, axis_index_groups=far)
     ints = shape((dom_count, blocks, LANES), I32)
     mine, wide, ids, spans, targets, rels, all_owners = call(
         source_kernel,
@@ -874,6 +927,7 @@
         scratch=[pltpu.VMEM((quarter, edge_count), F32), pltpu.VMEM((entities, edge_count), BF)],
         count=4,
         us=4,
+        far_out=(3, 4, 6),
     )(shared, feats, part, row)
     gathered = lax.all_gather(mine, "feat", axis=0, tiled=True)
     owner_list = all_owners[:, :, 0].reshape(dom_count * blocks)
@@ -903,6 +957,8 @@
         smem=(0,),
         count=2 + feat_count,
         us=10,
+        far=(0,),
+        far_out=(1,),
     )(place, spans, *doubled(wide))
     rows = doubled(rows.reshape(part_count, edge_count, model))
     ranks, slot_rows, slot_mix, mix = call(
@@ -921,6 +977,8 @@
         ],
         count=4,
         us=4,
+        far=(0,),
+        far_out=(0, 1, 2, 3),
     )(lax.axis_index("dom").astype(I32).reshape(1), ids, rels, coef_t)
 
     messages = call(
@@ -929,6 +987,7 @@
         smem=(0, 1),
         count=7,
         us=4,
+        far=(0, 1),
     )(owners, valid, gathered, bases_flat, coef_t, rel, dst)
     received = lax.all_to_all(messages, "dom", split_axis=0, concat_axis=0, tiled=True)
     slots = dom_count * block_cap
@@ -945,17 +1004,27 @@
         ],
         count=4,
         us=4,
+        far_out=(2,),
     )(received, gathered, weight_t, cotangent)
     nodes = lax.all_to_all(share, "dom", split_axis=0, concat_axis=0, tiled=True)
 
+    bases_t, products = call(
+        products_kernel,
+        (shape((model, flat), BF), shape((flat, edge_count), BF)),
+        count=2,
+        us=4,
+        far_out=(0, 1),
+    )(gathered, bases_flat)
     coef_part = call(
         coef_kernel,
         shape((dom_count, padded, relations), BF),
         smem=(0, 1),
-        scratch=[pltpu.VMEM((padded, 2 * LANES), F32), pltpu.VMEM((quarter, edge_count), F32)],
-        count=7,
+        scratch=[pltpu.VMEM((padded, edge_count), F32), pltpu.VMEM((quarter, edge_count), F32), pltpu.VMEM((flat, edge_count), BF), pltpu.SemaphoreType.DMA((1,))],
+        raw=(3,),
+        count=6,
         us=4,
-    )(owners, valid, nodes, gathered, bases_flat, rel, dst)
+        far=(0, 1),
+    )(owners, valid, nodes, products, rel, dst)
     coefs = lax.all_to_all(coef_part, "dom", split_axis=0, concat_axis=0, tiled=True)
     grads, slot_grads = call(
         grads_kernel,
@@ -967,11 +1036,18 @@
         ],
         count=4,
         us=6,
+        far=(0, 1, 2),
+        far_out=(0,),
     )(owner_list, targets, ranks, nodes)
     sent = call(
         scatter_kernel,
         shape((feat_count, quarter, entities + LANES), BF),
-        scratch=[pltpu.VMEM((model, entities), F32)],
+        scratch=[
+            pltpu.VMEM((model, entities), F32),
+            pltpu.VMEM((model, flat), BF),
+            pltpu.SemaphoreType.DMA((1,)),
+        ],
+        raw=(3,),
         count=7,
         us=5,
     )(slot_grads, slot_rows, slot_mix, bases_t, weight_t, grad_pre, coefs)
@@ -982,13 +1058,21 @@
         smem=(0,),
         count=5 + feat_count,
         us=12,
+        far=(0,),
+        raw=(1, 2, 3),
+        scratch=[
+            pltpu.VMEM((dom_count, padded, edge_count), F32),
+            pltpu.VMEM((dom_count, quarter, edge_count), BF),
+            pltpu.VMEM((model, dom_count * entities), BF),
+            pltpu.SemaphoreType.DMA((3,)),
+        ],
     )(place, mix, grads, full, nodes, *rows)
     grad_feats, coef_total = call(
         functools.partial(finish_kernel, padded, scale),
         (shape((quarter, entities), BF), shape((basis_count, relation_count), F32)),
-        count=2,
+        count=1,
         us=1,
-    )(arrived, grad_self)
+    )(arrived)
     return (
         output,
         grad_feats,

time: 153 us -> 137 us (0.90)
  blocking collectives: 9.27 us -> 41.6 us
  waiting for transfers between devices: 41 us -> 10.8 us
  starting transfers between devices: 27 us -> 17 us
  Pallas kernels: 66.2 us -> 60.9 us
  local copies, waits for them, and re-layouts: 7.7 us -> 3.8 us
    all_gather x0 -> x2, blocking collectives: none -> 23.8 us  [the longest x1 17.7 us: body_few(): lax.all_gather(shared, 'dom', axis=0, tiled=True, axis_index_groups=far)]
    all_to_all x2 -> x0, waiting for transfers between devices: 16.7 us -> none  [the longest x1 16.7 us: body_few(): lax.all_to_all(packed, 'dom', split_axis=0, concat_axis=0, tiled=True)]
    ppermute x6, waiting for transfers between devices: 18.6 us -> 6.92 us  [doubled(): pieces = pieces + [lax.ppermute(piece, 'feat', links) for piece in pieces]]
    all_to_all x2 -> x0, starting transfers between devices: 10.7 us -> none  [the longest x1 7.28 us: body_few(): lax.all_to_all(packed, 'dom', split_axis=0, concat_axis=0, tiled=True)]
    all_to_all x0 -> x1, blocking collectives: none -> 9.2 us  [body_few(): lax.all_to_all(sent, 'feat', split_axis=0, concat_axis=0, tiled=True)]
    pallas_call x11 -> x12, Pallas kernels: 66.2 us -> 60.9 us  [apply(): run(*(pltpu.with_memory_space_constraint(a, pltpu.HBM) if k in far or k i...]
    unnamed x28 -> x44, local copies, waits for them, and re-layouts: 4.86 us -> 2.93 us
  transfers between devices with their start and end apart: 11 -> 9, of which waited for: 5 -> 4; matrix products, arithmetic and copies ran while one was open for 2% -> 1% of each run, Pallas kernels for 38% -> 31%
where the time goes in v3:
time: 137 us; the launch traced here: 136 us
  Pallas kernels  60.9 us (44%)
  blocking collectives  41.6 us (30%)
  starting transfers between devices  17 us (12%)
  waiting for transfers between devices  10.8 us (8%)
  local copies, waits for them, and re-layouts  3.8 us (3%)
    pallas_call x12, Pallas kernels, apply(): run(*(pltpu.with_memory_space_constraint(a, pltpu.HBM) if k in far or k i...  60.9 us
    all_gather x1, blocking collectives, body_few(): lax.all_gather(shared, 'dom', axis=0, tiled=True, axis_index_groups=far)  17.7 us
    all_to_all x1, blocking collectives, body_few(): lax.all_to_all(sent, 'feat', split_axis=0, concat_axis=0, tiled=True)  9.2 us
    all_gather x1, blocking collectives, body_few(): gathered = lax.all_gather(mine, 'feat', axis=0, tiled=True)  8.62 us
    ppermute x6, waiting for transfers between devices, doubled(): pieces = pieces + [lax.ppermute(piece, 'feat', links) for piece in pieces]  6.92 us
    all_gather x1, blocking collectives, body_few(): lax.all_gather(packed, 'dom', axis=0, tiled=True, axis_index_groups=near)  6.06 us
    all_to_all x1, starting transfers between devices, body_few(): lax.all_to_all(coef_part, 'dom', split_axis=0, concat_axis=0, tiled=True)  6 us
    all_to_all x1, starting transfers between devices, body_few(): lax.all_to_all(messages, 'dom', split_axis=0, concat_axis=0, tiled=True)  5.25 us
  transfers between devices with their start and end apart: 9, of which 4 were waited for; matrix products, arithmetic and copies ran while one was open for 1% of the time, Pallas kernels for 31%

profile of v3, /device:TPU:0, one launch (start us, length us, event | category | flops | bytes accessed | tf_op | source)
XLA Modules:
  0.0 135.7 jit_solution(9800359520984071087)
XLA Ops:
  0.6 0.0 copy-start.5
  0.6 0.0 copy-start.8
  0.7 0.0 copy-start.9
  0.7 0.9 shard_map.146
  1.6 6.1 %all_gather.9 = bf16[2,320,128]{2,1,0:T(8,128)(2,1)S(1)} all-gather(bf16[1,320,128]{2,1,0:T(8,128)(2,1)S(1)} %shard_map.146), channel_id=1, replica_groups={{0,4},{8,12},{16,20},{24,28},{1,5},{9,13},{17,21},{25,29},{2,6},{10,14}..., dimensions={0}, use_global_device_ids=true | all-gather | bytes 245760 | tf_op jit(solution)/shard_map/all_gather | solution.py:913
  7.7 17.7 %all_gather.10.shared = bf16[8,320,128]{2,1,0:T(8,128)(2,1)S(1)} all-gather(bf16[2,320,128]{2,1,0:T(8,128)(2,1)S(1)} %all_gather.9), channel_id=1, replica_groups={{0,8,16,24},{4,12,20,28},{1,9,17,25},{5,13,21,29},{2,10,18,26},{6,14,22..., dimensions={0}, use_global_device_ids=true | all-gather | bytes 819200 | tf_op jit(solution)/shard_map/all_gather | solution.py:914
  25.4 0.0 copy-done.5
  25.4 0.0 copy-done.8
  25.4 0.0 copy-done.9
  25.4 0.0 copy-start.21
  25.4 0.0 copy-start
  25.4 0.0 copy-start.10
  25.4 0.0 copy-start.11
  25.4 3.9 %shard_map.147 = (bf16[64,1536]{1,0:T(8,128)(2,1)S(1)}, bf16[64,4096]{1,0:T(8,128)(2,1)S(1)}, s32[8,8,128]{2,1,0:T(8,128)S(1)}, s32[32,1,256]{2,1,0:T(1,128)}, s...) custom-call(bf16[8,320,128]{2,1,0:T(8,128)(2,1)S(1)} %all_gather.10.shared, ...), custom_call_target="tpu_custom_call" | custom-call | flops 4000000000 | bytes 1048576 | tf_op jit(solution)/shard_map/pallas_call | solution.py:59
  29.4 8.6 %all_gather.11.gathered = bf16[256,1536]{1,0:T(8,128)(2,1)S(1)} all-gather(bf16[64,1536]{1,0:T(8,128)(2,1)S(1)} %get-tuple-element.44), channel_id=1, replica_groups=mesh['dom'=8,'feat'=4] {'feat'}, dimensions={0}, use_global_device_ids=true | all-gather | bytes 983040 | tf_op jit(solution)/shard_map/all_gather | solution.py:932
  38.0 0.5 collective-permute-start
  38.5 0.0 copy-done.21
  38.5 0.0 copy-done.14
  38.5 0.0 copy-done.16
  38.5 0.0 copy-done
  38.5 0.0 copy-done.10
  38.5 0.0 copy-done.11
  38.6 0.0 copy-start.20
  38.6 0.0 copy-start.6
  38.6 0.0 copy-start.7
  38.6 3.0 %shard_map.148 = bf16[16,80,128]{2,1,0:T(8,128)(2,1)} custom-call(s32[8]{0:T(128)} %bitcast.37, s32[8]{0:T(128)} %bitcast.40, bf16[256,1536]{1,0:T(8,128)(2,1)S(1)} %all_gather.11.gathered, bf16[1920,256]{1,0:T(8,128)(2,1)S(1)} %bitcast.21, f32[32,256]{1,0:T(8,128)S(1)} %scatter.4.coef, s32[8,128]{1,0:T(8,128)S(1)} %bitcast.33, s32[8,128]{1,0:T(8,128)S(1)} %bitcast.30), custom_call_target="tpu_custom_call" | custom-call | flops 4000000000 | bytes 1048576 | tf_op jit(solution)/shard_map/pallas_call | solution.py:59
  41.6 5.2 %all-to-all-start = ((bf16[16,80,128]{2,1,0:T(8,128)(2,1)}), bf16[16,80,128]{2,1,0:T(8,128)(2,1)S(1)}, u32[]{:S(2)}, u32[]{:S(2)}) async-start(bf16[16,80,128]{2,1,0:T(8,128)(2,1)} %shard_map.148), calls=%async_computation | async-start | bytes 655360 | tf_op jit(solution)/shard_map/all_to_all | solution.py:992
  46.8 0.1 collective-permute-start.1
  46.9 5.2 %collective-permute-done.refs_1_ = bf16[64,4096]{1,0:T(8,128)(2,1)S(1)} collective-permute-done((bf16[64,4096]{1,0:T(8,128)(2,1)S(1)}, bf16[64,4096]{1,0:T(8,128)(2,1)S(1)}, u32[]{:S(2)}, u32[]{:S(2)}) %collective-permute-start) | collective-permute-done | bytes 524320 | tf_op jit(solution)/shard_map/ppermute | solution.py:939
  52.2 0.0 collective-permute-start.2
  52.2 0.2 slice_reduce_fusion
  52.4 0.7 reshape_squeeze.3.owners
  53.1 0.6 pad_add_fusion.place
  53.7 3.7 %all-to-all-done.received = bf16[16,80,128]{2,1,0:T(8,128)(2,1)S(1)} async-done(((bf16[16,80,128]{2,1,0:T(8,128)(2,1)}), bf16[16,80,128]{2,1,0:T(8,128)(2,1)S(1)}, u32[]{:S(2)}, u32[]{:S(2)}) %all-to-all-start) | async-done | bytes 327712 | tf_op jit(solution)/shard_map/all_to_all | solution.py:992
  57.4 0.0 copy-done.7
  57.4 1.8 %shard_map.149 = (bf16[64,512]{1,0:T(8,128)(2,1)}, bf16[8,80,512]{2,1,0:T(8,128)(2,1)}, bf16[64,512]{1,0:T(8,128)(2,1)}) custom-call(bf16[16,80,128]{2,1,0:T(8,128)(2,1)S(1)} %all-to-all-done.received, bf16[256,1536]{1,0:T(8,128)(2,1)S(1)} %all_gather.11.gathered, bf16[64,256]{1,0:T(8,128)(2,1)S(1)} %bitcast.23, bf16[64,512]{1,0:T(8,128)(2,1)S(1)} %copy-done.6), custom_call_target="tpu_custom_call" | custom-call | flops 4000000000 | bytes 1048576 | tf_op jit(solution)/shard_map/pallas_call | solution.py:59
  59.2 0.0 copy-done.3
  59.2 3.6 %all-to-all-start.1 = ((bf16[8,80,512]{2,1,0:T(8,128)(2,1)}), bf16[8,80,512]{2,1,0:T(8,128)(2,1)S(1)}, u32[]{:S(2)}, u32[]{:S(2)}) async-start(bf16[8,80,512]{2,1,0:T(8,128)(2,1)} %get-tuple-element.52), calls=%async_computation.1 | async-start | bytes 1310720 | tf_op jit(solution)/shard_map/all_to_all | solution.py:1009
  62.8 0.0 collective-permute-done.1.refs_2_
  62.8 0.0 collective-permute-done.2.refs_3_
  62.9 0.0 copy-start.2
  62.9 1.0 copy-done.2
  63.9 1.0 copy-done.4
  64.9 0.8 copy-done.18
  65.7 8.4 %shard_map.156 = (bf16[8,256,256]{2,1,0:T(8,128)(2,1)S(1)}, bf16[256,4096]{1,0:T(8,128)(2,1)}) custom-call(s32[4]{0:T(128)} %pad_add_fusion.place, s32[32,1,256]{2,1,0:T(1,128)S(1)} %copy-done.18, bf16[64,4096]{1,0:T(8,128)(2,1)S(1)} %copy-done.2, bf16[64,4096]{1,0:T(8,128)(2,1)S(1)} %copy-done.4, bf16[64,4096]{1,0:T(8,128)(2,1)} %collective-permute-done.1.refs_2_, ...), custom_call_target="tpu_custom_call" | custom-call | flops 10000000000 | bytes 1048576 | tf_op jit(solution)/shard_map/pallas_call | solution.py:59
  74.1 1.5 %collective-permute-start.3 = (bf16[2,1024,256]{2,1,0:T(8,128)(2,1)S(1)}, bf16[2,1024,256]{2,1,0:T(8,128)(2,1)}, u32[]{:S(2)}, u32[]{:S(2)}) collective-permute-start(bf16[2,1024,256]{2,1,0:T(8,128)(2,1)S(1)} %bitcast.18), channel_id=1, source_target_pairs={{0,2},{1,3},{2,0},{3,1},{4,6},{5,7},{6,4},{7,5},{8,10},{9,11},{10,... | collective-permute-start | bytes 3145736 | tf_op jit(solution)/shard_map/ppermute | solution.py:939
  75.6 3.4 %shard_map.152 = (bf16[256,1920]{1,0:T(8,128)(2,1)}, bf16[1920,1024]{1,0:T(8,128)(2,1)}) custom-call(bf16[256,1536]{1,0:T(8,128)(2,1)S(1)} %all_gather.11.gathered, bf16[1920,256]{1,0:T(8,128)(2,1)S(1)} %bitcast.22), custom_call_target="tpu_custom_call" | custom-call | flops 4000000000 | bytes 1048576 | tf_op jit(solution)/shard_map/pallas_call | solution.py:59
  78.9 0.0 copy-done.15
  79.0 7.0 %shard_map.150 = (s32[8,8,128]{2,1,0:T(8,128)}, s32[8,1,256]{2,1,0:T(1,128)}, f32[8,32,256]{2,1,0:T(8,128)}, f32[8,32,1024]{2,1,0:T(8,128)}) custom-call(s32[1]{0:T(128)} %bitcast.9.me, s32[8,8,128]{2,1,0:T(8,128)S(1)} %copy-done.15, s32[8,8,128]{2,1,0:T(8,128)S(1)} %copy-done.17, f32[32,256]{1,0:T(8,128)S(1)} %scatter.4.coef), custom_call_target="tpu_custom_call" | custom-call | flops 4000000000 | bytes 1048576 | tf_op jit(solution)/shard_map/pallas_call | solution.py:59
  85.9 0.0 collective-permute-start.4
  85.9 0.0 all-to-all-done.1.shared
  85.9 5.2 %shard_map.153 = bf16[8,32,256]{2,1,0:T(8,128)(2,1)} custom-call(s32[8]{0:T(128)} %bitcast.38, s32[8]{0:T(128)} %bitcast.41, bf16[8,80,512]{2,1,0:T(8,128)(2,1)S(1)} %all-to-all-done.1.shared, bf16[1920,1024]{1,0:T(8,128)(2,1)} %get-tuple-element.58.products_far, s32[8,128]{1,0:T(8,128)S(1)} %bitcast.34, s32[8,128]{1,0:T(8,128)S(1)} %bitcast.31), custom_call_target="tpu_custom_call" | custom-call | flops 4000000000 | bytes 1048576 | tf_op jit(solution)/shard_map/pallas_call | solution.py:59
  91.1 6.0 %all-to-all-start.2 = ((bf16[8,32,256]{2,1,0:T(8,128)(2,1)}), bf16[8,32,256]{2,1,0:T(8,128)(2,1)S(1)}, u32[]{:S(2)}, u32[]{:S(2)}) async-start(bf16[8,32,256]{2,1,0:T(8,128)(2,1)} %shard_map.153), calls=%async_computation.2 | async-start | bytes 262144 | tf_op jit(solution)/shard_map/all_to_all | solution.py:1028
  97.1 1.7 %collective-permute-done.3.refs_1_ = bf16[2,1024,256]{2,1,0:T(8,128)(2,1)} collective-permute-done((bf16[2,1024,256]{2,1,0:T(8,128)(2,1)S(1)}, bf16[2,1024,256]{2,1,0:T(8,128)(2,1)}, u32[]{:S(2)}, u32[]{:S(2)}) %collective-permute-start.3) | collective-permute-done | bytes 1048608 | tf_op jit(solution)/shard_map/ppermute | solution.py:939
  98.8 0.0 collective-permute-start.5
  98.8 5.8 %shard_map.151 = (bf16[8,64,1024]{2,1,0:T(8,128)(2,1)}, bf16[8,64,256]{2,1,0:T(8,128)(2,1)S(1)}) custom-call(s32[64]{0:T(128)} %reshape_squeeze.3.owners, s32[8,8,128]{2,1,0:T(8,128)} %get-tuple-element.48.targets, s32[8,8,128]{2,1,0:T(8,128)} %get-tuple-element.51.ranks, bf16[8,80,512]{2,1,0:T(8,128)(2,1)S(1)} %all-to-all-done.1.shared), custom_call_target="tpu_custom_call" | custom-call | flops 6000000000 | bytes 1048576 | tf_op jit(solution)/shard_map/pallas_call | solution.py:59
  104.5 0.2 all-to-all-done.2.coefs
  104.8 0.0 copy-done.13
  104.8 6.8 %shard_map.154 = bf16[4,64,640]{2,1,0:T(8,128)(2,1)S(1)} custom-call(bf16[8,64,256]{2,1,0:T(8,128)(2,1)S(1)} %get-tuple-element.53.slot_grads, s32[8,1,256]{2,1,0:T(1,128)S(1)} %copy-done.19, f32[8,32,256]{2,1,0:T(8,128)S(1)} %copy-done.12, bf16[256,1920]{1,0:T(8,128)(2,1)} %get-tuple-element.56.bases_far, bf16[64,256]{1,0:T(8,128)(2,1)S(1)} %bitcast.24, ...), custom_call_target="tpu_custom_call" | custom-call | flops 5000000000 | bytes 1048576 | tf_op jit(solution)/shard_map/pallas_call | solution.py:59
  111.6 9.2 %all_to_all.20.arrived = bf16[4,64,640]{2,1,0:T(8,128)(2,1)S(1)} all-to-all(bf16[4,64,640]{2,1,0:T(8,128)(2,1)S(1)} %shard_map.154), channel_id=1, replica_groups=mesh['dom'=8,'feat'=4] {'feat'}, dimensions={0} | all-to-all | bytes 655360 | tf_op jit(solution)/shard_map/all_to_all | solution.py:1054
  120.8 0.7 shard_map.155
  121.5 0.0 collective-permute-done.4.refs_2_
  121.5 0.0 collective-permute-done.5.refs_3_
  121.5 14.0 %shard_map.157 = (f32[1920,256]{1,0:T(8,128)}, f32[64,256]{1,0:T(8,128)}) custom-call(s32[4]{0:T(128)} %pad_add_fusion.place, f32[8,32,1024]{2,1,0:T(8,128)} %get-tuple-element.60.mix_far, bf16[8,64,1024]{2,1,0:T(8,128)(2,1)} %get-tuple-element.61.grads_far, bf16[256,4096]{1,0:T(8,128)(2,1)} %get-tuple-element.64.full_far, ...), custom_call_target="tpu_custom_call" | custom-call | flops 12000000000 | bytes 1048576 | tf_op jit(solution)/shard_map/pallas_call | solution.py:59
  (18 shorter events, 0.0 us)
Async XLA Ops:
  0.6 24.8 %copy-start.5 = (bf16[64,512]{1,0:T(8,128)(2,1)S(1)}, bf16[64,512]{1,0:T(8,128)(2,1)}, u32[]{:S(2)}) copy-start(bf16[64,512]{1,0:T(8,128)(2,1)} %feats.3) | copy-start | bytes 196612
  0.6 24.7 %copy-start.8 = (s32[1024,1]{0,1:T(1,128)S(1)}, s32[1024,1]{0,1:T(1,128)}, u32[]{:S(2)}) copy-start(s32[1024,1]{0,1:T(1,128)} %param.17) | copy-start | bytes 12292
  0.7 24.7 %copy-start.9 = (s32[1024]{0:T(1024)S(1)}, s32[1024]{0:T(1024)}, u32[]{:S(2)}) copy-start(s32[1024]{0:T(1024)} %param.18) | copy-start | bytes 12292
  25.4 13.1 %copy-start.21 = (f32[237,30]{0,1:T(8,128)S(1)}, f32[237,30]{0,1:T(8,128)}, u32[]{:S(2)}) copy-start(f32[237,30]{0,1:T(8,128)} %param.16) | copy-start | bytes 85324
  25.4 13.1 %copy-start = (bf16[30,64,256]{2,1,0:T(8,128)(2,1)S(1)}, bf16[30,64,256]{2,1,0:T(8,128)(2,1)}, u32[]{:S(2)}) copy-start(bf16[30,64,256]{2,1,0:T(8,128)(2,1)} %param.15) | copy-start | bytes 2949124
  25.4 13.1 %copy-start.10 = (s32[1024]{0:T(1024)S(1)}, s32[1024]{0:T(1024)}, u32[]{:S(2)}) copy-start(s32[1024]{0:T(1024)} %param.19) | copy-start | bytes 12292
  25.4 13.1 %copy-start.11 = (s32[1024]{0:T(1024)S(1)}, s32[1024]{0:T(1024)}, u32[]{:S(2)}) copy-start(s32[1024]{0:T(1024)} %param.20) | copy-start | bytes 12292
  29.4 9.1 %copy-start.14 = (s32[8,8,128]{2,1,0:T(8,128)}, s32[8,8,128]{2,1,0:T(8,128)S(1)}, u32[]{:S(2)}) copy-start(s32[8,8,128]{2,1,0:T(8,128)S(1)} %get-tuple-element.49.ids) | copy-start | bytes 98308
  29.4 9.2 %copy-start.16 = (s32[8,8,128]{2,1,0:T(8,128)}, s32[8,8,128]{2,1,0:T(8,128)S(1)}, u32[]{:S(2)}) copy-start(s32[8,8,128]{2,1,0:T(8,128)S(1)} %get-tuple-element.50.rels) | copy-start | bytes 98308
  29.4 17.5 %copy-start.1 = (bf16[64,4096]{1,0:T(8,128)(2,1)}, bf16[64,4096]{1,0:T(8,128)(2,1)S(1)}, u32[]{:S(2)}) copy-start(bf16[64,4096]{1,0:T(8,128)(2,1)S(1)} %get-tuple-element.63.refs_0_) | copy-start | bytes 1572868
  38.0 14.2 %collective-permute-start = (bf16[64,4096]{1,0:T(8,128)(2,1)S(1)}, bf16[64,4096]{1,0:T(8,128)(2,1)S(1)}, u32[]{:S(2)}, u32[]{:S(2)}) collective-permute-start(bf16[64,4096]{1,0:T(8,128)(2,1)S(1)} %get-tuple-element.63.refs_0_), channel_id=1, source_target_pairs={{0,2},{1,3},{2,0},{3,1},{4,6},{5,7},{6,4},{7,5},{8,10},{9,11},{10,... | collective-permute-start | bytes 1572872 | tf_op jit(solution)/shard_map/ppermute | solution.py:939
  38.6 13.6 %copy-start.20 = (s32[8,8,128]{2,1,0:T(8,128)S(1)}, s32[8,8,128]{2,1,0:T(8,128)}, u32[]{:S(2)}) copy-start(s32[8,8,128]{2,1,0:T(8,128)} %get-tuple-element.47) | copy-start | bytes 98308
  38.6 18.8 %copy-start.6 = (bf16[64,512]{1,0:T(8,128)(2,1)S(1)}, bf16[64,512]{1,0:T(8,128)(2,1)}, u32[]{:S(2)}) copy-start(bf16[64,512]{1,0:T(8,128)(2,1)} %cotangent.1) | copy-start | bytes 196612
  38.6 18.8 %copy-start.7 = (bf16[256,64]{0,1:T(8,128)(2,1)S(1)}, bf16[256,64]{0,1:T(8,128)(2,1)}, u32[]{:S(2)}) copy-start(bf16[256,64]{0,1:T(8,128)(2,1)} %param.14) | copy-start | bytes 98308
  41.6 15.8 %all-to-all-start = ((bf16[16,80,128]{2,1,0:T(8,128)(2,1)}), bf16[16,80,128]{2,1,0:T(8,128)(2,1)S(1)}, u32[]{:S(2)}, u32[]{:S(2)}) async-start(bf16[16,80,128]{2,1,0:T(8,128)(2,1)} %shard_map.148), calls=%async_computation | async-start | bytes 655360 | tf_op jit(solution)/shard_map/all_to_all | solution.py:992
  46.8 16.0 %collective-permute-start.1 = (bf16[64,4096]{1,0:T(8,128)(2,1)S(1)}, bf16[64,4096]{1,0:T(8,128)(2,1)}, u32[]{:S(2)}, u32[]{:S(2)}) collective-permute-start(bf16[64,4096]{1,0:T(8,128)(2,1)S(1)} %get-tuple-element.63.refs_0_), channel_id=1, source_target_pairs={{0,1},{1,0},{2,3},{3,2},{4,5},{5,4},{6,7},{7,6},{8,9},{9,8},{10,11... | collective-permute-start | bytes 1572872 | tf_op jit(solution)/shard_map/ppermute | solution.py:939
  52.2 7.0 %copy-start.3 = (bf16[64,4096]{1,0:T(8,128)(2,1)}, bf16[64,4096]{1,0:T(8,128)(2,1)S(1)}, u32[]{:S(2)}) copy-start(bf16[64,4096]{1,0:T(8,128)(2,1)S(1)} %collective-permute-done.refs_1_) | copy-start | bytes 1572868
  52.2 10.7 %collective-permute-start.2 = (bf16[64,4096]{1,0:T(8,128)(2,1)S(1)}, bf16[64,4096]{1,0:T(8,128)(2,1)}, u32[]{:S(2)}, u32[]{:S(2)}) collective-permute-start(bf16[64,4096]{1,0:T(8,128)(2,1)S(1)} %collective-permute-done.refs_1_), channel_id=1, source_target_pairs={{0,1},{1,0},{2,3},{3,2},{4,5},{5,4},{6,7},{7,6},{8,9},{9,8},{10,11... | collective-permute-start | bytes 1572872 | tf_op jit(solution)/shard_map/ppermute | solution.py:939
  59.2 26.7 %all-to-all-start.1 = ((bf16[8,80,512]{2,1,0:T(8,128)(2,1)}), bf16[8,80,512]{2,1,0:T(8,128)(2,1)S(1)}, u32[]{:S(2)}, u32[]{:S(2)}) async-start(bf16[8,80,512]{2,1,0:T(8,128)(2,1)} %get-tuple-element.52), calls=%async_computation.1 | async-start | bytes 1310720 | tf_op jit(solution)/shard_map/all_to_all | solution.py:1009
  62.9 1.0 copy-start.2
  63.9 1.0 copy-start.4
  64.9 0.8 copy-start.18
  74.1 4.9 %copy-start.15 = (s32[8,8,128]{2,1,0:T(8,128)S(1)}, s32[8,8,128]{2,1,0:T(8,128)}, u32[]{:S(2)}) copy-start(s32[8,8,128]{2,1,0:T(8,128)} %copy-done.14) | copy-start | bytes 98308
  74.1 4.9 %copy-start.17 = (s32[8,8,128]{2,1,0:T(8,128)S(1)}, s32[8,8,128]{2,1,0:T(8,128)}, u32[]{:S(2)}) copy-start(s32[8,8,128]{2,1,0:T(8,128)} %copy-done.16) | copy-start | bytes 98308
  74.1 24.7 %collective-permute-start.3 = (bf16[2,1024,256]{2,1,0:T(8,128)(2,1)S(1)}, bf16[2,1024,256]{2,1,0:T(8,128)(2,1)}, u32[]{:S(2)}, u32[]{:S(2)}) collective-permute-start(bf16[2,1024,256]{2,1,0:T(8,128)(2,1)S(1)} %bitcast.18), channel_id=1, source_target_pairs={{0,2},{1,3},{2,0},{3,1},{4,6},{5,7},{6,4},{7,5},{8,10},{9,11},{10,... | collective-permute-start | bytes 3145736 | tf_op jit(solution)/shard_map/ppermute | solution.py:939
  85.9 35.6 %collective-permute-start.4 = (bf16[2,1024,256]{2,1,0:T(8,128)(2,1)S(1)}, bf16[2,1024,256]{2,1,0:T(8,128)(2,1)}, u32[]{:S(2)}, u32[]{:S(2)}) collective-permute-start(bf16[2,1024,256]{2,1,0:T(8,128)(2,1)S(1)} %bitcast.19), channel_id=1, source_target_pairs={{0,1},{1,0},{2,3},{3,2},{4,5},{5,4},{6,7},{7,6},{8,9},{9,8},{10,11... | collective-permute-start | bytes 3145736 | tf_op jit(solution)/shard_map/ppermute | solution.py:939
  91.1 13.7 %all-to-all-start.2 = ((bf16[8,32,256]{2,1,0:T(8,128)(2,1)}), bf16[8,32,256]{2,1,0:T(8,128)(2,1)S(1)}, u32[]{:S(2)}, u32[]{:S(2)}) async-start(bf16[8,32,256]{2,1,0:T(8,128)(2,1)} %shard_map.153), calls=%async_computation.2 | async-start | bytes 262144 | tf_op jit(solution)/shard_map/all_to_all | solution.py:1028
  98.8 22.7 %collective-permute-start.5 = (bf16[2,1024,256]{2,1,0:T(8,128)(2,1)}, bf16[2,1024,256]{2,1,0:T(8,128)(2,1)}, u32[]{:S(2)}, u32[]{:S(2)}) collective-permute-start(bf16[2,1024,256]{2,1,0:T(8,128)(2,1)} %collective-permute-done.3.refs_1_), channel_id=1, source_target_pairs={{0,1},{1,0},{2,3},{3,2},{4,5},{5,4},{6,7},{7,6},{8,9},{9,8},{10,11... | collective-permute-start | bytes 3145736 | tf_op jit(solution)/shard_map/ppermute | solution.py:939
  98.8 6.0 %copy-start.12 = (f32[8,32,256]{2,1,0:T(8,128)S(1)}, f32[8,32,256]{2,1,0:T(8,128)}, u32[]{:S(2)}) copy-start(f32[8,32,256]{2,1,0:T(8,128)} %get-tuple-element.55.slot_mix) | copy-start | bytes 786436
  98.8 6.0 %copy-start.13 = (bf16[64,512]{1,0:T(8,128)(2,1)S(1)}, bf16[64,512]{1,0:T(8,128)(2,1)}, u32[]{:S(2)}) copy-start(bf16[64,512]{1,0:T(8,128)(2,1)} %get-tuple-element.57.grad_pre) | copy-start | bytes 196612
  98.8 6.0 %copy-start.19 = (s32[8,1,256]{2,1,0:T(1,128)S(1)}, s32[8,1,256]{2,1,0:T(1,128)}, u32[]{:S(2)}) copy-start(s32[8,1,256]{2,1,0:T(1,128)} %get-tuple-element.54.slot_rows) | copy-start | bytes 24580

commit v4 on v3

--- a/solution.py
+++ b/solution.py
@@ -29,7 +29,7 @@
 
 
 def call(
-    kernel, out_shape, smem=(), scratch=(), count=0, us=4, far=(), far_out=(), raw=()
+    kernel, out_shape, smem=(), scratch=(), count=0, us=4, far=(), far_out=(), raw=(), raw_out=()
 ):
     specs = [
         pl.BlockSpec(
@@ -42,12 +42,15 @@
     shapes = tuple(
         pltpu.HBM(o.shape, o.dtype) if k in far_out else o for k, o in enumerate(shapes)
     )
-    outs = pl.BlockSpec(memory_space=pltpu.VMEM)
+    outs = tuple(
+        pl.BlockSpec(memory_space=pltpu.HBM if k in raw_out else pltpu.VMEM)
+        for k in range(len(shapes))
+    )
     run = pl.pallas_call(
         kernel,
         out_shape=shapes[0] if single else shapes,
         in_specs=specs,
-        out_specs=outs if single else tuple(outs for _ in shapes),
+        out_specs=outs[0] if single else outs,
         scratch_shapes=scratch,
         compiler_params=pltpu.CompilerParams(vmem_limit_bytes=24 << 20),
         cost_estimate=pl.CostEstimate(
@@ -710,25 +713,52 @@
         out[start:stop, :] = dot(bases[start:stop, :], gathered[:, :edge_count]).astype(BF)
 
 
-def coef_kernel(
-    owners, valid, shared, products_far, rel, dst, out, scaled, grads, products, sems
+def grads_kernel(
+    owners,
+    me,
+    targets,
+    ranks,
+    shared,
+    products_far,
+    rel,
+    grads,
+    slot_grads,
+    coef_out,
+    node,
+    comp,
+    scaled,
+    products,
+    sems,
 ):
     fetched = fetch(((products_far, products),), sems)
-    blocks = rel.shape[0]
-    copies, _, relations = out.shape
+    dom_count, blocks, _ = targets.shape
+    slot_cap = comp.shape[2]
     entities = shared.shape[2]
     quarter = shared.shape[1] - 16
+    copies, _, relations = coef_out.shape
     basis_count = products.shape[0] // quarter
+    for q in range(dom_count):
+        node[q] = scaled_grad(shared, q, quarter)
+    for g in range(dom_count):
+        rows = targets[g]
+        rank = ranks[g].astype(F32).T.astype(I32)
+        for j in range(0, blocks, 2):
+            both = jnp.concatenate([rows[j : j + 1, :], rows[j + 1 : j + 2, :]], axis=1)
+            chosen = hot(iota((entities, 2 * LANES), 0) == both)
+            first, second = owners[g * blocks + j], owners[g * blocks + j + 1]
+            pair = dot(jnp.concatenate([node[first], node[second]], axis=0), chosen).astype(BF)
+            middle = (j + 1) * LANES
+            grads[g, :, j * LANES : middle] = pair[:quarter, :LANES]
+            grads[g, :, middle : middle + LANES] = pair[quarter:, LANES:]
+        for j in range(blocks):
+            lanes = slice(j * LANES, (j + 1) * LANES)
+            comp[g % 2, lanes, :] = hot(iota((LANES, slot_cap), 1) == rank[:, j : j + 1])
+        slot_grads[g] = dot(grads[g], comp[g % 2]).astype(BF)
     scaled[...] = jnp.zeros_like(scaled)
-    for j in range(blocks):
-        live = iota((1, LANES), 1) < valid[j]
-        target = jnp.where(live, dst[j : j + 1, :], entities)
-        chosen = hot(iota((entities, LANES), 0) == target)
-        grads[:, j * LANES : (j + 1) * LANES] = dot(scaled_grad(shared, owners[j], quarter), chosen)
     fetched[0].wait()
     for t in range(blocks // 2):
         lanes = slice(2 * t * LANES, 2 * (t + 1) * LANES)
-        grad = grads[:, lanes]
+        grad = grads[me[0], :, lanes].astype(F32)
         for b in range(basis_count):
             part = products[b * quarter : (b + 1) * quarter, lanes].astype(F32)
             scaled[b : b + 1, lanes] = jnp.sum(part * grad, axis=0, keepdims=True)
@@ -738,30 +768,7 @@
     chosen = rel_hot(kinds, relations)
     total = (dot(chosen, high, NT) + dot(chosen, low, NT)).T.astype(BF)
     for k in range(copies):
-        out[k] = total
-
-
-def grads_kernel(owners, targets, ranks, shared, grads, slot_grads, scaled, comp):
-    dom_count, blocks, _ = targets.shape
-    slot_cap = comp.shape[1]
-    entities = shared.shape[2]
-    quarter = shared.shape[1] - 16
-    for q in range(dom_count):
-        scaled[q] = scaled_grad(shared, q, quarter)
-
-    def step(g, carry):
-        rows = targets[g]
-        rank = ranks[g]
-        for j in range(blocks):
-            lanes = slice(j * LANES, (j + 1) * LANES)
-            chosen = hot(iota((entities, LANES), 0) == rows[j : j + 1, :])
-            grads[g, :, lanes] = dot(scaled[owners[g * blocks + j]], chosen).astype(BF)
-            comp[g % 2, :, lanes] = hot(iota((slot_cap, LANES), 0) == rank[j : j + 1, :])
-        slot_grads[g] = dot(grads[g], comp[g % 2], NT).astype(BF)
-        return carry
-
-    for g in range(dom_count):
-        step(g, 0)
+        coef_out[k] = total
 
 
 def mix_rows(mix, grad, quarter):
@@ -773,12 +780,15 @@
     return jnp.concatenate(pieces, axis=0)
 
 
+def column(row):
+    return jnp.broadcast_to(row.astype(F32), (8, row.shape[1])).T[:, :1].astype(I32)
+
+
 def scatter_kernel(
-    slot_grads, slot_rows, slot_mix, bases_far, weight, grad_pre, coefs, out, total, bases_t, sems
+    slot_grads, slot_rows, slot_mix, bases_far, weight, grad_pre, out, total, bases_t, rows, sems
 ):
     copies = fetch(((bases_far, bases_t),), sems)
     dom_count, quarter, slot_cap = slot_grads.shape
-    padded = slot_mix.shape[1]
     basis_count = bases_t.shape[1] // quarter
     entities = grad_pre.shape[1]
     peers = out.shape[0]
@@ -788,23 +798,18 @@
 
     copies[0].wait()
 
-    def step(g, carry):
-        combined = mix_rows(slot_mix[g][:basis_count], slot_grads[g], quarter)
-        partial = dot(bases_t[...], combined).astype(BF)
-        chosen = hot(iota((entities, slot_cap), 0) == slot_rows[g])
-        total[...] += dot(partial, chosen, NT)
-        return carry
-
-    for g in range(dom_count):
-        step(g, 0)
-    coef = coefs[0].astype(F32)
-    for g in range(1, dom_count):
-        coef = coef + coefs[g].astype(F32)
-    coef = coef.astype(BF)
+    group = 4 if dom_count % 4 == 0 else 1
+    for start in range(0, dom_count, group):
+        part = range(start, start + group)
+        mix = jnp.concatenate([slot_mix[g][:basis_count] for g in part], axis=1)
+        grad = jnp.concatenate([slot_grads[g] for g in part], axis=1)
+        partial = dot(bases_t[...], mix_rows(mix, grad, quarter)).astype(BF)
+        for n, g in enumerate(part):
+            chosen = hot(iota((slot_cap, entities), 1) == column(slot_rows[g]))
+            rows[n * slot_cap : (n + 1) * slot_cap, :] = chosen
+        total[...] += dot(partial, rows[: group * slot_cap, :])
     for f in range(peers):
-        out[f, :, :entities] = total[f * quarter : (f + 1) * quarter].astype(BF)
-        out[f, :padded, entities:] = coef[:, :LANES]
-        out[f, padded : 2 * padded, entities:] = coef[:, LANES:]
+        out[f] = total[f * quarter : (f + 1) * quarter].astype(BF)
 
 
 def fetch(pairs, sems):
@@ -817,45 +822,67 @@
 
 
 def weights_kernel(scale, place, mix_far, grads_far, full_far, shared, *refs):
-    rows, (out, own_out, mix, grads, full, sems) = refs[:-6], refs[-6:]
-    copies = fetch(((mix_far, mix), (grads_far, grads), (full_far, full)), sems)
+    rows, (out, own_out, total, mix, grads, full, sems, done) = refs[:-8], refs[-8:]
     dom_count, quarter, _ = grads.shape
     entities = shared.shape[2]
     basis_count = out.shape[0] // quarter
     group = 5
-    copies[0].wait()
-    copies[1].wait()
-    for part, piece in enumerate(rows):
-        count = piece.shape[0]
-        for k in range(count):
-            g = place[part] * count + k
-            grad = grads[g]
-            for c in range(0, basis_count, group):
-                stop = min(c + group, basis_count)
-                combined = mix_rows(mix[g, c:stop, :], grad, quarter)
-                total = dot(combined, piece[k])
-                lanes = slice(c * quarter, stop * quarter)
-                if part > 0 or k > 0:
-                    total = total + out[lanes, :]
-                if part == len(rows) - 1 and k == count - 1:
-                    total = total * scale
-                out[lanes, :] = total
-    copies[2].wait()
-    own = jnp.zeros(own_out.shape, F32)
+    count = rows[0].shape[0]
+    order = [place[part] * count + k for part in range(len(rows)) for k in range(count)]
+    pairs = []
+    for n, g in enumerate(order):
+        pairs += [(mix_far.at[g], mix.at[n]), (grads_far.at[g], grads.at[n])]
+    copies = fetch(pairs + [(full_far, full)], sems)
+    stores = []
+    for n in range(dom_count):
+        copies[2 * n].wait()
+        copies[2 * n + 1].wait()
+        grad = grads[n]
+        for c in range(0, basis_count, group):
+            stop = min(c + group, basis_count)
+            lanes = slice(c * quarter, stop * quarter)
+            sums = dot(mix_rows(mix[n, c:stop, :], grad, quarter), rows[n // count][n % count])
+            if n > 0:
+                sums = sums + total[lanes, :]
+            if n == dom_count - 1:
+                sums = sums * scale
+            total[lanes, :] = sums
+            if n == dom_count - 1:
+                store = pltpu.make_async_copy(
+                    total.at[lanes, :], out.at[lanes, :], done.at[c // group]
+                )
+                store.start()
+                stores.append(store)
+    copies[2 * dom_count].wait()
+    own = jnp.zeros((full.shape[0], quarter), F32)
     for q in range(dom_count):
         lanes = slice(q * entities, (q + 1) * entities)
-        own = own + dot(shared[q, :quarter, :], full[:, lanes], NT)
-    own_out[...] = own * scale
+        own = own + dot(full[:, lanes], shared[q, :quarter, :], NT)
+    own_out[...] = own.T * scale
+    for store in stores:
+        store.wait()
+
+
+def merge_kernel(sums, coefs, out):
+    peers, _, entities = sums.shape
+    padded = coefs.shape[1]
+    coef = coefs[0].astype(F32)
+    for g in range(1, coefs.shape[0]):
+        coef = coef + coefs[g].astype(F32)
+    coef = coef.astype(BF)
+    for f in range(peers):
+        out[f, :, :entities] = sums[f]
+        out[f, :padded, entities:] = coef[:, :LANES]
+        out[f, padded:, entities:] = coef[:, LANES:]
 
 
 def finish_kernel(padded, scale, arrived, grad_feats, coef_out):
-    peers, _, _ = arrived.shape
     entities = grad_feats.shape[1]
     sums = arrived[0].astype(F32)
-    for f in range(1, peers):
+    for f in range(1, arrived.shape[0]):
         sums = sums + arrived[f].astype(F32)
     grad_feats[...] = sums[:, :entities].astype(BF)
-    coef = jnp.concatenate([sums[:padded, entities:], sums[padded : 2 * padded, entities:]], axis=1)
+    coef = jnp.concatenate([sums[:padded, entities:], sums[padded:, entities:]], axis=1)
     coef_out[...] = coef[: coef_out.shape[0], : coef_out.shape[1]] * scale
 
 
@@ -895,6 +922,7 @@
     bases_flat = bases.reshape(flat, model)
     weight_t = self_weight.T
     coef_t = jnp.zeros((padded, relations), F32).at[:basis_count, :relation_count].set(coef.T)
+    dom_place = lax.axis_index("dom").astype(I32).reshape(1)
     feat_place = lax.axis_index("feat").astype(I32)
 
     tall = (entities // LANES) * quarter + 8 * blocks
@@ -957,7 +985,7 @@
         smem=(0,),
         count=2 + feat_count,
         us=10,
-        far=(0,),
+        far=tuple(range(2 + feat_count)),
         far_out=(1,),
     )(place, spans, *doubled(wide))
     rows = doubled(rows.reshape(part_count, edge_count, model))
@@ -979,7 +1007,7 @@
         us=4,
         far=(0,),
         far_out=(0, 1, 2, 3),
-    )(lax.axis_index("dom").astype(I32).reshape(1), ids, rels, coef_t)
+    )(dom_place, ids, rels, coef_t)
 
     messages = call(
         functools.partial(message_kernel, block_cap, entities),
@@ -1015,42 +1043,47 @@
         us=4,
         far_out=(0, 1),
     )(gathered, bases_flat)
-    coef_part = call(
-        coef_kernel,
-        shape((dom_count, padded, relations), BF),
+    grads, slot_grads, coef_part = call(
+        grads_kernel,
+        (
+            shape((dom_count, quarter, edge_count), BF),
+            shape((dom_count, quarter, slot_cap), BF),
+            shape((dom_count, padded, relations), BF),
+        ),
         smem=(0, 1),
-        scratch=[pltpu.VMEM((padded, edge_count), F32), pltpu.VMEM((quarter, edge_count), F32), pltpu.VMEM((flat, edge_count), BF), pltpu.SemaphoreType.DMA((1,))],
-        raw=(3,),
-        count=6,
-        us=4,
-        far=(0, 1),
-    )(owners, valid, nodes, products, rel, dst)
-    coefs = lax.all_to_all(coef_part, "dom", split_axis=0, concat_axis=0, tiled=True)
-    grads, slot_grads = call(
-        grads_kernel,
-        (shape((dom_count, quarter, edge_count), BF), shape((dom_count, quarter, slot_cap), BF)),
-        smem=(0,),
         scratch=[
             pltpu.VMEM((dom_count, quarter, entities), BF),
-            pltpu.VMEM((2, slot_cap, edge_count), BF),
+            pltpu.VMEM((2, edge_count, slot_cap), BF),
+            pltpu.VMEM((padded, edge_count), F32),
+            pltpu.VMEM((flat, edge_count), BF),
+            pltpu.SemaphoreType.DMA((1,)),
         ],
-        count=4,
-        us=6,
-        far=(0, 1, 2),
+        count=7,
+        us=8,
+        far=(0, 1, 2, 3),
         far_out=(0,),
-    )(owner_list, targets, ranks, nodes)
-    sent = call(
+        raw=(5,),
+    )(owner_list, dom_place, targets, ranks, nodes, products, rel)
+    coefs = lax.all_to_all(
+        coef_part, "dom", split_axis=0, concat_axis=0, tiled=True
+    )
+    sums = call(
         scatter_kernel,
-        shape((feat_count, quarter, entities + LANES), BF),
+        shape((feat_count, quarter, entities), BF),
         scratch=[
             pltpu.VMEM((model, entities), F32),
             pltpu.VMEM((model, flat), BF),
+            pltpu.VMEM((4 * slot_cap, entities), BF),
             pltpu.SemaphoreType.DMA((1,)),
         ],
         raw=(3,),
-        count=7,
+        far=(1, 2, 5),
+        count=6,
         us=5,
-    )(slot_grads, slot_rows, slot_mix, bases_t, weight_t, grad_pre, coefs)
+    )(slot_grads, slot_rows, slot_mix, bases_t, weight_t, grad_pre)
+    sent = call(
+        merge_kernel, shape((feat_count, quarter, entities + LANES), BF), count=2, us=1
+    )(sums, coefs)
     arrived = lax.all_to_all(sent, "feat", split_axis=0, concat_axis=0, tiled=True)
     grad_bases, grad_self = call(
         functools.partial(weights_kernel, scale),
@@ -1060,11 +1093,14 @@
         us=12,
         far=(0,),
         raw=(1, 2, 3),
+        raw_out=(0,),
         scratch=[
+            pltpu.VMEM((flat, model), F32),
             pltpu.VMEM((dom_count, padded, edge_count), F32),
             pltpu.VMEM((dom_count, quarter, edge_count), BF),
             pltpu.VMEM((model, dom_count * entities), BF),
-            pltpu.SemaphoreType.DMA((3,)),
+            pltpu.SemaphoreType.DMA((2 * dom_count + 1,)),
+            pltpu.SemaphoreType.DMA((basis_count,)),
         ],
     )(place, mix, grads, full, nodes, *rows)
     grad_feats, coef_total = call(

time: 137 us -> 142 us (1.036)
  waiting for transfers between devices: 10.8 us -> 24.1 us
  Pallas kernels: 60.9 us -> 56.3 us
  local copies, waits for them, and re-layouts: 3.8 us -> 0.96 us
    ppermute x6, waiting for transfers between devices: 6.92 us -> 17.1 us  [doubled(): pieces = pieces + [lax.ppermute(piece, 'feat', links) for piece in pieces]]
    pallas_call x12, Pallas kernels: 60.9 us -> 56.3 us  [apply(): run(*(pltpu.with_memory_space_constraint(a, pltpu.HBM) if k in far or k i...]
    unnamed x44 -> x32, local copies, waits for them, and re-layouts: 2.93 us -> 0.08 us
    all_to_all x1, waiting for transfers between devices: 0.21 us -> 2.57 us  [body_few(): lax.all_to_all(coef_part, 'dom', split_axis=0, concat_axis=0, tiled=True)]
  transfers between devices with their start and end apart: 9 -> 9, of which waited for: 4 -> 4; matrix products, arithmetic and copies ran while one was open for 1% -> 1% of each run, Pallas kernels for 31% -> 26%
where the time goes in v4:
time: 142 us
  Pallas kernels  56.3 us (40%)
  blocking collectives  41.7 us (29%)
  waiting for transfers between devices  24.1 us (17%)
  starting transfers between devices  16.8 us (12%)
    pallas_call x12, Pallas kernels, apply(): run(*(pltpu.with_memory_space_constraint(a, pltpu.HBM) if k in far or k i...  56.3 us
    all_gather x1, blocking collectives, body_few(): lax.all_gather(shared, 'dom', axis=0, tiled=True, axis_index_groups=far)  17.7 us
    ppermute x6, waiting for transfers between devices, doubled(): pieces = pieces + [lax.ppermute(piece, 'feat', links) for piece in pieces]  17.1 us
    all_to_all x1, blocking collectives, body_few(): lax.all_to_all(sent, 'feat', split_axis=0, concat_axis=0, tiled=True)  9.28 us
    all_gather x1, blocking collectives, body_few(): gathered = lax.all_gather(mine, 'feat', axis=0, tiled=True)  8.62 us
    all_gather x1, blocking collectives, body_few(): lax.all_gather(packed, 'dom', axis=0, tiled=True, axis_index_groups=near)  6.06 us
    all_to_all x1, starting transfers between devices, body_few(): lax.all_to_all(coef_part, 'dom', split_axis=0, concat_axis=0, tiled=True)  5.72 us
    all_to_all x1, starting transfers between devices, body_few(): lax.all_to_all(messages, 'dom', split_axis=0, concat_axis=0, tiled=True)  5.25 us
  transfers between devices with their start and end apart: 9, of which 4 were waited for; matrix products, arithmetic and copies ran while one was open for 1% of the time, Pallas kernels for 26%

profile of v4, /device:TPU:0, one launch (start us, length us, event | category | flops | bytes accessed | tf_op | source)
XLA Modules:
  0.0 141.6 jit_solution(4760561035910918107)
XLA Ops:
  0.6 0.0 copy-start.2
  0.6 0.0 copy-start.5
  0.7 0.0 copy-start.6
  0.7 0.9 shard_map.146
  1.6 6.1 %all_gather.9 = bf16[2,320,128]{2,1,0:T(8,128)(2,1)S(1)} all-gather(bf16[1,320,128]{2,1,0:T(8,128)(2,1)S(1)} %shard_map.146), channel_id=1, replica_groups={{0,4},{8,12},{16,20},{24,28},{1,5},{9,13},{17,21},{25,29},{2,6},{10,14}..., dimensions={0}, use_global_device_ids=true | all-gather | bytes 245760 | tf_op jit(solution)/shard_map/all_gather | solution.py:941
  7.7 17.7 %all_gather.10.shared = bf16[8,320,128]{2,1,0:T(8,128)(2,1)S(1)} all-gather(bf16[2,320,128]{2,1,0:T(8,128)(2,1)S(1)} %all_gather.9), channel_id=1, replica_groups={{0,8,16,24},{4,12,20,28},{1,9,17,25},{5,13,21,29},{2,10,18,26},{6,14,22..., dimensions={0}, use_global_device_ids=true | all-gather | bytes 819200 | tf_op jit(solution)/shard_map/all_gather | solution.py:942
  25.4 0.0 copy-done.2
  25.4 0.0 copy-done.5
  25.4 0.0 copy-done.6
  25.4 0.0 copy-start.14
  25.4 0.0 copy-start
  25.4 0.0 copy-start.7
  25.4 0.0 copy-start.8
  25.4 3.9 %shard_map.147 = (bf16[64,1536]{1,0:T(8,128)(2,1)S(1)}, bf16[64,4096]{1,0:T(8,128)(2,1)S(1)}, s32[8,8,128]{2,1,0:T(8,128)S(1)}, s32[32,1,256]{2,1,0:T(1,128)}, s...) custom-call(bf16[8,320,128]{2,1,0:T(8,128)(2,1)S(1)} %all_gather.10.shared, ...), custom_call_target="tpu_custom_call" | custom-call | flops 4000000000 | bytes 1048576 | tf_op jit(solution)/shard_map/pallas_call | solution.py:62
  29.4 0.0 copy-start.9
  29.4 0.0 copy-start.11
  29.4 8.6 %all_gather.11.gathered = bf16[256,1536]{1,0:T(8,128)(2,1)S(1)} all-gather(bf16[64,1536]{1,0:T(8,128)(2,1)S(1)} %get-tuple-element.45), channel_id=1, replica_groups=mesh['dom'=8,'feat'=4] {'feat'}, dimensions={0}, use_global_device_ids=true | all-gather | bytes 983040 | tf_op jit(solution)/shard_map/all_gather | solution.py:960
  38.0 0.5 collective-permute-start
  38.5 0.0 copy-done.14
  38.5 0.0 copy-done.9
  38.5 0.0 copy-done.11
  38.5 0.0 copy-done
  38.5 0.0 copy-done.7
  38.5 0.0 copy-done.8
  38.6 0.0 copy-start.3
  38.6 0.0 copy-start.4
  38.6 3.0 %shard_map.148 = bf16[16,80,128]{2,1,0:T(8,128)(2,1)} custom-call(s32[8]{0:T(128)} %bitcast.36, s32[8]{0:T(128)} %bitcast.38, bf16[256,1536]{1,0:T(8,128)(2,1)S(1)} %all_gather.11.gathered, bf16[1920,256]{1,0:T(8,128)(2,1)S(1)} %bitcast.21, f32[32,256]{1,0:T(8,128)S(1)} %scatter.4.coef, s32[8,128]{1,0:T(8,128)S(1)} %bitcast.32, s32[8,128]{1,0:T(8,128)S(1)} %bitcast.30), custom_call_target="tpu_custom_call" | custom-call | flops 4000000000 | bytes 1048576 | tf_op jit(solution)/shard_map/pallas_call | solution.py:62
  41.6 5.2 %all-to-all-start = ((bf16[16,80,128]{2,1,0:T(8,128)(2,1)}), bf16[16,80,128]{2,1,0:T(8,128)(2,1)S(1)}, u32[]{:S(2)}, u32[]{:S(2)}) async-start(bf16[16,80,128]{2,1,0:T(8,128)(2,1)} %shard_map.148), calls=%async_computation | async-start | bytes 655360 | tf_op jit(solution)/shard_map/all_to_all | solution.py:1020
  46.9 0.0 copy-done.1
  46.9 0.1 collective-permute-start.1
  46.9 5.2 %collective-permute-done.refs_1_ = bf16[64,4096]{1,0:T(8,128)(2,1)S(1)} collective-permute-done((bf16[64,4096]{1,0:T(8,128)(2,1)S(1)}, bf16[64,4096]{1,0:T(8,128)(2,1)S(1)}, u32[]{:S(2)}, u32[]{:S(2)}) %collective-permute-start) | collective-permute-done | bytes 524320 | tf_op jit(solution)/shard_map/ppermute | solution.py:967
  52.2 0.0 collective-permute-start.2
  52.2 0.8 pad_add_fusion.place
  52.9 4.4 %all-to-all-done.received = bf16[16,80,128]{2,1,0:T(8,128)(2,1)S(1)} async-done(((bf16[16,80,128]{2,1,0:T(8,128)(2,1)}), bf16[16,80,128]{2,1,0:T(8,128)(2,1)S(1)}, u32[]{:S(2)}, u32[]{:S(2)}) %all-to-all-start) | async-done | bytes 327712 | tf_op jit(solution)/shard_map/all_to_all | solution.py:1020
  57.4 0.0 copy-done.3
  57.4 0.0 copy-done.4
  57.4 1.8 %shard_map.149 = (bf16[64,512]{1,0:T(8,128)(2,1)}, bf16[8,80,512]{2,1,0:T(8,128)(2,1)}, bf16[64,512]{1,0:T(8,128)(2,1)}) custom-call(bf16[16,80,128]{2,1,0:T(8,128)(2,1)S(1)} %all-to-all-done.received, bf16[256,1536]{1,0:T(8,128)(2,1)S(1)} %all_gather.11.gathered, bf16[64,256]{1,0:T(8,128)(2,1)S(1)} %bitcast.23, bf16[64,512]{1,0:T(8,128)(2,1)S(1)} %copy-done.3), custom_call_target="tpu_custom_call" | custom-call | flops 4000000000 | bytes 1048576 | tf_op jit(solution)/shard_map/pallas_call | solution.py:62
  59.2 0.0 copy-done.15
  59.2 3.7 %all-to-all-start.1 = ((bf16[8,80,512]{2,1,0:T(8,128)(2,1)}), bf16[8,80,512]{2,1,0:T(8,128)(2,1)S(1)}, u32[]{:S(2)}, u32[]{:S(2)}) async-start(bf16[8,80,512]{2,1,0:T(8,128)(2,1)} %get-tuple-element.53), calls=%async_computation.1 | async-start | bytes 1310720 | tf_op jit(solution)/shard_map/all_to_all | solution.py:1037
  62.9 0.0 collective-permute-done.1.refs_2_
  63.0 0.0 collective-permute-done.2.refs_3_
  63.0 0.0 copy-start.13
  63.0 8.7 %shard_map.156 = (bf16[8,256,256]{2,1,0:T(8,128)(2,1)S(1)}, bf16[256,4096]{1,0:T(8,128)(2,1)}) custom-call(s32[4]{0:T(128)} %pad_add_fusion.place, s32[32,1,256]{2,1,0:T(1,128)} %get-tuple-element.64.spans, bf16[64,4096]{1,0:T(8,128)(2,1)} %copy-done.1, bf16[64,4096]{1,0:T(8,128)(2,1)} %copy-done.15, bf16[64,4096]{1,0:T(8,128)(2,1)} %collective-permute-done.1.refs_2_, ...), custom_call_target="tpu_custom_call" | custom-call | flops 10000000000 | bytes 1048576 | tf_op jit(solution)/shard_map/pallas_call | solution.py:62
  71.7 1.5 %collective-permute-start.3 = (bf16[2,1024,256]{2,1,0:T(8,128)(2,1)S(1)}, bf16[2,1024,256]{2,1,0:T(8,128)(2,1)}, u32[]{:S(2)}, u32[]{:S(2)}) collective-permute-start(bf16[2,1024,256]{2,1,0:T(8,128)(2,1)S(1)} %bitcast.18), channel_id=1, source_target_pairs={{0,2},{1,3},{2,0},{3,1},{4,6},{5,7},{6,4},{7,5},{8,10},{9,11},{10,... | collective-permute-start | bytes 3145736 | tf_op jit(solution)/shard_map/ppermute | solution.py:967
  73.2 0.0 copy-done.13
  73.2 0.2 slice_reduce_fusion
  73.4 0.7 reshape_squeeze.3.owners
  74.1 3.4 %shard_map.151 = (bf16[256,1920]{1,0:T(8,128)(2,1)}, bf16[1920,1024]{1,0:T(8,128)(2,1)}) custom-call(bf16[256,1536]{1,0:T(8,128)(2,1)S(1)} %all_gather.11.gathered, bf16[1920,256]{1,0:T(8,128)(2,1)S(1)} %bitcast.22), custom_call_target="tpu_custom_call" | custom-call | flops 4000000000 | bytes 1048576 | tf_op jit(solution)/shard_map/pallas_call | solution.py:62
  77.5 0.0 copy-done.10
  77.5 0.0 copy-done.12
  77.5 6.9 %shard_map.150 = (s32[8,8,128]{2,1,0:T(8,128)}, s32[8,1,256]{2,1,0:T(1,128)}, f32[8,32,256]{2,1,0:T(8,128)}, f32[8,32,1024]{2,1,0:T(8,128)}) custom-call(s32[1]{0:T(128)} %bitcast.9.me, s32[8,8,128]{2,1,0:T(8,128)S(1)} %copy-done.10, s32[8,8,128]{2,1,0:T(8,128)S(1)} %copy-done.12, f32[32,256]{1,0:T(8,128)S(1)} %scatter.4.coef), custom_call_target="tpu_custom_call" | custom-call | flops 4000000000 | bytes 1048576 | tf_op jit(solution)/shard_map/pallas_call | solution.py:62
  84.4 0.0 collective-permute-start.4
  84.4 11.9 %collective-permute-done.3.refs_1_ = bf16[2,1024,256]{2,1,0:T(8,128)(2,1)} collective-permute-done((bf16[2,1024,256]{2,1,0:T(8,128)(2,1)S(1)}, bf16[2,1024,256]{2,1,0:T(8,128)(2,1)}, u32[]{:S(2)}, u32[]{:S(2)}) %collective-permute-start.3) | collective-permute-done | bytes 1048608 | tf_op jit(solution)/shard_map/ppermute | solution.py:967
  96.3 0.0 collective-permute-start.5
  96.3 0.0 all-to-all-done.1.shared
  96.3 7.2 %shard_map.152 = (bf16[8,64,1024]{2,1,0:T(8,128)(2,1)}, bf16[8,64,256]{2,1,0:T(8,128)(2,1)S(1)}, bf16[8,32,256]{2,1,0:T(8,128)(2,1)}) custom-call(s32[64]{0:T(128)} %reshape_squeeze.3.owners, s32[1]{0:T(128)} %bitcast.9.me, s32[8,8,128]{2,1,0:T(8,128)} %get-tuple-element.49.targets, s32[8,8,128]{2,1,0:T(8,128)} %get-tuple-element.52.ranks, ...), custom_call_target="tpu_custom_call" | custom-call | flops 8000000000 | bytes 1048576 | tf_op jit(solution)/shard_map/pallas_call | solution.py:62
  103.5 5.7 %all-to-all-start.2 = ((bf16[8,32,256]{2,1,0:T(8,128)(2,1)}), bf16[8,32,256]{2,1,0:T(8,128)(2,1)S(1)}, u32[]{:S(2)}, u32[]{:S(2)}) async-start(bf16[8,32,256]{2,1,0:T(8,128)(2,1)} %get-tuple-element.60), calls=%async_computation.2 | async-start | bytes 262144 | tf_op jit(solution)/shard_map/all_to_all | solution.py:1067
  109.2 5.1 %shard_map.153.sums = bf16[4,64,512]{2,1,0:T(8,128)(2,1)S(1)} custom-call(bf16[8,64,256]{2,1,0:T(8,128)(2,1)S(1)} %get-tuple-element.55.slot_grads, s32[8,1,256]{2,1,0:T(1,128)} %get-tuple-element.56.slot_rows, f32[8,32,256]{2,1,0:T(8,128)} %get-tuple-element.57.slot_mix, bf16[256,1920]{1,0:T(8,128)(2,1)} %get-tuple-element.58.bases_far, ...), custom_call_target="tpu_custom_call" | custom-call | flops 5000000000 | bytes 1048576 | tf_op jit(solution)/shard_map/pallas_call | solution.py:62
  114.3 2.6 %all-to-all-done.2.coefs = bf16[8,32,256]{2,1,0:T(8,128)(2,1)S(1)} async-done(((bf16[8,32,256]{2,1,0:T(8,128)(2,1)}), bf16[8,32,256]{2,1,0:T(8,128)(2,1)S(1)}, u32[]{:S(2)}, u32[]{:S(2)}) %all-to-all-start.2) | async-done | bytes 131104 | tf_op jit(solution)/shard_map/all_to_all | solution.py:1067
  116.9 9.3 %all_to_all.20.arrived = bf16[4,64,640]{2,1,0:T(8,128)(2,1)S(1)} all-to-all(bf16[4,64,640]{2,1,0:T(8,128)(2,1)S(1)} %shard_map.154), channel_id=1, replica_groups=mesh['dom'=8,'feat'=4] {'feat'}, dimensions={0} | all-to-all | bytes 655360 | tf_op jit(solution)/shard_map/all_to_all | solution.py:1087
  126.2 0.7 shard_map.155
  126.9 0.0 collective-permute-done.4.refs_2_
  126.9 0.0 collective-permute-done.5.refs_3_
  126.9 14.5 %shard_map.157 = (f32[1920,256]{1,0:T(8,128)}, f32[64,256]{1,0:T(8,128)}) custom-call(s32[4]{0:T(128)} %pad_add_fusion.place, f32[8,32,1024]{2,1,0:T(8,128)} %get-tuple-element.62.mix_far, bf16[8,64,1024]{2,1,0:T(8,128)(2,1)} %get-tuple-element.63.grads_far, bf16[256,4096]{1,0:T(8,128)(2,1)} %get-tuple-element.66.full_far, ...), custom_call_target="tpu_custom_call" | custom-call | flops 12000000000 | bytes 1048576 | tf_op jit(solution)/shard_map/pallas_call | solution.py:62
  (6 shorter events, 0.0 us)
Async XLA Ops:
  0.6 24.8 %copy-start.2 = (bf16[64,512]{1,0:T(8,128)(2,1)S(1)}, bf16[64,512]{1,0:T(8,128)(2,1)}, u32[]{:S(2)}) copy-start(bf16[64,512]{1,0:T(8,128)(2,1)} %feats.3) | copy-start | bytes 196612
  0.6 24.7 %copy-start.5 = (s32[1024,1]{0,1:T(1,128)S(1)}, s32[1024,1]{0,1:T(1,128)}, u32[]{:S(2)}) copy-start(s32[1024,1]{0,1:T(1,128)} %param.17) | copy-start | bytes 12292
  0.7 24.7 %copy-start.6 = (s32[1024]{0:T(1024)S(1)}, s32[1024]{0:T(1024)}, u32[]{:S(2)}) copy-start(s32[1024]{0:T(1024)} %param.18) | copy-start | bytes 12292
  25.4 13.1 %copy-start.14 = (f32[237,30]{0,1:T(8,128)S(1)}, f32[237,30]{0,1:T(8,128)}, u32[]{:S(2)}) copy-start(f32[237,30]{0,1:T(8,128)} %param.16) | copy-start | bytes 85324
  25.4 13.1 %copy-start = (bf16[30,64,256]{2,1,0:T(8,128)(2,1)S(1)}, bf16[30,64,256]{2,1,0:T(8,128)(2,1)}, u32[]{:S(2)}) copy-start(bf16[30,64,256]{2,1,0:T(8,128)(2,1)} %param.15) | copy-start | bytes 2949124
  25.4 13.1 %copy-start.7 = (s32[1024]{0:T(1024)S(1)}, s32[1024]{0:T(1024)}, u32[]{:S(2)}) copy-start(s32[1024]{0:T(1024)} %param.19) | copy-start | bytes 12292
  25.4 13.1 %copy-start.8 = (s32[1024]{0:T(1024)S(1)}, s32[1024]{0:T(1024)}, u32[]{:S(2)}) copy-start(s32[1024]{0:T(1024)} %param.20) | copy-start | bytes 12292
  29.4 9.1 %copy-start.9 = (s32[8,8,128]{2,1,0:T(8,128)}, s32[8,8,128]{2,1,0:T(8,128)S(1)}, u32[]{:S(2)}) copy-start(s32[8,8,128]{2,1,0:T(8,128)S(1)} %get-tuple-element.50.ids) | copy-start | bytes 98308
  29.4 9.2 %copy-start.11 = (s32[8,8,128]{2,1,0:T(8,128)}, s32[8,8,128]{2,1,0:T(8,128)S(1)}, u32[]{:S(2)}) copy-start(s32[8,8,128]{2,1,0:T(8,128)S(1)} %get-tuple-element.51.rels) | copy-start | bytes 98308
  29.4 17.5 %copy-start.1 = (bf16[64,4096]{1,0:T(8,128)(2,1)}, bf16[64,4096]{1,0:T(8,128)(2,1)S(1)}, u32[]{:S(2)}) copy-start(bf16[64,4096]{1,0:T(8,128)(2,1)S(1)} %get-tuple-element.65.refs_0_) | copy-start | bytes 1572868
  38.0 14.2 %collective-permute-start = (bf16[64,4096]{1,0:T(8,128)(2,1)S(1)}, bf16[64,4096]{1,0:T(8,128)(2,1)S(1)}, u32[]{:S(2)}, u32[]{:S(2)}) collective-permute-start(bf16[64,4096]{1,0:T(8,128)(2,1)S(1)} %get-tuple-element.65.refs_0_), channel_id=1, source_target_pairs={{0,2},{1,3},{2,0},{3,1},{4,6},{5,7},{6,4},{7,5},{8,10},{9,11},{10,... | collective-permute-start | bytes 1572872 | tf_op jit(solution)/shard_map/ppermute | solution.py:967
  38.6 18.8 %copy-start.3 = (bf16[64,512]{1,0:T(8,128)(2,1)S(1)}, bf16[64,512]{1,0:T(8,128)(2,1)}, u32[]{:S(2)}) copy-start(bf16[64,512]{1,0:T(8,128)(2,1)} %cotangent.1) | copy-start | bytes 196612
  38.6 18.8 %copy-start.4 = (bf16[256,64]{0,1:T(8,128)(2,1)S(1)}, bf16[256,64]{0,1:T(8,128)(2,1)}, u32[]{:S(2)}) copy-start(bf16[256,64]{0,1:T(8,128)(2,1)} %param.14) | copy-start | bytes 98308
  41.6 15.8 %all-to-all-start = ((bf16[16,80,128]{2,1,0:T(8,128)(2,1)}), bf16[16,80,128]{2,1,0:T(8,128)(2,1)S(1)}, u32[]{:S(2)}, u32[]{:S(2)}) async-start(bf16[16,80,128]{2,1,0:T(8,128)(2,1)} %shard_map.148), calls=%async_computation | async-start | bytes 655360 | tf_op jit(solution)/shard_map/all_to_all | solution.py:1020
  46.9 16.1 %collective-permute-start.1 = (bf16[64,4096]{1,0:T(8,128)(2,1)S(1)}, bf16[64,4096]{1,0:T(8,128)(2,1)}, u32[]{:S(2)}, u32[]{:S(2)}) collective-permute-start(bf16[64,4096]{1,0:T(8,128)(2,1)S(1)} %get-tuple-element.65.refs_0_), channel_id=1, source_target_pairs={{0,1},{1,0},{2,3},{3,2},{4,5},{5,4},{6,7},{7,6},{8,9},{9,8},{10,11... | collective-permute-start | bytes 1572872 | tf_op jit(solution)/shard_map/ppermute | solution.py:967
  52.2 7.1 %copy-start.15 = (bf16[64,4096]{1,0:T(8,128)(2,1)}, bf16[64,4096]{1,0:T(8,128)(2,1)S(1)}, u32[]{:S(2)}) copy-start(bf16[64,4096]{1,0:T(8,128)(2,1)S(1)} %collective-permute-done.refs_1_) | copy-start | bytes 1572868
  52.2 10.8 %collective-permute-start.2 = (bf16[64,4096]{1,0:T(8,128)(2,1)S(1)}, bf16[64,4096]{1,0:T(8,128)(2,1)}, u32[]{:S(2)}, u32[]{:S(2)}) collective-permute-start(bf16[64,4096]{1,0:T(8,128)(2,1)S(1)} %collective-permute-done.refs_1_), channel_id=1, source_target_pairs={{0,1},{1,0},{2,3},{3,2},{4,5},{5,4},{6,7},{7,6},{8,9},{9,8},{10,11... | collective-permute-start | bytes 1572872 | tf_op jit(solution)/shard_map/ppermute | solution.py:967
  59.2 37.1 %all-to-all-start.1 = ((bf16[8,80,512]{2,1,0:T(8,128)(2,1)}), bf16[8,80,512]{2,1,0:T(8,128)(2,1)S(1)}, u32[]{:S(2)}, u32[]{:S(2)}) async-start(bf16[8,80,512]{2,1,0:T(8,128)(2,1)} %get-tuple-element.53), calls=%async_computation.1 | async-start | bytes 1310720 | tf_op jit(solution)/shard_map/all_to_all | solution.py:1037
  63.0 10.2 %copy-start.13 = (s32[8,8,128]{2,1,0:T(8,128)S(1)}, s32[8,8,128]{2,1,0:T(8,128)}, u32[]{:S(2)}) copy-start(s32[8,8,128]{2,1,0:T(8,128)} %get-tuple-element.48) | copy-start | bytes 98308
  71.7 24.6 %collective-permute-start.3 = (bf16[2,1024,256]{2,1,0:T(8,128)(2,1)S(1)}, bf16[2,1024,256]{2,1,0:T(8,128)(2,1)}, u32[]{:S(2)}, u32[]{:S(2)}) collective-permute-start(bf16[2,1024,256]{2,1,0:T(8,128)(2,1)S(1)} %bitcast.18), channel_id=1, source_target_pairs={{0,2},{1,3},{2,0},{3,1},{4,6},{5,7},{6,4},{7,5},{8,10},{9,11},{10,... | collective-permute-start | bytes 3145736 | tf_op jit(solution)/shard_map/ppermute | solution.py:967
  74.1 3.4 %copy-start.10 = (s32[8,8,128]{2,1,0:T(8,128)S(1)}, s32[8,8,128]{2,1,0:T(8,128)}, u32[]{:S(2)}) copy-start(s32[8,8,128]{2,1,0:T(8,128)} %copy-done.9) | copy-start | bytes 98308
  74.1 3.4 %copy-start.12 = (s32[8,8,128]{2,1,0:T(8,128)S(1)}, s32[8,8,128]{2,1,0:T(8,128)}, u32[]{:S(2)}) copy-start(s32[8,8,128]{2,1,0:T(8,128)} %copy-done.11) | copy-start | bytes 98308
  84.4 42.4 %collective-permute-start.4 = (bf16[2,1024,256]{2,1,0:T(8,128)(2,1)S(1)}, bf16[2,1024,256]{2,1,0:T(8,128)(2,1)}, u32[]{:S(2)}, u32[]{:S(2)}) collective-permute-start(bf16[2,1024,256]{2,1,0:T(8,128)(2,1)S(1)} %bitcast.19), channel_id=1, source_target_pairs={{0,1},{1,0},{2,3},{3,2},{4,5},{5,4},{6,7},{7,6},{8,9},{9,8},{10,11... | collective-permute-start | bytes 3145736 | tf_op jit(solution)/shard_map/ppermute | solution.py:967
  96.3 30.6 %collective-permute-start.5 = (bf16[2,1024,256]{2,1,0:T(8,128)(2,1)}, bf16[2,1024,256]{2,1,0:T(8,128)(2,1)}, u32[]{:S(2)}, u32[]{:S(2)}) collective-permute-start(bf16[2,1024,256]{2,1,0:T(8,128)(2,1)} %collective-permute-done.3.refs_1_), channel_id=1, source_target_pairs={{0,1},{1,0},{2,3},{3,2},{4,5},{5,4},{6,7},{7,6},{8,9},{9,8},{10,11... | collective-permute-start | bytes 3145736 | tf_op jit(solution)/shard_map/ppermute | solution.py:967
  103.5 13.4 %all-to-all-start.2 = ((bf16[8,32,256]{2,1,0:T(8,128)(2,1)}), bf16[8,32,256]{2,1,0:T(8,128)(2,1)S(1)}, u32[]{:S(2)}, u32[]{:S(2)}) async-start(bf16[8,32,256]{2,1,0:T(8,128)(2,1)} %get-tuple-element.60), calls=%async_computation.2 | async-start | bytes 262144 | tf_op jit(solution)/shard_map/all_to_all | solution.py:1067

commit v5 on v4

--- a/solution.py
+++ b/solution.py
@@ -569,10 +569,10 @@
 def message_kernel(block_cap, entities, owners, valid, gathered, bases, coef, rel, dst, send):
     slots, tall, rows = send.shape
     blocks = rel.shape[0]
-    quarter = tall - 16
+    quarter = tall - 8
     basis_count = bases.shape[0] // quarter
     group = 5
-    first = iota((16, rows), 0)
+    first = iota((8, rows), 0)
     empty = jnp.where(first == 0, entities >> 8, jnp.where(first == 1, entities & 255, 0))
     empty = empty.astype(F32).astype(BF)
     for s in range(slots):
@@ -626,7 +626,7 @@
     pre = (cotangent[...].astype(F32) * gate * (1.0 + preact * (1.0 - gate))).astype(BF)
     grad_pre[...] = pre
     whole = count.astype(I32)
-    first = iota((16, entities), 0)
+    first = iota((8, entities), 0)
     code = jnp.where(first == 0, whole >> 8, jnp.where(first == 1, whole & 255, 0))
     code = code.astype(F32).astype(BF)
     for k in range(copies):
@@ -734,7 +734,7 @@
     dom_count, blocks, _ = targets.shape
     slot_cap = comp.shape[2]
     entities = shared.shape[2]
-    quarter = shared.shape[1] - 16
+    quarter = shared.shape[1] - 8
     copies, _, relations = coef_out.shape
     basis_count = products.shape[0] // quarter
     for q in range(dom_count):
@@ -1011,7 +1011,7 @@
 
     messages = call(
         functools.partial(message_kernel, block_cap, entities),
-        shape((dom_count * block_cap, quarter + 16, LANES), BF),
+        shape((dom_count * block_cap, quarter + 8, LANES), BF),
         smem=(0, 1),
         count=7,
         us=4,
@@ -1023,7 +1023,7 @@
         node_kernel,
         (
             shape((quarter, entities), BF),
-            shape((dom_count, quarter + 16, entities), BF),
+            shape((dom_count, quarter + 8, entities), BF),
             shape((quarter, entities), BF),
         ),
         scratch=[

time: 142 us -> 141 us (level)
  waiting for transfers between devices: 24.1 us -> 20.4 us
  local copies, waits for them, and re-layouts: 0.96 us -> 2.87 us
    all_to_all x1, waiting for transfers between devices: 4.43 us -> 0.36 us  [body_few(): lax.all_to_all(messages, 'dom', split_axis=0, concat_axis=0, tiled=True)]
    all_to_all x1, starting transfers between devices: 3.72 us -> 5.65 us  [body_few(): lax.all_to_all(share, 'dom', split_axis=0, concat_axis=0, tiled=True)]
  transfers between devices with their start and end apart: 9 -> 9, of which waited for: 4 -> 4; matrix products, arithmetic and copies ran while one was open for 1% -> 2% of each run, Pallas kernels for 26% -> 26%
where the time goes in v5:
time: 141 us; the launch traced here: 140 us
  Pallas kernels  55.9 us (40%)
  blocking collectives  41.5 us (29%)
  waiting for transfers between devices  20.4 us (14%)
  starting transfers between devices  17.7 us (13%)
  local copies, waits for them, and re-layouts  2.87 us (2%)
    pallas_call x12, Pallas kernels, apply(): run(*(pltpu.with_memory_space_constraint(a, pltpu.HBM) if k in far or k i...  55.9 us
    all_gather x1, blocking collectives, body_few(): lax.all_gather(shared, 'dom', axis=0, tiled=True, axis_index_groups=far)  17.7 us
    ppermute x6, waiting for transfers between devices, doubled(): pieces = pieces + [lax.ppermute(piece, 'feat', links) for piece in pieces]  17.5 us
    all_to_all x1, blocking collectives, body_few(): lax.all_to_all(sent, 'feat', split_axis=0, concat_axis=0, tiled=True)  9.08 us
    all_gather x1, blocking collectives, body_few(): gathered = lax.all_gather(mine, 'feat', axis=0, tiled=True)  8.62 us
    all_gather x1, blocking collectives, body_few(): lax.all_gather(packed, 'dom', axis=0, tiled=True, axis_index_groups=near)  6.06 us
    all_to_all x1, starting transfers between devices, body_few(): lax.all_to_all(coef_part, 'dom', split_axis=0, concat_axis=0, tiled=True)  5.73 us
    all_to_all x1, starting transfers between devices, body_few(): lax.all_to_all(share, 'dom', split_axis=0, concat_axis=0, tiled=True)  5.65 us
  transfers between devices with their start and end apart: 9, of which 4 were waited for; matrix products, arithmetic and copies ran while one was open for 2% of the time, Pallas kernels for 26%

profile of v5, /device:TPU:0, one launch (start us, length us, event | category | flops | bytes accessed | tf_op | source)
XLA Modules:
  0.0 139.9 jit_solution(1194506239078073685)
XLA Ops:
  0.6 0.0 copy-start.3
  0.6 0.0 copy-start.6
  0.7 0.0 copy-start.7
  0.7 0.9 shard_map.146
  1.6 6.1 %all_gather.9 = bf16[2,320,128]{2,1,0:T(8,128)(2,1)S(1)} all-gather(bf16[1,320,128]{2,1,0:T(8,128)(2,1)S(1)} %shard_map.146), channel_id=1, replica_groups={{0,4},{8,12},{16,20},{24,28},{1,5},{9,13},{17,21},{25,29},{2,6},{10,14}..., dimensions={0}, use_global_device_ids=true | all-gather | bytes 245760 | tf_op jit(solution)/shard_map/all_gather | solution.py:941
  7.7 17.7 %all_gather.10.shared = bf16[8,320,128]{2,1,0:T(8,128)(2,1)S(1)} all-gather(bf16[2,320,128]{2,1,0:T(8,128)(2,1)S(1)} %all_gather.9), channel_id=1, replica_groups={{0,8,16,24},{4,12,20,28},{1,9,17,25},{5,13,21,29},{2,10,18,26},{6,14,22..., dimensions={0}, use_global_device_ids=true | all-gather | bytes 819200 | tf_op jit(solution)/shard_map/all_gather | solution.py:942
  25.4 0.0 copy-done.3
  25.4 0.0 copy-done.6
  25.4 0.0 copy-done.7
  25.4 0.0 copy-start.14
  25.4 0.0 copy-start
  25.4 0.0 copy-start.8
  25.4 0.0 copy-start.9
  25.4 3.9 %shard_map.147 = (bf16[64,1536]{1,0:T(8,128)(2,1)S(1)}, bf16[64,4096]{1,0:T(8,128)(2,1)S(1)}, s32[8,8,128]{2,1,0:T(8,128)S(1)}, s32[32,1,256]{2,1,0:T(1,128)}, s...) custom-call(bf16[8,320,128]{2,1,0:T(8,128)(2,1)S(1)} %all_gather.10.shared, ...), custom_call_target="tpu_custom_call" | custom-call | flops 4000000000 | bytes 1048576 | tf_op jit(solution)/shard_map/pallas_call | solution.py:62
  29.4 0.0 copy-start.10
  29.4 0.0 copy-start.12
  29.4 0.0 copy-start.2
  29.4 8.6 %all_gather.11.gathered = bf16[256,1536]{1,0:T(8,128)(2,1)S(1)} all-gather(bf16[64,1536]{1,0:T(8,128)(2,1)S(1)} %get-tuple-element.45), channel_id=1, replica_groups=mesh['dom'=8,'feat'=4] {'feat'}, dimensions={0}, use_global_device_ids=true | all-gather | bytes 983040 | tf_op jit(solution)/shard_map/all_gather | solution.py:960
  38.0 0.5 collective-permute-start
  38.5 0.1 collective-permute-start.1
  38.6 13.7 %collective-permute-done.refs_1_ = bf16[64,4096]{1,0:T(8,128)(2,1)} collective-permute-done((bf16[64,4096]{1,0:T(8,128)(2,1)S(1)}, bf16[64,4096]{1,0:T(8,128)(2,1)}, u32[]{:S(2)}, u32[]{:S(2)}) %collective-permute-start) | collective-permute-done | bytes 524320 | tf_op jit(solution)/shard_map/ppermute | solution.py:967
  52.3 0.0 collective-permute-start.2
  52.3 0.0 copy-done.10
  52.3 0.0 copy-done.12
  52.3 0.0 copy-done.14
  52.3 0.0 copy-done
  52.3 0.0 copy-done.8
  52.3 0.0 copy-done.9
  52.3 2.9 %shard_map.148 = bf16[16,72,128]{2,1,0:T(8,128)(2,1)} custom-call(s32[8]{0:T(128)} %bitcast.36, s32[8]{0:T(128)} %bitcast.38, bf16[256,1536]{1,0:T(8,128)(2,1)S(1)} %all_gather.11.gathered, bf16[1920,256]{1,0:T(8,128)(2,1)S(1)} %bitcast.21, f32[32,256]{1,0:T(8,128)S(1)} %scatter.4.coef, s32[8,128]{1,0:T(8,128)S(1)} %bitcast.32, s32[8,128]{1,0:T(8,128)S(1)} %bitcast.30), custom_call_target="tpu_custom_call" | custom-call | flops 4000000000 | bytes 1048576 | tf_op jit(solution)/shard_map/pallas_call | solution.py:62
  55.2 0.0 copy-done.2
  55.2 5.2 %all-to-all-start = ((bf16[16,72,128]{2,1,0:T(8,128)(2,1)}), bf16[16,72,128]{2,1,0:T(8,128)(2,1)S(1)}, u32[]{:S(2)}, u32[]{:S(2)}) async-start(bf16[16,72,128]{2,1,0:T(8,128)(2,1)} %shard_map.148), calls=%async_computation | async-start | bytes 589824 | tf_op jit(solution)/shard_map/all_to_all | solution.py:1020
  60.5 0.6 pad_add_fusion.place
  61.1 0.0 collective-permute-done.1.refs_2_
  61.1 0.0 collective-permute-done.2.refs_3_
  61.1 0.0 copy-start.4
  61.1 0.0 copy-start.5
  61.1 8.7 %shard_map.156 = (bf16[8,256,256]{2,1,0:T(8,128)(2,1)S(1)}, bf16[256,4096]{1,0:T(8,128)(2,1)}) custom-call(s32[4]{0:T(128)} %pad_add_fusion.place, s32[32,1,256]{2,1,0:T(1,128)} %get-tuple-element.64.spans, bf16[64,4096]{1,0:T(8,128)(2,1)} %copy-done.2, bf16[64,4096]{1,0:T(8,128)(2,1)} %collective-permute-done.refs_1_, ...), custom_call_target="tpu_custom_call" | custom-call | flops 10000000000 | bytes 1048576 | tf_op jit(solution)/shard_map/pallas_call | solution.py:62
  69.8 0.5 collective-permute-start.3
  70.3 0.4 all-to-all-done.received
  70.7 0.0 copy-done.4
  70.7 0.0 copy-done.5
  70.7 1.8 %shard_map.149 = (bf16[64,512]{1,0:T(8,128)(2,1)}, bf16[8,72,512]{2,1,0:T(8,128)(2,1)}, bf16[64,512]{1,0:T(8,128)(2,1)}) custom-call(bf16[16,72,128]{2,1,0:T(8,128)(2,1)S(1)} %all-to-all-done.received, bf16[256,1536]{1,0:T(8,128)(2,1)S(1)} %all_gather.11.gathered, bf16[64,256]{1,0:T(8,128)(2,1)S(1)} %bitcast.23, bf16[64,512]{1,0:T(8,128)(2,1)S(1)} %copy-done.4), custom_call_target="tpu_custom_call" | custom-call | flops 4000000000 | bytes 1048576 | tf_op jit(solution)/shard_map/pallas_call | solution.py:62
  72.5 5.6 %all-to-all-start.1 = ((bf16[8,72,512]{2,1,0:T(8,128)(2,1)}), bf16[8,72,512]{2,1,0:T(8,128)(2,1)S(1)}, u32[]{:S(2)}, u32[]{:S(2)}) async-start(bf16[8,72,512]{2,1,0:T(8,128)(2,1)} %get-tuple-element.53), calls=%async_computation.1 | async-start | bytes 1179648 | tf_op jit(solution)/shard_map/all_to_all | solution.py:1037
  78.2 1.0 slice_reduce_fusion
  79.1 0.6 reshape_squeeze.3.owners
  79.8 0.0 copy-start.1
  79.8 1.2 copy-done.1
  81.0 3.4 %shard_map.151 = (bf16[256,1920]{1,0:T(8,128)(2,1)}, bf16[1920,1024]{1,0:T(8,128)(2,1)}) custom-call(bf16[256,1536]{1,0:T(8,128)(2,1)S(1)} %all_gather.11.gathered, bf16[1920,256]{1,0:T(8,128)(2,1)S(1)} %bitcast.22), custom_call_target="tpu_custom_call" | custom-call | flops 4000000000 | bytes 1048576 | tf_op jit(solution)/shard_map/pallas_call | solution.py:62
  84.4 0.0 copy-done.11
  84.4 0.0 copy-done.13
  84.4 7.0 %shard_map.150 = (s32[8,8,128]{2,1,0:T(8,128)}, s32[8,1,256]{2,1,0:T(1,128)}, f32[8,32,256]{2,1,0:T(8,128)}, f32[8,32,1024]{2,1,0:T(8,128)}) custom-call(s32[1]{0:T(128)} %bitcast.9.me, s32[8,8,128]{2,1,0:T(8,128)S(1)} %copy-done.11, s32[8,8,128]{2,1,0:T(8,128)S(1)} %copy-done.13, f32[32,256]{1,0:T(8,128)S(1)} %scatter.4.coef), custom_call_target="tpu_custom_call" | custom-call | flops 4000000000 | bytes 1048576 | tf_op jit(solution)/shard_map/pallas_call | solution.py:62
  91.4 0.0 collective-permute-start.4
  91.4 3.7 %collective-permute-done.3.refs_1_ = bf16[2,1024,256]{2,1,0:T(8,128)(2,1)S(1)} collective-permute-done((bf16[2,1024,256]{2,1,0:T(8,128)(2,1)S(1)}, bf16[2,1024,256]{2,1,0:T(8,128)(2,1)S(1)}, u32[]{:S(2)}, u32[]{:S(2)}) %collective-permute-start.3) | collective-permute-done | bytes 1048608 | tf_op jit(solution)/shard_map/ppermute | solution.py:967
  95.1 0.0 collective-permute-start.5
  95.1 0.0 all-to-all-done.1.shared
  95.1 7.2 %shard_map.152 = (bf16[8,64,1024]{2,1,0:T(8,128)(2,1)}, bf16[8,64,256]{2,1,0:T(8,128)(2,1)S(1)}, bf16[8,32,256]{2,1,0:T(8,128)(2,1)}) custom-call(s32[64]{0:T(128)} %reshape_squeeze.3.owners, s32[1]{0:T(128)} %bitcast.9.me, s32[8,8,128]{2,1,0:T(8,128)} %get-tuple-element.49.targets, s32[8,8,128]{2,1,0:T(8,128)} %get-tuple-element.52.ranks, ...), custom_call_target="tpu_custom_call" | custom-call | flops 8000000000 | bytes 1048576 | tf_op jit(solution)/shard_map/pallas_call | solution.py:62
  102.3 5.7 %all-to-all-start.2 = ((bf16[8,32,256]{2,1,0:T(8,128)(2,1)}), bf16[8,32,256]{2,1,0:T(8,128)(2,1)S(1)}, u32[]{:S(2)}, u32[]{:S(2)}) async-start(bf16[8,32,256]{2,1,0:T(8,128)(2,1)} %get-tuple-element.60), calls=%async_computation.2 | async-start | bytes 262144 | tf_op jit(solution)/shard_map/all_to_all | solution.py:1067
  108.0 5.1 %shard_map.153.sums = bf16[4,64,512]{2,1,0:T(8,128)(2,1)S(1)} custom-call(bf16[8,64,256]{2,1,0:T(8,128)(2,1)S(1)} %get-tuple-element.55.slot_grads, s32[8,1,256]{2,1,0:T(1,128)} %get-tuple-element.56.slot_rows, f32[8,32,256]{2,1,0:T(8,128)} %get-tuple-element.57.slot_mix, bf16[256,1920]{1,0:T(8,128)(2,1)} %get-tuple-element.58.bases_far, ...), custom_call_target="tpu_custom_call" | custom-call | flops 5000000000 | bytes 1048576 | tf_op jit(solution)/shard_map/pallas_call | solution.py:62
  113.1 2.6 %all-to-all-done.2.coefs = bf16[8,32,256]{2,1,0:T(8,128)(2,1)S(1)} async-done(((bf16[8,32,256]{2,1,0:T(8,128)(2,1)}), bf16[8,32,256]{2,1,0:T(8,128)(2,1)S(1)}, u32[]{:S(2)}, u32[]{:S(2)}) %all-to-all-start.2) | async-done | bytes 131104 | tf_op jit(solution)/shard_map/all_to_all | solution.py:1067
  115.7 9.1 %all_to_all.20.arrived = bf16[4,64,640]{2,1,0:T(8,128)(2,1)S(1)} all-to-all(bf16[4,64,640]{2,1,0:T(8,128)(2,1)S(1)} %shard_map.154), channel_id=1, replica_groups=mesh['dom'=8,'feat'=4] {'feat'}, dimensions={0} | all-to-all | bytes 655360 | tf_op jit(solution)/shard_map/all_to_all | solution.py:1087
  124.8 0.7 shard_map.155
  125.5 0.0 collective-permute-done.4.refs_2_
  125.5 0.0 collective-permute-done.5.refs_3_
  125.5 14.2 %shard_map.157 = (f32[1920,256]{1,0:T(8,128)}, f32[64,256]{1,0:T(8,128)}) custom-call(s32[4]{0:T(128)} %pad_add_fusion.place, f32[8,32,1024]{2,1,0:T(8,128)} %get-tuple-element.62.mix_far, bf16[8,64,1024]{2,1,0:T(8,128)(2,1)} %get-tuple-element.63.grads_far, bf16[256,4096]{1,0:T(8,128)(2,1)} %get-tuple-element.66.full_far, ...), custom_call_target="tpu_custom_call" | custom-call | flops 12000000000 | bytes 1048576 | tf_op jit(solution)/shard_map/pallas_call | solution.py:62
  (4 shorter events, 0.0 us)
Async XLA Ops:
  0.6 24.8 %copy-start.3 = (bf16[64,512]{1,0:T(8,128)(2,1)S(1)}, bf16[64,512]{1,0:T(8,128)(2,1)}, u32[]{:S(2)}) copy-start(bf16[64,512]{1,0:T(8,128)(2,1)} %feats.3) | copy-start | bytes 196612
  0.6 24.7 %copy-start.6 = (s32[1024,1]{0,1:T(1,128)S(1)}, s32[1024,1]{0,1:T(1,128)}, u32[]{:S(2)}) copy-start(s32[1024,1]{0,1:T(1,128)} %param.17) | copy-start | bytes 12292
  0.7 24.7 %copy-start.7 = (s32[1024]{0:T(1024)S(1)}, s32[1024]{0:T(1024)}, u32[]{:S(2)}) copy-start(s32[1024]{0:T(1024)} %param.18) | copy-start | bytes 12292
  25.4 26.9 %copy-start.14 = (f32[237,30]{0,1:T(8,128)S(1)}, f32[237,30]{0,1:T(8,128)}, u32[]{:S(2)}) copy-start(f32[237,30]{0,1:T(8,128)} %param.16) | copy-start | bytes 85324
  25.4 26.9 %copy-start = (bf16[30,64,256]{2,1,0:T(8,128)(2,1)S(1)}, bf16[30,64,256]{2,1,0:T(8,128)(2,1)}, u32[]{:S(2)}) copy-start(bf16[30,64,256]{2,1,0:T(8,128)(2,1)} %param.15) | copy-start | bytes 2949124
  25.4 26.9 %copy-start.8 = (s32[1024]{0:T(1024)S(1)}, s32[1024]{0:T(1024)}, u32[]{:S(2)}) copy-start(s32[1024]{0:T(1024)} %param.19) | copy-start | bytes 12292
  25.4 26.9 %copy-start.9 = (s32[1024]{0:T(1024)S(1)}, s32[1024]{0:T(1024)}, u32[]{:S(2)}) copy-start(s32[1024]{0:T(1024)} %param.20) | copy-start | bytes 12292
  29.4 22.9 %copy-start.10 = (s32[8,8,128]{2,1,0:T(8,128)}, s32[8,8,128]{2,1,0:T(8,128)S(1)}, u32[]{:S(2)}) copy-start(s32[8,8,128]{2,1,0:T(8,128)S(1)} %get-tuple-element.50.ids) | copy-start | bytes 98308
  29.4 22.9 %copy-start.12 = (s32[8,8,128]{2,1,0:T(8,128)}, s32[8,8,128]{2,1,0:T(8,128)S(1)}, u32[]{:S(2)}) copy-start(s32[8,8,128]{2,1,0:T(8,128)S(1)} %get-tuple-element.51.rels) | copy-start | bytes 98308
  29.4 25.9 %copy-start.2 = (bf16[64,4096]{1,0:T(8,128)(2,1)}, bf16[64,4096]{1,0:T(8,128)(2,1)S(1)}, u32[]{:S(2)}) copy-start(bf16[64,4096]{1,0:T(8,128)(2,1)S(1)} %get-tuple-element.65.refs_0_) | copy-start | bytes 1572868
  38.0 14.3 %collective-permute-start = (bf16[64,4096]{1,0:T(8,128)(2,1)S(1)}, bf16[64,4096]{1,0:T(8,128)(2,1)}, u32[]{:S(2)}, u32[]{:S(2)}) collective-permute-start(bf16[64,4096]{1,0:T(8,128)(2,1)S(1)} %get-tuple-element.65.refs_0_), channel_id=1, source_target_pairs={{0,2},{1,3},{2,0},{3,1},{4,6},{5,7},{6,4},{7,5},{8,10},{9,11},{10,... | collective-permute-start | bytes 1572872 | tf_op jit(solution)/shard_map/ppermute | solution.py:967
  38.5 22.6 %collective-permute-start.1 = (bf16[64,4096]{1,0:T(8,128)(2,1)S(1)}, bf16[64,4096]{1,0:T(8,128)(2,1)}, u32[]{:S(2)}, u32[]{:S(2)}) collective-permute-start(bf16[64,4096]{1,0:T(8,128)(2,1)S(1)} %get-tuple-element.65.refs_0_), channel_id=1, source_target_pairs={{0,1},{1,0},{2,3},{3,2},{4,5},{5,4},{6,7},{7,6},{8,9},{9,8},{10,11... | collective-permute-start | bytes 1572872 | tf_op jit(solution)/shard_map/ppermute | solution.py:967
  52.3 8.8 %collective-permute-start.2 = (bf16[64,4096]{1,0:T(8,128)(2,1)}, bf16[64,4096]{1,0:T(8,128)(2,1)}, u32[]{:S(2)}, u32[]{:S(2)}) collective-permute-start(bf16[64,4096]{1,0:T(8,128)(2,1)} %collective-permute-done.refs_1_), channel_id=1, source_target_pairs={{0,1},{1,0},{2,3},{3,2},{4,5},{5,4},{6,7},{7,6},{8,9},{9,8},{10,11... | collective-permute-start | bytes 1572872 | tf_op jit(solution)/shard_map/ppermute | solution.py:967
  55.2 15.5 %all-to-all-start = ((bf16[16,72,128]{2,1,0:T(8,128)(2,1)}), bf16[16,72,128]{2,1,0:T(8,128)(2,1)S(1)}, u32[]{:S(2)}, u32[]{:S(2)}) async-start(bf16[16,72,128]{2,1,0:T(8,128)(2,1)} %shard_map.148), calls=%async_computation | async-start | bytes 589824 | tf_op jit(solution)/shard_map/all_to_all | solution.py:1020
  61.1 9.6 %copy-start.4 = (bf16[64,512]{1,0:T(8,128)(2,1)S(1)}, bf16[64,512]{1,0:T(8,128)(2,1)}, u32[]{:S(2)}) copy-start(bf16[64,512]{1,0:T(8,128)(2,1)} %cotangent.1) | copy-start | bytes 196612
  61.1 9.6 %copy-start.5 = (bf16[256,64]{0,1:T(8,128)(2,1)S(1)}, bf16[256,64]{0,1:T(8,128)(2,1)}, u32[]{:S(2)}) copy-start(bf16[256,64]{0,1:T(8,128)(2,1)} %param.14) | copy-start | bytes 98308
  69.8 25.3 %collective-permute-start.3 = (bf16[2,1024,256]{2,1,0:T(8,128)(2,1)S(1)}, bf16[2,1024,256]{2,1,0:T(8,128)(2,1)S(1)}, u32[]{:S(2)}, u32[]{:S(2)}) collective-permute-start(bf16[2,1024,256]{2,1,0:T(8,128)(2,1)S(1)} %bitcast.18), channel_id=1, source_target_pairs={{0,2},{1,3},{2,0},{3,1},{4,6},{5,7},{6,4},{7,5},{8,10},{9,11},{10,... | collective-permute-start | bytes 3145736 | tf_op jit(solution)/shard_map/ppermute | solution.py:967
  72.5 22.6 %all-to-all-start.1 = ((bf16[8,72,512]{2,1,0:T(8,128)(2,1)}), bf16[8,72,512]{2,1,0:T(8,128)(2,1)S(1)}, u32[]{:S(2)}, u32[]{:S(2)}) async-start(bf16[8,72,512]{2,1,0:T(8,128)(2,1)} %get-tuple-element.53), calls=%async_computation.1 | async-start | bytes 1179648 | tf_op jit(solution)/shard_map/all_to_all | solution.py:1037
  79.8 1.2 copy-start.1
  81.0 3.4 %copy-start.11 = (s32[8,8,128]{2,1,0:T(8,128)S(1)}, s32[8,8,128]{2,1,0:T(8,128)}, u32[]{:S(2)}) copy-start(s32[8,8,128]{2,1,0:T(8,128)} %copy-done.10) | copy-start | bytes 98308
  81.0 3.4 %copy-start.13 = (s32[8,8,128]{2,1,0:T(8,128)S(1)}, s32[8,8,128]{2,1,0:T(8,128)}, u32[]{:S(2)}) copy-start(s32[8,8,128]{2,1,0:T(8,128)} %copy-done.12) | copy-start | bytes 98308
  91.4 34.1 %collective-permute-start.4 = (bf16[2,1024,256]{2,1,0:T(8,128)(2,1)S(1)}, bf16[2,1024,256]{2,1,0:T(8,128)(2,1)}, u32[]{:S(2)}, u32[]{:S(2)}) collective-permute-start(bf16[2,1024,256]{2,1,0:T(8,128)(2,1)S(1)} %bitcast.19), channel_id=1, source_target_pairs={{0,1},{1,0},{2,3},{3,2},{4,5},{5,4},{6,7},{7,6},{8,9},{9,8},{10,11... | collective-permute-start | bytes 3145736 | tf_op jit(solution)/shard_map/ppermute | solution.py:967
  95.1 30.4 %collective-permute-start.5 = (bf16[2,1024,256]{2,1,0:T(8,128)(2,1)S(1)}, bf16[2,1024,256]{2,1,0:T(8,128)(2,1)}, u32[]{:S(2)}, u32[]{:S(2)}) collective-permute-start(bf16[2,1024,256]{2,1,0:T(8,128)(2,1)S(1)} %collective-permute-done.3.refs_1_), channel_id=1, source_target_pairs={{0,1},{1,0},{2,3},{3,2},{4,5},{5,4},{6,7},{7,6},{8,9},{9,8},{10,11... | collective-permute-start | bytes 3145736 | tf_op jit(solution)/shard_map/ppermute | solution.py:967
  102.3 13.4 %all-to-all-start.2 = ((bf16[8,32,256]{2,1,0:T(8,128)(2,1)}), bf16[8,32,256]{2,1,0:T(8,128)(2,1)S(1)}, u32[]{:S(2)}, u32[]{:S(2)}) async-start(bf16[8,32,256]{2,1,0:T(8,128)(2,1)} %get-tuple-element.60), calls=%async_computation.2 | async-start | bytes 262144 | tf_op jit(solution)/shard_map/all_to_all | solution.py:1067
